TPU v7x, 512 devices: a whole 4x8x8 slice. The times are simulated.
512 devices in a mesh: grp: 32 (over z, y_lo, core), dom: 16 (over y_hi, x).
Axes of the slice: x: 4, y: 8 (y_hi: 4, y_lo: 2; y = y_hi * 2 + y_lo), z: 8, core: 2. Of those that a mesh axis runs over, the one named last changes fastest.
Arguments:
- connect: int32 [20, 65536], P(None, ('grp', 'dom')), may hold values from 0 to 511, as said below
- interface_nodes: int32 [512, 4, 32], P(('grp', 'dom')), may hold values from 0 to 511, as said below
- neighbours: int32 [512, 4], P(('grp', 'dom')), may hold values from 0 to 1, as said below
- point_rank: int32 [512, 2048], P(('grp', 'dom')), may hold values from 0 to 2047, each once within a row
- shape_grad: float32 [48, 20], replicated, may hold values from -1.25 to 1.25
- inverse_jacobian: float32 [9, 65536], P(None, ('grp', 'dom')), may hold values from -0.45 to 2.5
- lame_moduli: float32 [2, 65536], P(None, ('grp', 'dom')), may hold values from 0.5 to 2
- point_weights: float32 [16, 65536], P(None, ('grp', 'dom')), may hold values from 0.003 to 0.02
- mass_elem: float32 [20, 65536], P(None, ('grp', 'dom')), may hold values from 0.5 to 2
- source_pattern: float32 [3, 262144], P(None, ('grp', 'dom')), may hold values from -6 to 6
- wavelet: float32 [16], replicated, may hold values from -6 to 6
Outputs:
- strain_db: bfloat16 [16, 6, 1048576], P(None, None, ('grp', 'dom'))
Inputs may be any that keep to these rules, and one draw needn't show every extreme that they name: `connect`: every one of a partition's 512 nodes is named by some element of that partition. `interface_nodes`: entry i of list k of a partition and entry i of the opposite list of the partition beside it in direction k are copies of one node; no node stands twice among a partition's four lists. `neighbours`: the entry of a partition in direction k equals that of the partition beside it in the opposite direction; it is 0 where no partition lies in direction k.
All inputs are finite; a program needn't handle non-finite values.
Results may differ from a plain program's by a relative error of at most 0.001.
Values may be sent and summed in bfloat16 or wider, within the bound.
No kernel may reach another device: no remote copies, remote signals or barrier semaphores. Data moves between devices by JAX's collectives and lax.ppermute only.
A program may use at most 64 MiB of HBM per device.

v0:
```python
import jax
import jax.numpy as jnp
from jax import lax
from jax.experimental import pallas as pl
from jax.experimental.pallas import tpu as pltpu
from jax.sharding import PartitionSpec as P


EL_NODES = 20
NODE_ROWS = 24
POINTS = 16
STRAIN = 6
STEPS = 16
LANES = 128
FACES = 4
ORDER_WIDTH = 256

time_step = 0.5

DOM_ROW = 4

EXCHANGES = ("dom1", "grp1", "dom0", "grp0")

VMEM = pl.BlockSpec(memory_space=pltpu.VMEM)
HBM = pl.BlockSpec(memory_space=pltpu.MemorySpace.HBM)


def snake(axis, index):
    row, column = index // DOM_ROW, index % DOM_ROW
    return index if axis == "grp" or row % 2 == 0 else row * DOM_ROW + DOM_ROW - 1 - column


def kernel_call(body, outs, specs, scratch=()):
    return pl.pallas_call(
        body,
        out_shape=outs,
        in_specs=specs,
        out_specs=[VMEM] * len(outs),
        scratch_shapes=list(scratch),
        compiler_params=pltpu.CompilerParams(vmem_limit_bytes=24 * 1024 * 1024),
    )


def parts_of(x):
    high = x.astype(jnp.bfloat16).astype(jnp.float32)
    rest = x - high
    middle = rest.astype(jnp.bfloat16).astype(jnp.float32)
    low = (rest - middle).astype(jnp.bfloat16).astype(jnp.float32)
    return high, middle, low


def matmul(left, right):
    return jnp.dot(left, right, preferred_element_type=jnp.float32)


def lane_gather(row, index):
    return jnp.take_along_axis(row, index, axis=1)


def pick_lanes(field, index):
    low = jnp.bitwise_and(index, LANES - 1)
    chunk = jnp.right_shift(index, 7)
    out = lane_gather(field[:, 0:LANES], low)
    for j in range(1, field.shape[1] // LANES):
        out = jnp.where(
            chunk == j, lane_gather(field[:, j * LANES : (j + 1) * LANES], low), out
        )
    return out


def spread(received, inverse):
    out = []
    for j in range(inverse.shape[1] // LANES):
        index = inverse[:, j * LANES : (j + 1) * LANES]
        taken = lane_gather(received, jnp.maximum(index, 0))
        out.append(jnp.where(index >= 0, taken, 0.0))
    return jnp.concatenate(out, axis=1)


def merge_received(source, dom1, grp1, dom0, grp0):
    out = jnp.where(source == 0, grp0, grp1)
    out = jnp.where(source == 2, dom0, out)
    return jnp.where(source == 3, dom1, out)


def scatter_nodes(pieces, chunks, incidence):
    group = lax.broadcasted_iota(jnp.int32, (8, LANES), 0) // 4
    parts = [[], [], []]
    for piece, chunk in zip(pieces, chunks):
        both = [jnp.where(chunk == group + base, piece, 0.0) for base in (0, 2)]
        for i, part in enumerate(parts_of(jnp.concatenate(both, axis=0))):
            parts[i].append(part.astype(jnp.bfloat16))
    left = jnp.concatenate([jnp.concatenate(p, axis=1) for p in parts], axis=0)
    sums = matmul(left, incidence)
    total = (sums[32:48] + sums[16:32]) + sums[0:16]
    fields = []
    for base in (0, 8):
        rows = total[base : base + 8]
        fields += [rows, pltpu.roll(rows, 4, 0)]
    return jnp.concatenate(fields, axis=1)


CONNECT_ROW = 0
MASS_ROW = 24
LAME_ROW = 44
LISTED_ROW = 46
SWAPPED_ROW = 47
JACOBIAN_ROW = 48
WEIGHTS_ROW = 64
SOURCE_ROW = 80
RANK_ROW = 96
PACKED_ROWS = 112


def set_incidence(packed, incidence):
    element_nodes = packed[CONNECT_ROW : CONNECT_ROW + NODE_ROWS, :].astype(jnp.int32)
    low = jnp.bitwise_and(element_nodes, LANES - 1)
    own_lane = lax.broadcasted_iota(jnp.int32, (LANES, LANES), 1)
    for n in range(EL_NODES):
        column = jnp.broadcast_to(low[n : n + 1, :], (LANES, LANES)).T
        incidence[n * LANES : (n + 1) * LANES, :] = jnp.where(
            column == own_lane, 1.0, 0.0
        ).astype(jnp.bfloat16)


def set_field(packed, incidence, field):
    element_nodes = packed[CONNECT_ROW : CONNECT_ROW + NODE_ROWS, :].astype(jnp.int32)
    chunk = jnp.right_shift(element_nodes, 7)
    masses = [
        jnp.broadcast_to(packed[MASS_ROW + n : MASS_ROW + n + 1, :], (8, LANES))
        for n in range(EL_NODES)
    ]
    chunks = [chunk[n : n + 1, :] for n in range(EL_NODES)]
    field[...] = scatter_nodes(masses, chunks, incidence[...])
    for j in range(field.shape[1] // LANES):
        row = SOURCE_ROW + 3 * j
        field[0:3, j * LANES : (j + 1) * LANES] = packed[row : row + 3, :]


def pack_kernel(
    wavelet_in,
    neighbours_in,
    connect_in,
    lists_in,
    mass_in,
    source_in,
    shape_in,
    jacobian_in,
    lame_in,
    weights_in,
    rank_in,
    packed,
    shape_t,
    wave,
    send,
    wavelet,
    neighbours,
    connect,
    lists,
    mass_elem,
    source_pattern,
    jacobian,
    lame,
    weights,
    rank,
    sems,
    incidence,
    field,
):
    moves = [
        (wavelet_in, wavelet),
        (neighbours_in, neighbours),
        (connect_in, connect),
        (lists_in, lists),
        (mass_in, mass_elem),
        (source_in, source_pattern),
        (shape_in, shape_t),
        (jacobian_in, jacobian),
        (lame_in, lame),
        (weights_in, weights),
        (rank_in, rank),
    ]
    copies = [pltpu.make_async_copy(a, b, sems.at[i]) for i, (a, b) in enumerate(moves)]
    for copy in copies:
        copy.start()
    packed[...] = jnp.zeros(packed.shape, jnp.float32)
    for copy in copies:
        copy.wait()
    wave[...] = jnp.concatenate(
        [jnp.full((1, LANES), wavelet[t], jnp.float32) for t in range(STEPS)], axis=0
    )
    packed[CONNECT_ROW : CONNECT_ROW + EL_NODES, :] = connect[...].astype(jnp.float32)
    packed[MASS_ROW : MASS_ROW + EL_NODES, :] = mass_elem[...]
    packed[LAME_ROW : LAME_ROW + 2, :] = lame[...]
    packed[JACOBIAN_ROW : JACOBIAN_ROW + 9, :] = jacobian[...]
    packed[WEIGHTS_ROW : WEIGHTS_ROW + POINTS, :] = weights[...]
    packed[RANK_ROW : RANK_ROW + POINTS, :] = rank[...].astype(jnp.float32)
    for j in range(source_pattern.shape[1] // LANES):
        row = SOURCE_ROW + 3 * j
        packed[row : row + 3, :] = source_pattern[:, j * LANES : (j + 1) * LANES]
    face = [lists[0, k : k + 1, :] for k in range(FACES)]
    listed = jnp.concatenate(face, axis=1)
    swapped = jnp.concatenate([face[1], face[0], face[3], face[2]], axis=1)
    side = lax.broadcasted_iota(jnp.int32, (1, LANES), 1) // (LANES // FACES)
    open_side = jnp.where(
        side < 2,
        jnp.where(side == 0, neighbours[0, 0], neighbours[0, 1]),
        jnp.where(side == 2, neighbours[0, 2], neighbours[0, 3]),
    )
    listed = jnp.where(open_side != 0, listed, -1)
    packed[LISTED_ROW : LISTED_ROW + 1, :] = listed.astype(jnp.float32)
    packed[SWAPPED_ROW : SWAPPED_ROW + 1, :] = swapped.astype(jnp.float32)
    set_incidence(packed, incidence)
    set_field(packed, incidence, field)
    send[...] = pick_lanes(field[...], jnp.broadcast_to(swapped, (8, LANES)))


def prepare_kernel(
    packed,
    shape_t,
    incidence,
    field,
    pick_index,
    inverse_index,
    connect,
    wide_gradient,
    wide_force,
    inverse_jacobian,
    lame_moduli,
    point_weights,
    rank,
):
    nodes = field.shape[1]
    element_nodes = packed[CONNECT_ROW : CONNECT_ROW + NODE_ROWS, :].astype(jnp.int32)
    connect[...] = element_nodes
    inverse_jacobian[...] = packed[JACOBIAN_ROW : JACOBIAN_ROW + 9, :]
    lame_moduli[...] = packed[LAME_ROW : LAME_ROW + 2, :]
    point_weights[...] = packed[WEIGHTS_ROW : WEIGHTS_ROW + POINTS, :]
    rank[...] = packed[RANK_ROW : RANK_ROW + POINTS, :].astype(jnp.int32)
    set_incidence(packed, incidence)
    lane = lax.broadcasted_iota(jnp.int32, (LANES, nodes), 1)
    listed = packed[LISTED_ROW : LISTED_ROW + 1, :].astype(jnp.int32)
    column = jnp.broadcast_to(listed, (LANES, LANES)).T
    wide = jnp.concatenate([column] * (nodes // LANES), axis=1)
    slot = lax.broadcasted_iota(jnp.int32, (LANES, nodes), 0) + 1
    found = jnp.sum(jnp.where(wide == lane, slot, 0), axis=0, keepdims=True)
    inverse_index[...] = jnp.broadcast_to(found - 1, (8, nodes))
    swapped = packed[SWAPPED_ROW : SWAPPED_ROW + 1, :].astype(jnp.int32)
    index = jnp.broadcast_to(swapped, (8, LANES))
    pick_index[...] = index
    set_field(packed, incidence, field)

    reference_rows = 3 * POINTS
    shape_rows = jnp.concatenate(
        [shape_t[...], jnp.zeros((EL_NODES, LANES - reference_rows), jnp.float32)], axis=1
    )
    shape_rows = jnp.concatenate(
        [shape_rows, jnp.zeros((LANES - EL_NODES, LANES), jnp.float32)], axis=0
    )
    shape_columns = shape_rows.T
    for n in range(EL_NODES):
        wide_gradient[n] = jnp.broadcast_to(
            shape_columns[0:reference_rows, n : n + 1], (reference_rows, LANES)
        )
    for m in range(reference_rows):
        wide_force[m] = jnp.broadcast_to(shape_rows[0:NODE_ROWS, m : m + 1], (NODE_ROWS, LANES))


def contract(table, columns, count):
    sums = [[None, None] for _ in columns]
    for i in range(count):
        weights = table[i]
        for c, column in enumerate(columns):
            term = weights * column[i : i + 1, :]
            old = sums[c][i % 2]
            sums[c][i % 2] = term if old is None else old + term
    return [even + odd for even, odd in sums]


def wave_row(wave, width):
    return jnp.concatenate([wave[0:1, :]] * (width // LANES), axis=1)


def moved_up(wave):
    return pltpu.roll(wave[...], STEPS - 1, 0)


def strain_and_force(
    displace,
    strain,
    connect,
    wide_gradient,
    wide_force,
    inverse_jacobian,
    lame_moduli,
    point_weights,
    incidence,
    need_force,
):
    index = connect[...]
    low = jnp.bitwise_and(index, LANES - 1)
    chunk = jnp.right_shift(index, 7)
    is_chunk = [chunk == j for j in range(1, displace.shape[1] // LANES)]
    columns = []
    for c in range(3):
        pieces = []
        for b in range(NODE_ROWS // 8):
            rows = slice(8 * b, 8 * b + 8)
            out = None
            for j in range(displace.shape[1] // LANES):
                row = jnp.broadcast_to(displace[c : c + 1, j * LANES : (j + 1) * LANES], (8, LANES))
                taken = lane_gather(row, low[rows])
                out = taken if j == 0 else jnp.where(is_chunk[j - 1][rows], taken, out)
            pieces.append(out)
        columns.append(jnp.concatenate(pieces, axis=0))
    along = contract(wide_gradient, columns, EL_NODES)
    jac = [inverse_jacobian[i : i + 1, :] for i in range(9)]

    def ref_derivative(c, r):
        return along[c][r * POINTS : (r + 1) * POINTS, :]

    grad = [
        [
            (ref_derivative(c, 0) * jac[d] + ref_derivative(c, 1) * jac[3 + d])
            + ref_derivative(c, 2) * jac[6 + d]
            for d in range(3)
        ]
        for c in range(3)
    ]
    shear = {(c, d): grad[c][d] + grad[d][c] for c, d in ((1, 2), (0, 2), (0, 1))}
    rows = [grad[0][0], grad[1][1], grad[2][2]] + [0.5 * shear[k] for k in ((1, 2), (0, 2), (0, 1))]
    for s in range(STRAIN):
        strain[s * POINTS : (s + 1) * POINTS, :] = rows[s]
    if not need_force:
        return None
    volume = (grad[0][0] + grad[1][1]) + grad[2][2]
    weights = point_weights[...]
    shear_scale = lame_moduli[1:2, :] * weights
    pressure = (lame_moduli[0:1, :] * weights) * volume
    stress = [[None] * 3 for _ in range(3)]
    for c in range(3):
        for d in range(3):
            if c == d:
                stress[c][d] = shear_scale * (grad[c][c] + grad[c][c]) + pressure
            else:
                stress[c][d] = shear_scale * shear[(min(c, d), max(c, d))]
    columns = []
    for c in range(3):
        mapped = [
            (stress[c][0] * jac[3 * r] + stress[c][1] * jac[3 * r + 1])
            + stress[c][2] * jac[3 * r + 2]
            for r in range(3)
        ]
        columns.append(jnp.concatenate(mapped, axis=0))
    node_forces = contract(wide_force, columns, 3 * POINTS)
    row_id = lax.broadcasted_iota(jnp.int32, (8, LANES), 0) % 4
    pieces = []
    for n in range(EL_NODES):
        first, second, third = (
            jnp.broadcast_to(node_forces[c][n : n + 1, :], (8, LANES))
            for c in range(3)
        )
        pieces.append(jnp.where(row_id == 0, first, jnp.where(row_id == 1, second, third)))
    chunks = [chunk[n : n + 1, :] for n in range(EL_NODES)]
    return scatter_nodes(pieces, chunks, incidence[...])


def first_kernel(
    wave,
    dom1,
    grp1,
    dom0,
    grp0,
    source,
    inverse_index,
    pick_index,
    field,
    connect,
    wide_gradient,
    wide_force,
    inverse_jacobian,
    lame_moduli,
    point_weights,
    incidence,
    strain,
    displace,
    velocity,
    pattern,
    half_inverse_mass,
    force,
    send,
    next_wave,
):
    next_wave[...] = moved_up(wave)
    received = merge_received(source[...], dom1[...], grp1[...], dom0[...], grp0[...])
    total = field[...] + spread(received, inverse_index[...])
    scale = jnp.broadcast_to(time_step * (1.0 / total[3:4, :]), total.shape)
    pattern[...] = total
    half_inverse_mass[...] = scale
    new_velocity = scale * (wave_row(wave, total.shape[1]) * total)
    velocity[...] = new_velocity
    new_displace = time_step * new_velocity
    displace[...] = new_displace
    new_force = strain_and_force(
        new_displace,
        strain,
        connect,
        wide_gradient,
        wide_force,
        inverse_jacobian,
        lame_moduli,
        point_weights,
        incidence,
        True,
    )
    force[...] = new_force
    send[...] = pick_lanes(new_force, pick_index[...])


def step_kernel(
    wave,
    dom1,
    grp1,
    dom0,
    grp0,
    source,
    inverse_index,
    pick_index,
    connect,
    wide_gradient,
    wide_force,
    inverse_jacobian,
    lame_moduli,
    point_weights,
    incidence,
    pattern,
    half_inverse_mass,
    old_displace,
    old_velocity,
    old_force,
    strain,
    *rest,
):
    received = merge_received(source[...], dom1[...], grp1[...], dom0[...], grp0[...])
    stiff = old_force[...] + spread(received, inverse_index[...])
    total = wave_row(wave, stiff.shape[1]) * pattern[...] - stiff
    new_velocity = old_velocity[...] + half_inverse_mass[...] * total
    new_displace = old_displace[...] + time_step * new_velocity
    new_force = strain_and_force(
        new_displace,
        strain,
        connect,
        wide_gradient,
        wide_force,
        inverse_jacobian,
        lame_moduli,
        point_weights,
        incidence,
        bool(rest),
    )
    if rest:
        displace, velocity, force, send, next_wave = rest
        next_wave[...] = moved_up(wave)
        displace[...] = new_displace
        velocity[...] = new_velocity
        force[...] = new_force
        send[...] = pick_lanes(new_force, pick_index[...])


def order_kernel(rank, strains, last, out, store):
    for t in range(STEPS):
        for c in range(STRAIN):
            row = (c * STEPS + t) * POINTS
            rows = slice(c * POINTS, (c + 1) * POINTS)
            store[row : row + POINTS, :] = strains[t, rows, :] if t < STEPS - 1 else last[rows, :]
    lane = lax.broadcasted_iota(jnp.int32, (LANES, ORDER_WIDTH), 1)
    groups = rank.shape[0] * LANES // ORDER_WIDTH
    values, chosen = [], []
    for q in range(POINTS):
        block = store[pl.ds(q, STEPS * STRAIN, stride=POINTS), :]
        row = rank[q : q + 1, :]
        group = row // ORDER_WIDTH
        masked = [jnp.where(group == k, block, 0.0) for k in range(groups)]
        values.append(jnp.concatenate(masked, axis=0).astype(jnp.bfloat16))
        column = jnp.broadcast_to(row % ORDER_WIDTH, (LANES, LANES)).T
        wide = jnp.concatenate([column] * (ORDER_WIDTH // LANES), axis=1)
        chosen.append(jnp.where(wide == lane, 1.0, 0.0).astype(jnp.bfloat16))
    total = matmul(jnp.concatenate(values, axis=1), jnp.concatenate(chosen, axis=0))
    height = STEPS * STRAIN
    for w in range(rank.shape[0]):
        k, i = w * LANES // ORDER_WIDTH, w % (ORDER_WIDTH // LANES)
        block = total[k * height : (k + 1) * height, i * LANES : (i + 1) * LANES]
        out[w] = block.astype(jnp.bfloat16)


def place_kernel(pieces, out):
    for w in range(pieces.shape[0]):
        held = snake("dom", w)
        for c in range(STRAIN):
            out[c, :, w * LANES : (w + 1) * LANES] = pieces[held, c * STEPS : (c + 1) * STEPS, :]


def shards(
    connect,
    interface_nodes,
    neighbours,
    point_rank,
    shape_grad,
    inverse_jacobian,
    lame_moduli,
    point_weights,
    mass_elem,
    source_pattern,
    wavelet,
):
    nodes = source_pattern.shape[1]
    f32 = jnp.float32
    field_t = jax.ShapeDtypeStruct((8, nodes), f32)
    lanes_t = jax.ShapeDtypeStruct((8, LANES), f32)
    index_t = jax.ShapeDtypeStruct((8, LANES), jnp.int32)
    strain_t = jax.ShapeDtypeStruct((STRAIN * POINTS, LANES), f32)

    face = lax.broadcasted_iota(jnp.int32, (8, LANES), 1) // (LANES // FACES)
    dom = lax.axis_index("dom")
    parity = jnp.where(face < 2, lax.axis_index("grp") % 2, (dom // DOM_ROW + dom) % 2)
    source = 2 * (face // 2) + jnp.bitwise_xor(parity, 1 - face % 2)

    def exchange(send):
        received = []
        for name in EXCHANGES:
            axis, offset = name[:3], int(name[3])
            count = lax.axis_size(axis)
            pairs = []
            for i in range(offset, count - 1, 2):
                first, second = snake(axis, i), snake(axis, i + 1)
                pairs += [(first, second), (second, first)]
            received.append(lax.ppermute(send, axis, pairs))
        return received

    i32, bf16 = jnp.int32, jnp.bfloat16
    rank_rows = point_rank.reshape(POINTS, LANES)
    arguments = (
        wavelet,
        neighbours,
        connect,
        interface_nodes,
        mass_elem,
        source_pattern,
        shape_grad.T,
        inverse_jacobian,
        lame_moduli,
        point_weights,
        rank_rows,
    )
    buffers = [pltpu.SMEM(x.shape, x.dtype) for x in arguments[:2]]
    buffers += [pltpu.VMEM(x.shape, x.dtype) for x in arguments[2:6] + arguments[7:]]
    packed, shape_t, wave, send = kernel_call(
        pack_kernel,
        [
            jax.ShapeDtypeStruct((PACKED_ROWS, LANES), f32),
            jax.ShapeDtypeStruct(shape_grad.T.shape, f32),
            jax.ShapeDtypeStruct((STEPS, LANES), f32),
            lanes_t,
        ],
        [HBM] * len(arguments),
        scratch=buffers
        + [
            pltpu.SemaphoreType.DMA((len(arguments),)),
            pltpu.VMEM((EL_NODES * LANES, LANES), bf16),
            pltpu.VMEM(field_t.shape, f32),
        ],
    )(*(pltpu.with_memory_space_constraint(x, pltpu.MemorySpace.HBM) for x in arguments))
    writers = lax.axis_size("dom")
    packed = lax.ppermute(packed, "dom", [(i, snake("dom", i)) for i in range(writers)])
    received = []
    for name in EXCHANGES:
        axis, offset = name[:3], int(name[3])
        pairs = []
        for g in range(lax.axis_size("grp")):
            for w in range(writers):
                index, count = (g, lax.axis_size("grp")) if axis == "grp" else (w, writers)
                other = index + 1 if index % 2 == offset else index - 1
                if 0 <= other < count:
                    to_g, to_w = (other, w) if axis == "grp" else (g, other)
                    target = to_g * writers + snake("dom", to_w)
                    pairs.append((g * writers + w, target))
        received.append(lax.ppermute(send, ("grp", "dom"), pairs))

    prepare = kernel_call(
        prepare_kernel,
        [
            jax.ShapeDtypeStruct((EL_NODES * LANES, LANES), bf16),
            field_t,
            index_t,
            jax.ShapeDtypeStruct((8, nodes), i32),
            jax.ShapeDtypeStruct((NODE_ROWS, LANES), i32),
            jax.ShapeDtypeStruct((EL_NODES, 3 * POINTS, LANES), f32),
            jax.ShapeDtypeStruct((3 * POINTS, NODE_ROWS, LANES), f32),
            jax.ShapeDtypeStruct(inverse_jacobian.shape, f32),
            jax.ShapeDtypeStruct(lame_moduli.shape, f32),
            jax.ShapeDtypeStruct(point_weights.shape, f32),
            jax.ShapeDtypeStruct(rank_rows.shape, i32),
        ],
        [VMEM, VMEM],
    )
    outs = prepare(packed, shape_t)
    incidence, field, pick_index, inverse_index = outs[:4]
    rank = outs[10]
    element_data = (*outs[4:10], incidence)
    wave_t = jax.ShapeDtypeStruct((STEPS, LANES), f32)
    strain, displace, velocity, pattern, half_inverse_mass, force, send, wave = kernel_call(
        first_kernel,
        [strain_t, field_t, field_t, field_t, field_t, field_t, lanes_t, wave_t],
        [VMEM] * 16,
    )(wave, *received, source, inverse_index, pick_index, field, *element_data)
    strains = jnp.zeros((STEPS - 1, STRAIN * POINTS, LANES), f32)
    strains = lax.dynamic_update_index_in_dim(strains, strain, 0, 0)

    def advance(last, displace, velocity, force, send, wave):
        received = exchange(send)
        return kernel_call(
            step_kernel,
            [strain_t] + ([] if last else [field_t, field_t, field_t, lanes_t, wave_t]),
            [VMEM] * 20,
        )(
            wave,
            *received,
            source,
            inverse_index,
            pick_index,
            *element_data,
            pattern,
            half_inverse_mass,
            displace,
            velocity,
            force,
        )

    def body(step, carried):
        strains, *state = carried
        strain, *state = advance(False, *state)
        return (lax.dynamic_update_index_in_dim(strains, strain, step, 0), *state)

    carried = (strains, displace, velocity, force, send, wave)
    strains, *state = lax.fori_loop(1, STEPS - 1, body, carried)
    (strain,) = advance(True, *state)
    (ordered,) = kernel_call(
        order_kernel,
        [jax.ShapeDtypeStruct((writers, STEPS * STRAIN, LANES), jnp.bfloat16)],
        [VMEM] * 3,
        scratch=[pltpu.VMEM((STEPS * STRAIN * POINTS, LANES), f32)],
    )(rank, strains, strain)
    pieces = lax.all_to_all(ordered, "dom", split_axis=0, concat_axis=0, tiled=True)
    (placed,) = kernel_call(
        place_kernel, [jax.ShapeDtypeStruct((STRAIN, STEPS, writers * LANES), jnp.bfloat16)], [VMEM]
    )(pieces)
    return placed.transpose(1, 0, 2)


def solution(mesh):
    placed = (
        P(None, ("grp", "dom")),
        P(("grp", "dom"), None, None),
        P(("grp", "dom"), None),
        P(("grp", "dom"), None),
        P(),
        P(None, ("grp", "dom")),
        P(None, ("grp", "dom")),
        P(None, ("grp", "dom")),
        P(None, ("grp", "dom")),
        P(None, ("grp", "dom")),
        P(),
    )
    return jax.shard_map(
        shards, mesh=mesh, in_specs=placed, out_specs=P(None, None, ("grp", "dom")), check_vma=False
    )
```

profile of v0, /device:TPU:200, one launch (start us, length us, event | category | flops | bytes accessed | tf_op | source)
XLA Modules:
  0.0 283.9 jit_solution(2778924578028657602)
XLA Ops:
  12.8 232.0 %while.26 = (s32[]{:T(128)}, f32[15,96,128]{2,1,0:T(8,128)S(1)}, f32[8,512]{1,0:T(8,128)S(1)}, f32[8,512]{1,0:T(8,128)S(1)}, f32[8,512]{1,0:T(8,128)S(1)}, /*ind...) while((s32[]{:T(128)}, f32[15,96,128]{2,1,0:T(8,128)S(1)}, ...), condition=%wide.region_1.2_spmd.clone, body=%wide.region_0.1_spmd.clone.sunk | while | flops 26629 | bytes 284211 | solution.py:645
  13.5 5.0 %collective-permute-start.3 = (f32[8,128]{1,0:T(8,128)S(1)}, f32[8,128]{1,0:T(8,128)S(1)}, u32[]{:S(2)}, u32[]{:S(2)}) collective-permute-start(f32[8,128]{1,0:T(8,128)S(1)} %get-tuple-element.786), channel_id=1, source_target_pairs={{0,16},{16,0},{32,48},{48,32},{64,80},{80,64},{96,112},{112,96},{1... | collective-permute-start | bytes 12296 | tf_op jit(solution)/shard_map/while/body/eval_jaxpr/ppermute | solution.py:537
  18.5 7.4 %collective-permute-start.2 = (f32[8,128]{1,0:T(8,128)S(1)}, f32[8,128]{1,0:T(8,128)S(1)}, u32[]{:S(2)}, u32[]{:S(2)}) collective-permute-start(f32[8,128]{1,0:T(8,128)S(1)} %get-tuple-element.786), channel_id=1, source_target_pairs={{0,1},{1,0},{2,3},{3,2},{7,6},{6,7},{5,4},{4,5},{8,9},{9,8},{10,11... | collective-permute-start | bytes 12296 | tf_op jit(solution)/shard_map/while/body/eval_jaxpr/ppermute | solution.py:537
  36.1 15.2 %collective-permute-start.2 = (f32[8,128]{1,0:T(8,128)S(1)}, f32[8,128]{1,0:T(8,128)S(1)}, u32[]{:S(2)}, u32[]{:S(2)}) collective-permute-start(f32[8,128]{1,0:T(8,128)S(1)} %get-tuple-element.786), channel_id=1, source_target_pairs={{0,1},{1,0},{2,3},{3,2},{7,6},{6,7},{5,4},{4,5},{8,9},{9,8},{10,11... | collective-permute-start | bytes 12296 | tf_op jit(solution)/shard_map/while/body/eval_jaxpr/ppermute | solution.py:537
  75.1 5.8 %collective-permute-start.2 = (f32[8,128]{1,0:T(8,128)S(1)}, f32[8,128]{1,0:T(8,128)S(1)}, u32[]{:S(2)}, u32[]{:S(2)}) collective-permute-start(f32[8,128]{1,0:T(8,128)S(1)} %get-tuple-element.786), channel_id=1, source_target_pairs={{0,1},{1,0},{2,3},{3,2},{7,6},{6,7},{5,4},{4,5},{8,9},{9,8},{10,11... | collective-permute-start | bytes 12296 | tf_op jit(solution)/shard_map/while/body/eval_jaxpr/ppermute | solution.py:537
  91.1 5.8 %collective-permute-start.2 = (f32[8,128]{1,0:T(8,128)S(1)}, f32[8,128]{1,0:T(8,128)S(1)}, u32[]{:S(2)}, u32[]{:S(2)}) collective-permute-start(f32[8,128]{1,0:T(8,128)S(1)} %get-tuple-element.786), channel_id=1, source_target_pairs={{0,1},{1,0},{2,3},{3,2},{7,6},{6,7},{5,4},{4,5},{8,9},{9,8},{10,11... | collective-permute-start | bytes 12296 | tf_op jit(solution)/shard_map/while/body/eval_jaxpr/ppermute | solution.py:537
  103.3 4.3 %collective-permute-start.3 = (f32[8,128]{1,0:T(8,128)S(1)}, f32[8,128]{1,0:T(8,128)S(1)}, u32[]{:S(2)}, u32[]{:S(2)}) collective-permute-start(f32[8,128]{1,0:T(8,128)S(1)} %get-tuple-element.786), channel_id=1, source_target_pairs={{0,16},{16,0},{32,48},{48,32},{64,80},{80,64},{96,112},{112,96},{1... | collective-permute-start | bytes 12296 | tf_op jit(solution)/shard_map/while/body/eval_jaxpr/ppermute | solution.py:537
  107.6 4.9 %collective-permute-start.2 = (f32[8,128]{1,0:T(8,128)S(1)}, f32[8,128]{1,0:T(8,128)S(1)}, u32[]{:S(2)}, u32[]{:S(2)}) collective-permute-start(f32[8,128]{1,0:T(8,128)S(1)} %get-tuple-element.786), channel_id=1, source_target_pairs={{0,1},{1,0},{2,3},{3,2},{7,6},{6,7},{5,4},{4,5},{8,9},{9,8},{10,11... | collective-permute-start | bytes 12296 | tf_op jit(solution)/shard_map/while/body/eval_jaxpr/ppermute | solution.py:537
  123.2 5.0 %collective-permute-start.2 = (f32[8,128]{1,0:T(8,128)S(1)}, f32[8,128]{1,0:T(8,128)S(1)}, u32[]{:S(2)}, u32[]{:S(2)}) collective-permute-start(f32[8,128]{1,0:T(8,128)S(1)} %get-tuple-element.786), channel_id=1, source_target_pairs={{0,1},{1,0},{2,3},{3,2},{7,6},{6,7},{5,4},{4,5},{8,9},{9,8},{10,11... | collective-permute-start | bytes 12296 | tf_op jit(solution)/shard_map/while/body/eval_jaxpr/ppermute | solution.py:537
  134.6 4.3 %collective-permute-start.3 = (f32[8,128]{1,0:T(8,128)S(1)}, f32[8,128]{1,0:T(8,128)S(1)}, u32[]{:S(2)}, u32[]{:S(2)}) collective-permute-start(f32[8,128]{1,0:T(8,128)S(1)} %get-tuple-element.786), channel_id=1, source_target_pairs={{0,16},{16,0},{32,48},{48,32},{64,80},{80,64},{96,112},{112,96},{1... | collective-permute-start | bytes 12296 | tf_op jit(solution)/shard_map/while/body/eval_jaxpr/ppermute | solution.py:537
  138.9 5.4 %collective-permute-start.2 = (f32[8,128]{1,0:T(8,128)S(1)}, f32[8,128]{1,0:T(8,128)S(1)}, u32[]{:S(2)}, u32[]{:S(2)}) collective-permute-start(f32[8,128]{1,0:T(8,128)S(1)} %get-tuple-element.786), channel_id=1, source_target_pairs={{0,1},{1,0},{2,3},{3,2},{7,6},{6,7},{5,4},{4,5},{8,9},{9,8},{10,11... | collective-permute-start | bytes 12296 | tf_op jit(solution)/shard_map/while/body/eval_jaxpr/ppermute | solution.py:537
  150.8 4.3 %collective-permute-start.3 = (f32[8,128]{1,0:T(8,128)S(1)}, f32[8,128]{1,0:T(8,128)S(1)}, u32[]{:S(2)}, u32[]{:S(2)}) collective-permute-start(f32[8,128]{1,0:T(8,128)S(1)} %get-tuple-element.786), channel_id=1, source_target_pairs={{0,16},{16,0},{32,48},{48,32},{64,80},{80,64},{96,112},{112,96},{1... | collective-permute-start | bytes 12296 | tf_op jit(solution)/shard_map/while/body/eval_jaxpr/ppermute | solution.py:537
  155.1 5.2 %collective-permute-start.2 = (f32[8,128]{1,0:T(8,128)S(1)}, f32[8,128]{1,0:T(8,128)S(1)}, u32[]{:S(2)}, u32[]{:S(2)}) collective-permute-start(f32[8,128]{1,0:T(8,128)S(1)} %get-tuple-element.786), channel_id=1, source_target_pairs={{0,1},{1,0},{2,3},{3,2},{7,6},{6,7},{5,4},{4,5},{8,9},{9,8},{10,11... | collective-permute-start | bytes 12296 | tf_op jit(solution)/shard_map/while/body/eval_jaxpr/ppermute | solution.py:537
  166.7 4.3 %collective-permute-start.3 = (f32[8,128]{1,0:T(8,128)S(1)}, f32[8,128]{1,0:T(8,128)S(1)}, u32[]{:S(2)}, u32[]{:S(2)}) collective-permute-start(f32[8,128]{1,0:T(8,128)S(1)} %get-tuple-element.786), channel_id=1, source_target_pairs={{0,16},{16,0},{32,48},{48,32},{64,80},{80,64},{96,112},{112,96},{1... | collective-permute-start | bytes 12296 | tf_op jit(solution)/shard_map/while/body/eval_jaxpr/ppermute | solution.py:537
  171.0 4.9 %collective-permute-start.2 = (f32[8,128]{1,0:T(8,128)S(1)}, f32[8,128]{1,0:T(8,128)S(1)}, u32[]{:S(2)}, u32[]{:S(2)}) collective-permute-start(f32[8,128]{1,0:T(8,128)S(1)} %get-tuple-element.786), channel_id=1, source_target_pairs={{0,1},{1,0},{2,3},{3,2},{7,6},{6,7},{5,4},{4,5},{8,9},{9,8},{10,11... | collective-permute-start | bytes 12296 | tf_op jit(solution)/shard_map/while/body/eval_jaxpr/ppermute | solution.py:537
  182.3 4.3 %collective-permute-start.3 = (f32[8,128]{1,0:T(8,128)S(1)}, f32[8,128]{1,0:T(8,128)S(1)}, u32[]{:S(2)}, u32[]{:S(2)}) collective-permute-start(f32[8,128]{1,0:T(8,128)S(1)} %get-tuple-element.786), channel_id=1, source_target_pairs={{0,16},{16,0},{32,48},{48,32},{64,80},{80,64},{96,112},{112,96},{1... | collective-permute-start | bytes 12296 | tf_op jit(solution)/shard_map/while/body/eval_jaxpr/ppermute | solution.py:537
  186.6 5.0 %collective-permute-start.2 = (f32[8,128]{1,0:T(8,128)S(1)}, f32[8,128]{1,0:T(8,128)S(1)}, u32[]{:S(2)}, u32[]{:S(2)}) collective-permute-start(f32[8,128]{1,0:T(8,128)S(1)} %get-tuple-element.786), channel_id=1, source_target_pairs={{0,1},{1,0},{2,3},{3,2},{7,6},{6,7},{5,4},{4,5},{8,9},{9,8},{10,11... | collective-permute-start | bytes 12296 | tf_op jit(solution)/shard_map/while/body/eval_jaxpr/ppermute | solution.py:537
  202.4 5.4 %collective-permute-start.2 = (f32[8,128]{1,0:T(8,128)S(1)}, f32[8,128]{1,0:T(8,128)S(1)}, u32[]{:S(2)}, u32[]{:S(2)}) collective-permute-start(f32[8,128]{1,0:T(8,128)S(1)} %get-tuple-element.786), channel_id=1, source_target_pairs={{0,1},{1,0},{2,3},{3,2},{7,6},{6,7},{5,4},{4,5},{8,9},{9,8},{10,11... | collective-permute-start | bytes 12296 | tf_op jit(solution)/shard_map/while/body/eval_jaxpr/ppermute | solution.py:537
  218.5 4.9 %collective-permute-start.2 = (f32[8,128]{1,0:T(8,128)S(1)}, f32[8,128]{1,0:T(8,128)S(1)}, u32[]{:S(2)}, u32[]{:S(2)}) collective-permute-start(f32[8,128]{1,0:T(8,128)S(1)} %get-tuple-element.786), channel_id=1, source_target_pairs={{0,1},{1,0},{2,3},{3,2},{7,6},{6,7},{5,4},{4,5},{8,9},{9,8},{10,11... | collective-permute-start | bytes 12296 | tf_op jit(solution)/shard_map/while/body/eval_jaxpr/ppermute | solution.py:537
  229.8 4.3 %collective-permute-start.3 = (f32[8,128]{1,0:T(8,128)S(1)}, f32[8,128]{1,0:T(8,128)S(1)}, u32[]{:S(2)}, u32[]{:S(2)}) collective-permute-start(f32[8,128]{1,0:T(8,128)S(1)} %get-tuple-element.786), channel_id=1, source_target_pairs={{0,16},{16,0},{32,48},{48,32},{64,80},{80,64},{96,112},{112,96},{1... | collective-permute-start | bytes 12296 | tf_op jit(solution)/shard_map/while/body/eval_jaxpr/ppermute | solution.py:537
  234.1 5.0 %collective-permute-start.2 = (f32[8,128]{1,0:T(8,128)S(1)}, f32[8,128]{1,0:T(8,128)S(1)}, u32[]{:S(2)}, u32[]{:S(2)}) collective-permute-start(f32[8,128]{1,0:T(8,128)S(1)} %get-tuple-element.786), channel_id=1, source_target_pairs={{0,1},{1,0},{2,3},{3,2},{7,6},{6,7},{5,4},{4,5},{8,9},{9,8},{10,11... | collective-permute-start | bytes 12296 | tf_op jit(solution)/shard_map/while/body/eval_jaxpr/ppermute | solution.py:537
  247.5 8.1 %collective-permute-start.12 = (f32[8,128]{1,0:T(8,128)S(1)}, f32[8,128]{1,0:T(8,128)S(1)}, u32[]{:S(2)}, u32[]{:S(2)}) collective-permute-start(f32[8,128]{1,0:T(8,128)S(1)} %get-tuple-element.493), channel_id=1, source_target_pairs={{0,16},{16,0},{32,48},{48,32},{64,80},{80,64},{96,112},{112,96},{1... | collective-permute-start | bytes 12296 | tf_op jit(solution)/shard_map/ppermute | solution.py:537
  255.6 5.2 %collective-permute-start.11 = (f32[8,128]{1,0:T(8,128)S(1)}, f32[8,128]{1,0:T(8,128)S(1)}, u32[]{:S(2)}, u32[]{:S(2)}) collective-permute-start(f32[8,128]{1,0:T(8,128)S(1)} %get-tuple-element.493), channel_id=1, source_target_pairs={{0,1},{1,0},{2,3},{3,2},{7,6},{6,7},{5,4},{4,5},{8,9},{9,8},{10,11... | collective-permute-start | bytes 12296 | tf_op jit(solution)/shard_map/ppermute | solution.py:537
  263.9 19.2 %all_to_all.5.pieces = bf16[16,96,128]{2,1,0:T(8,128)(2,1)S(1)} all-to-all(bf16[16,96,128]{2,1,0:T(8,128)(2,1)S(1)} %shard_map.113), channel_id=1, replica_groups=mesh['grp'=32,'dom'=16] {'dom'}, dimensions={0} | all-to-all | bytes 786432 | tf_op jit(solution)/shard_map/all_to_all | solution.py:653
  (216 shorter events, 138.6 us)
Async XLA Ops:
  12.8 15.1 %collective-permute-start = (f32[8,128]{1,0:T(8,128)S(1)}, f32[8,128]{1,0:T(8,128)S(1)}, u32[]{:S(2)}, u32[]{:S(2)}) collective-permute-start(f32[8,128]{1,0:T(8,128)S(1)} %get-tuple-element.786), channel_id=1, source_target_pairs={{1,2},{2,1},{3,7},{7,3},{6,5},{5,6},{4,8},{8,4},{9,10},{10,9},{11,... | collective-permute-start | bytes 12296 | tf_op jit(solution)/shard_map/while/body/eval_jaxpr/ppermute | solution.py:537
  13.5 14.4 %collective-permute-start.3 = (f32[8,128]{1,0:T(8,128)S(1)}, f32[8,128]{1,0:T(8,128)S(1)}, u32[]{:S(2)}, u32[]{:S(2)}) collective-permute-start(f32[8,128]{1,0:T(8,128)S(1)} %get-tuple-element.786), channel_id=1, source_target_pairs={{0,16},{16,0},{32,48},{48,32},{64,80},{80,64},{96,112},{112,96},{1... | collective-permute-start | bytes 12296 | tf_op jit(solution)/shard_map/while/body/eval_jaxpr/ppermute | solution.py:537
  31.7 21.7 %collective-permute-start = (f32[8,128]{1,0:T(8,128)S(1)}, f32[8,128]{1,0:T(8,128)S(1)}, u32[]{:S(2)}, u32[]{:S(2)}) collective-permute-start(f32[8,128]{1,0:T(8,128)S(1)} %get-tuple-element.786), channel_id=1, source_target_pairs={{1,2},{2,1},{3,7},{7,3},{6,5},{5,6},{4,8},{8,4},{9,10},{10,9},{11,... | collective-permute-start | bytes 12296 | tf_op jit(solution)/shard_map/while/body/eval_jaxpr/ppermute | solution.py:537
  32.3 21.0 %collective-permute-start.3 = (f32[8,128]{1,0:T(8,128)S(1)}, f32[8,128]{1,0:T(8,128)S(1)}, u32[]{:S(2)}, u32[]{:S(2)}) collective-permute-start(f32[8,128]{1,0:T(8,128)S(1)} %get-tuple-element.786), channel_id=1, source_target_pairs={{0,16},{16,0},{32,48},{48,32},{64,80},{80,64},{96,112},{112,96},{1... | collective-permute-start | bytes 12296 | tf_op jit(solution)/shard_map/while/body/eval_jaxpr/ppermute | solution.py:537
  36.1 17.3 %collective-permute-start.2 = (f32[8,128]{1,0:T(8,128)S(1)}, f32[8,128]{1,0:T(8,128)S(1)}, u32[]{:S(2)}, u32[]{:S(2)}) collective-permute-start(f32[8,128]{1,0:T(8,128)S(1)} %get-tuple-element.786), channel_id=1, source_target_pairs={{0,1},{1,0},{2,3},{3,2},{7,6},{6,7},{5,4},{4,5},{8,9},{9,8},{10,11... | collective-permute-start | bytes 12296 | tf_op jit(solution)/shard_map/while/body/eval_jaxpr/ppermute | solution.py:537
  70.7 12.2 %collective-permute-start = (f32[8,128]{1,0:T(8,128)S(1)}, f32[8,128]{1,0:T(8,128)S(1)}, u32[]{:S(2)}, u32[]{:S(2)}) collective-permute-start(f32[8,128]{1,0:T(8,128)S(1)} %get-tuple-element.786), channel_id=1, source_target_pairs={{1,2},{2,1},{3,7},{7,3},{6,5},{5,6},{4,8},{8,4},{9,10},{10,9},{11,... | collective-permute-start | bytes 12296 | tf_op jit(solution)/shard_map/while/body/eval_jaxpr/ppermute | solution.py:537
  71.4 11.6 %collective-permute-start.3 = (f32[8,128]{1,0:T(8,128)S(1)}, f32[8,128]{1,0:T(8,128)S(1)}, u32[]{:S(2)}, u32[]{:S(2)}) collective-permute-start(f32[8,128]{1,0:T(8,128)S(1)} %get-tuple-element.786), channel_id=1, source_target_pairs={{0,16},{16,0},{32,48},{48,32},{64,80},{80,64},{96,112},{112,96},{1... | collective-permute-start | bytes 12296 | tf_op jit(solution)/shard_map/while/body/eval_jaxpr/ppermute | solution.py:537
  86.6 12.2 %collective-permute-start = (f32[8,128]{1,0:T(8,128)S(1)}, f32[8,128]{1,0:T(8,128)S(1)}, u32[]{:S(2)}, u32[]{:S(2)}) collective-permute-start(f32[8,128]{1,0:T(8,128)S(1)} %get-tuple-element.786), channel_id=1, source_target_pairs={{1,2},{2,1},{3,7},{7,3},{6,5},{5,6},{4,8},{8,4},{9,10},{10,9},{11,... | collective-permute-start | bytes 12296 | tf_op jit(solution)/shard_map/while/body/eval_jaxpr/ppermute | solution.py:537
  87.3 11.6 %collective-permute-start.3 = (f32[8,128]{1,0:T(8,128)S(1)}, f32[8,128]{1,0:T(8,128)S(1)}, u32[]{:S(2)}, u32[]{:S(2)}) collective-permute-start(f32[8,128]{1,0:T(8,128)S(1)} %get-tuple-element.786), channel_id=1, source_target_pairs={{0,16},{16,0},{32,48},{48,32},{64,80},{80,64},{96,112},{112,96},{1... | collective-permute-start | bytes 12296 | tf_op jit(solution)/shard_map/while/body/eval_jaxpr/ppermute | solution.py:537
  102.6 11.9 %collective-permute-start = (f32[8,128]{1,0:T(8,128)S(1)}, f32[8,128]{1,0:T(8,128)S(1)}, u32[]{:S(2)}, u32[]{:S(2)}) collective-permute-start(f32[8,128]{1,0:T(8,128)S(1)} %get-tuple-element.786), channel_id=1, source_target_pairs={{1,2},{2,1},{3,7},{7,3},{6,5},{5,6},{4,8},{8,4},{9,10},{10,9},{11,... | collective-permute-start | bytes 12296 | tf_op jit(solution)/shard_map/while/body/eval_jaxpr/ppermute | solution.py:537
  118.2 12.0 %collective-permute-start = (f32[8,128]{1,0:T(8,128)S(1)}, f32[8,128]{1,0:T(8,128)S(1)}, u32[]{:S(2)}, u32[]{:S(2)}) collective-permute-start(f32[8,128]{1,0:T(8,128)S(1)} %get-tuple-element.786), channel_id=1, source_target_pairs={{1,2},{2,1},{3,7},{7,3},{6,5},{5,6},{4,8},{8,4},{9,10},{10,9},{11,... | collective-permute-start | bytes 12296 | tf_op jit(solution)/shard_map/while/body/eval_jaxpr/ppermute | solution.py:537
  134.0 12.4 %collective-permute-start = (f32[8,128]{1,0:T(8,128)S(1)}, f32[8,128]{1,0:T(8,128)S(1)}, u32[]{:S(2)}, u32[]{:S(2)}) collective-permute-start(f32[8,128]{1,0:T(8,128)S(1)} %get-tuple-element.786), channel_id=1, source_target_pairs={{1,2},{2,1},{3,7},{7,3},{6,5},{5,6},{4,8},{8,4},{9,10},{10,9},{11,... | collective-permute-start | bytes 12296 | tf_op jit(solution)/shard_map/while/body/eval_jaxpr/ppermute | solution.py:537
  134.6 11.8 %collective-permute-start.3 = (f32[8,128]{1,0:T(8,128)S(1)}, f32[8,128]{1,0:T(8,128)S(1)}, u32[]{:S(2)}, u32[]{:S(2)}) collective-permute-start(f32[8,128]{1,0:T(8,128)S(1)} %get-tuple-element.786), channel_id=1, source_target_pairs={{0,16},{16,0},{32,48},{48,32},{64,80},{80,64},{96,112},{112,96},{1... | collective-permute-start | bytes 12296 | tf_op jit(solution)/shard_map/while/body/eval_jaxpr/ppermute | solution.py:537
  150.1 12.2 %collective-permute-start = (f32[8,128]{1,0:T(8,128)S(1)}, f32[8,128]{1,0:T(8,128)S(1)}, u32[]{:S(2)}, u32[]{:S(2)}) collective-permute-start(f32[8,128]{1,0:T(8,128)S(1)} %get-tuple-element.786), channel_id=1, source_target_pairs={{1,2},{2,1},{3,7},{7,3},{6,5},{5,6},{4,8},{8,4},{9,10},{10,9},{11,... | collective-permute-start | bytes 12296 | tf_op jit(solution)/shard_map/while/body/eval_jaxpr/ppermute | solution.py:537
  150.8 11.5 %collective-permute-start.3 = (f32[8,128]{1,0:T(8,128)S(1)}, f32[8,128]{1,0:T(8,128)S(1)}, u32[]{:S(2)}, u32[]{:S(2)}) collective-permute-start(f32[8,128]{1,0:T(8,128)S(1)} %get-tuple-element.786), channel_id=1, source_target_pairs={{0,16},{16,0},{32,48},{48,32},{64,80},{80,64},{96,112},{112,96},{1... | collective-permute-start | bytes 12296 | tf_op jit(solution)/shard_map/while/body/eval_jaxpr/ppermute | solution.py:537
  166.0 11.9 %collective-permute-start = (f32[8,128]{1,0:T(8,128)S(1)}, f32[8,128]{1,0:T(8,128)S(1)}, u32[]{:S(2)}, u32[]{:S(2)}) collective-permute-start(f32[8,128]{1,0:T(8,128)S(1)} %get-tuple-element.786), channel_id=1, source_target_pairs={{1,2},{2,1},{3,7},{7,3},{6,5},{5,6},{4,8},{8,4},{9,10},{10,9},{11,... | collective-permute-start | bytes 12296 | tf_op jit(solution)/shard_map/while/body/eval_jaxpr/ppermute | solution.py:537
  181.6 12.0 %collective-permute-start = (f32[8,128]{1,0:T(8,128)S(1)}, f32[8,128]{1,0:T(8,128)S(1)}, u32[]{:S(2)}, u32[]{:S(2)}) collective-permute-start(f32[8,128]{1,0:T(8,128)S(1)} %get-tuple-element.786), channel_id=1, source_target_pairs={{1,2},{2,1},{3,7},{7,3},{6,5},{5,6},{4,8},{8,4},{9,10},{10,9},{11,... | collective-permute-start | bytes 12296 | tf_op jit(solution)/shard_map/while/body/eval_jaxpr/ppermute | solution.py:537
  197.4 12.4 %collective-permute-start = (f32[8,128]{1,0:T(8,128)S(1)}, f32[8,128]{1,0:T(8,128)S(1)}, u32[]{:S(2)}, u32[]{:S(2)}) collective-permute-start(f32[8,128]{1,0:T(8,128)S(1)} %get-tuple-element.786), channel_id=1, source_target_pairs={{1,2},{2,1},{3,7},{7,3},{6,5},{5,6},{4,8},{8,4},{9,10},{10,9},{11,... | collective-permute-start | bytes 12296 | tf_op jit(solution)/shard_map/while/body/eval_jaxpr/ppermute | solution.py:537
  198.0 11.8 %collective-permute-start.3 = (f32[8,128]{1,0:T(8,128)S(1)}, f32[8,128]{1,0:T(8,128)S(1)}, u32[]{:S(2)}, u32[]{:S(2)}) collective-permute-start(f32[8,128]{1,0:T(8,128)S(1)} %get-tuple-element.786), channel_id=1, source_target_pairs={{0,16},{16,0},{32,48},{48,32},{64,80},{80,64},{96,112},{112,96},{1... | collective-permute-start | bytes 12296 | tf_op jit(solution)/shard_map/while/body/eval_jaxpr/ppermute | solution.py:537
  213.5 11.9 %collective-permute-start = (f32[8,128]{1,0:T(8,128)S(1)}, f32[8,128]{1,0:T(8,128)S(1)}, u32[]{:S(2)}, u32[]{:S(2)}) collective-permute-start(f32[8,128]{1,0:T(8,128)S(1)} %get-tuple-element.786), channel_id=1, source_target_pairs={{1,2},{2,1},{3,7},{7,3},{6,5},{5,6},{4,8},{8,4},{9,10},{10,9},{11,... | collective-permute-start | bytes 12296 | tf_op jit(solution)/shard_map/while/body/eval_jaxpr/ppermute | solution.py:537
  229.2 12.0 %collective-permute-start = (f32[8,128]{1,0:T(8,128)S(1)}, f32[8,128]{1,0:T(8,128)S(1)}, u32[]{:S(2)}, u32[]{:S(2)}) collective-permute-start(f32[8,128]{1,0:T(8,128)S(1)} %get-tuple-element.786), channel_id=1, source_target_pairs={{1,2},{2,1},{3,7},{7,3},{6,5},{5,6},{4,8},{8,4},{9,10},{10,9},{11,... | collective-permute-start | bytes 12296 | tf_op jit(solution)/shard_map/while/body/eval_jaxpr/ppermute | solution.py:537
  244.9 15.9 %collective-permute-start.10 = (f32[8,128]{1,0:T(8,128)S(1)}, f32[8,128]{1,0:T(8,128)S(1)}, u32[]{:S(2)}, u32[]{:S(2)}) collective-permute-start(f32[8,128]{1,0:T(8,128)S(1)} %get-tuple-element.493), channel_id=1, source_target_pairs={{16,32},{32,16},{48,64},{64,48},{80,96},{96,80},{112,128},{128,112... | collective-permute-start | bytes 12296 | tf_op jit(solution)/shard_map/ppermute | solution.py:537
  246.8 14.0 %collective-permute-start.9 = (f32[8,128]{1,0:T(8,128)S(1)}, f32[8,128]{1,0:T(8,128)S(1)}, u32[]{:S(2)}, u32[]{:S(2)}) collective-permute-start(f32[8,128]{1,0:T(8,128)S(1)} %get-tuple-element.493), channel_id=1, source_target_pairs={{1,2},{2,1},{3,7},{7,3},{6,5},{5,6},{4,8},{8,4},{9,10},{10,9},{11,... | collective-permute-start | bytes 12296 | tf_op jit(solution)/shard_map/ppermute | solution.py:537
  247.5 13.3 %collective-permute-start.12 = (f32[8,128]{1,0:T(8,128)S(1)}, f32[8,128]{1,0:T(8,128)S(1)}, u32[]{:S(2)}, u32[]{:S(2)}) collective-permute-start(f32[8,128]{1,0:T(8,128)S(1)} %get-tuple-element.493), channel_id=1, source_target_pairs={{0,16},{16,0},{32,48},{48,32},{64,80},{80,64},{96,112},{112,96},{1... | collective-permute-start | bytes 12296 | tf_op jit(solution)/shard_map/ppermute | solution.py:537
  (41 other events, 283.8 us)
where the time goes:
time: 286 us; the launch traced here: 284 us
  starting transfers between devices  203 us (71%)
  waiting for transfers between devices  42.4 us (15%)
  blocking collectives  19.2 us (7%)
  Pallas kernels  16.7 us (6%)
    ppermute x60, starting transfers between devices, exchange(): received.append(lax.ppermute(send, axis, pairs))  194 us
    ppermute x60, waiting for transfers between devices, exchange(): received.append(lax.ppermute(send, axis, pairs))  42.1 us
    all_to_all x1, blocking collectives, shards(): lax.all_to_all(ordered, 'dom', split_axis=0, concat_axis=0, tiled=True)  19.2 us
    pallas_call x15, Pallas kernels, advance(): kernel_call(step_kernel, [strain_t] + ([] if last else [field_t, field_t,...  11.1 us
    ppermute x4, starting transfers between devices, shards(): received.append(lax.ppermute(send, ('grp', 'dom'), pairs))  8.16 us
  transfers between devices with their start and end apart: 65, of which 16 were waited for; matrix products, arithmetic and copies ran while one was open for 0% of the time, Pallas kernels for 0%

commit v1 on v0

--- a/solution.py
+++ b/solution.py
@@ -121,6 +121,16 @@
         incidence[n * LANES : (n + 1) * LANES, :] = jnp.where(
             column == own_lane, 1.0, 0.0
         ).astype(jnp.bfloat16)
+
+
+def set_faces(packed, faces):
+    element_nodes = packed[CONNECT_ROW : CONNECT_ROW + NODE_ROWS, :].astype(jnp.int32)
+    sent = packed[SWAPPED_ROW : SWAPPED_ROW + 1, :].astype(jnp.int32)
+    for n in range(EL_NODES):
+        column = jnp.broadcast_to(element_nodes[n : n + 1, :], (LANES, LANES)).T
+        faces[n * LANES : (n + 1) * LANES, :] = jnp.where(column == sent, 1.0, 0.0).astype(
+            jnp.bfloat16
+        )
 
 
 def set_field(packed, incidence, field):
@@ -220,7 +230,7 @@
     shape_t,
     incidence,
     field,
-    pick_index,
+    faces,
     inverse_index,
     connect,
     wide_gradient,
@@ -245,9 +255,7 @@
     slot = lax.broadcasted_iota(jnp.int32, (LANES, nodes), 0) + 1
     found = jnp.sum(jnp.where(wide == lane, slot, 0), axis=0, keepdims=True)
     inverse_index[...] = jnp.broadcast_to(found - 1, (8, nodes))
-    swapped = packed[SWAPPED_ROW : SWAPPED_ROW + 1, :].astype(jnp.int32)
-    index = jnp.broadcast_to(swapped, (8, LANES))
-    pick_index[...] = index
+    set_faces(packed, faces)
     set_field(packed, incidence, field)
 
     reference_rows = 3 * POINTS
@@ -294,7 +302,7 @@
     inverse_jacobian,
     lame_moduli,
     point_weights,
-    incidence,
+    faces,
     need_force,
 ):
     index = connect[...]
@@ -353,16 +361,34 @@
         ]
         columns.append(jnp.concatenate(mapped, axis=0))
     node_forces = contract(wide_force, columns, 3 * POINTS)
+    parts = parts_of(jnp.concatenate(node_rows(node_forces), axis=1))
+    sums = matmul(jnp.concatenate(parts, axis=0).astype(jnp.bfloat16), faces[...])
+    return node_forces, (sums[16:24] + sums[8:16]) + sums[0:8]
+
+
+def node_rows(node_forces):
     row_id = lax.broadcasted_iota(jnp.int32, (8, LANES), 0) % 4
     pieces = []
     for n in range(EL_NODES):
         first, second, third = (
-            jnp.broadcast_to(node_forces[c][n : n + 1, :], (8, LANES))
-            for c in range(3)
+            jnp.broadcast_to(node_forces[c][n : n + 1, :], (8, LANES)) for c in range(3)
         )
         pieces.append(jnp.where(row_id == 0, first, jnp.where(row_id == 1, second, third)))
+    return pieces
+
+
+def scatter_kernel(node_forces, connect, incidence, force):
+    parts = [node_forces[c] for c in range(3)]
+    chunk = jnp.right_shift(connect[...], 7)
     chunks = [chunk[n : n + 1, :] for n in range(EL_NODES)]
-    return scatter_nodes(pieces, chunks, incidence[...])
+    force[...] = scatter_nodes(node_rows(parts), chunks, incidence[...])
+
+
+def keep_forces(result, node_forces, send):
+    forces, faces = result
+    for c in range(3):
+        node_forces[c] = forces[c]
+    send[...] = faces
 
 
 def first_kernel(
@@ -373,7 +399,6 @@
     grp0,
     source,
     inverse_index,
-    pick_index,
     field,
     connect,
     wide_gradient,
@@ -381,13 +406,13 @@
     inverse_jacobian,
     lame_moduli,
     point_weights,
-    incidence,
+    faces,
     strain,
     displace,
     velocity,
     pattern,
     half_inverse_mass,
-    force,
+    node_forces,
     send,
     next_wave,
 ):
@@ -401,7 +426,7 @@
     velocity[...] = new_velocity
     new_displace = time_step * new_velocity
     displace[...] = new_displace
-    new_force = strain_and_force(
+    result = strain_and_force(
         new_displace,
         strain,
         connect,
@@ -410,11 +435,10 @@
         inverse_jacobian,
         lame_moduli,
         point_weights,
-        incidence,
+        faces,
         True,
     )
-    force[...] = new_force
-    send[...] = pick_lanes(new_force, pick_index[...])
+    keep_forces(result, node_forces, send)
 
 
 def step_kernel(
@@ -425,14 +449,13 @@
     grp0,
     source,
     inverse_index,
-    pick_index,
     connect,
     wide_gradient,
     wide_force,
     inverse_jacobian,
     lame_moduli,
     point_weights,
-    incidence,
+    faces,
     pattern,
     half_inverse_mass,
     old_displace,
@@ -446,7 +469,7 @@
     total = wave_row(wave, stiff.shape[1]) * pattern[...] - stiff
     new_velocity = old_velocity[...] + half_inverse_mass[...] * total
     new_displace = old_displace[...] + time_step * new_velocity
-    new_force = strain_and_force(
+    result = strain_and_force(
         new_displace,
         strain,
         connect,
@@ -455,16 +478,15 @@
         inverse_jacobian,
         lame_moduli,
         point_weights,
-        incidence,
+        faces,
         bool(rest),
     )
     if rest:
-        displace, velocity, force, send, next_wave = rest
+        displace, velocity, node_forces, send, next_wave = rest
         next_wave[...] = moved_up(wave)
         displace[...] = new_displace
         velocity[...] = new_velocity
-        force[...] = new_force
-        send[...] = pick_lanes(new_force, pick_index[...])
+        keep_forces(result, node_forces, send)
 
 
 def order_kernel(rank, strains, last, out, store):
@@ -517,7 +539,6 @@
     f32 = jnp.float32
     field_t = jax.ShapeDtypeStruct((8, nodes), f32)
     lanes_t = jax.ShapeDtypeStruct((8, LANES), f32)
-    index_t = jax.ShapeDtypeStruct((8, LANES), jnp.int32)
     strain_t = jax.ShapeDtypeStruct((STRAIN * POINTS, LANES), f32)
 
     face = lax.broadcasted_iota(jnp.int32, (8, LANES), 1) // (LANES // FACES)
@@ -591,7 +612,7 @@
         [
             jax.ShapeDtypeStruct((EL_NODES * LANES, LANES), bf16),
             field_t,
-            index_t,
+            jax.ShapeDtypeStruct((EL_NODES * LANES, LANES), bf16),
             jax.ShapeDtypeStruct((8, nodes), i32),
             jax.ShapeDtypeStruct((NODE_ROWS, LANES), i32),
             jax.ShapeDtypeStruct((EL_NODES, 3 * POINTS, LANES), f32),
@@ -604,30 +625,33 @@
         [VMEM, VMEM],
     )
     outs = prepare(packed, shape_t)
-    incidence, field, pick_index, inverse_index = outs[:4]
+    incidence, field, faces, inverse_index = outs[:4]
     rank = outs[10]
-    element_data = (*outs[4:10], incidence)
+    connect_rows = outs[4]
+    element_data = (*outs[4:10], faces)
     wave_t = jax.ShapeDtypeStruct((STEPS, LANES), f32)
-    strain, displace, velocity, pattern, half_inverse_mass, force, send, wave = kernel_call(
+    forces_t = jax.ShapeDtypeStruct((3, NODE_ROWS, LANES), f32)
+    strain, displace, velocity, pattern, half_inverse_mass, node_forces, send, wave = kernel_call(
         first_kernel,
-        [strain_t, field_t, field_t, field_t, field_t, field_t, lanes_t, wave_t],
-        [VMEM] * 16,
-    )(wave, *received, source, inverse_index, pick_index, field, *element_data)
+        [strain_t, field_t, field_t, field_t, field_t, forces_t, lanes_t, wave_t],
+        [VMEM] * 15,
+    )(wave, *received, source, inverse_index, field, *element_data)
     strains = jnp.zeros((STEPS - 1, STRAIN * POINTS, LANES), f32)
     strains = lax.dynamic_update_index_in_dim(strains, strain, 0, 0)
 
-    def advance(last, displace, velocity, force, send, wave):
+    def advance(last, displace, velocity, node_forces, send, wave):
         received = exchange(send)
+        scatter = kernel_call(scatter_kernel, [field_t], [VMEM] * 3)
+        (force,) = scatter(node_forces, connect_rows, incidence)
         return kernel_call(
             step_kernel,
-            [strain_t] + ([] if last else [field_t, field_t, field_t, lanes_t, wave_t]),
-            [VMEM] * 20,
+            [strain_t] + ([] if last else [field_t, field_t, forces_t, lanes_t, wave_t]),
+            [VMEM] * 19,
         )(
             wave,
             *received,
             source,
             inverse_index,
-            pick_index,
             *element_data,
             pattern,
             half_inverse_mass,
@@ -641,7 +665,7 @@
         strain, *state = advance(False, *state)
         return (lax.dynamic_update_index_in_dim(strains, strain, step, 0), *state)
 
-    carried = (strains, displace, velocity, force, send, wave)
+    carried = (strains, displace, velocity, node_forces, send, wave)
     strains, *state = lax.fori_loop(1, STEPS - 1, body, carried)
     (strain,) = advance(True, *state)
     (ordered,) = kernel_call(

time: 286 us -> 285 us (level)
  waiting for transfers between devices: 42.4 us -> 38.7 us
    pallas_call x0 -> x15, Pallas kernels: none -> 3.49 us  [advance(): force, = scatter(node_forces, connect_rows, incidence)]
    ppermute x60, waiting for transfers between devices: 42.1 us -> 38.7 us  [exchange(): received.append(lax.ppermute(send, axis, pairs))]
  transfers between devices with their start and end apart: 65 -> 65, of which waited for: 16 -> 15; matrix products, arithmetic and copies ran while one was open for 0% -> 0% of each run, Pallas kernels for 0% -> 2%
where the time goes in v1:
time: 285 us; the launch traced here: 283 us
  starting transfers between devices  203 us (71%)
  waiting for transfers between devices  38.7 us (14%)
  blocking collectives  19.2 us (7%)
  Pallas kernels  19 us (7%)
    ppermute x60, starting transfers between devices, exchange(): received.append(lax.ppermute(send, axis, pairs))  194 us
    ppermute x60, waiting for transfers between devices, exchange(): received.append(lax.ppermute(send, axis, pairs))  38.7 us
    all_to_all x1, blocking collectives, shards(): lax.all_to_all(ordered, 'dom', split_axis=0, concat_axis=0, tiled=True)  19.2 us
    pallas_call x15, Pallas kernels, advance(): kernel_call(step_kernel, [strain_t] + ([] if last else [field_t, field_t,...  9.78 us
    ppermute x4, starting transfers between devices, shards(): received.append(lax.ppermute(send, ('grp', 'dom'), pairs))  8.16 us
  transfers between devices with their start and end apart: 65, of which 15 were waited for; matrix products, arithmetic and copies ran while one was open for 0% of the time, Pallas kernels for 2%

profile of v1, /device:TPU:200, one launch (start us, length us, event | category | flops | bytes accessed | tf_op | source)
XLA Modules:
  0.0 282.8 jit_solution(5410538315190203869)
XLA Ops:
  12.8 230.9 %while.26 = (s32[]{:T(128)}, f32[15,96,128]{2,1,0:T(8,128)S(1)}, f32[8,512]{1,0:T(8,128)S(1)}, f32[8,512]{1,0:T(8,128)S(1)}, f32[3,24,128]{2,1,0:T(8,128)S(1)}, ...) while((s32[]{:T(128)}, f32[15,96,128]{2,1,0:T(8,128)S(1)}, ...), condition=%wide.region_1.2_spmd.clone, body=%wide.region_0.1_spmd.clone.sunk | while | flops 26629 | bytes 251443 | solution.py:669
  13.5 5.2 %collective-permute-start.3 = (f32[8,128]{1,0:T(8,128)S(1)}, f32[8,128]{1,0:T(8,128)S(1)}, u32[]{:S(2)}, u32[]{:S(2)}) collective-permute-start(f32[8,128]{1,0:T(8,128)S(1)} %get-tuple-element.786), channel_id=1, source_target_pairs={{0,16},{16,0},{32,48},{48,32},{64,80},{80,64},{96,112},{112,96},{1... | collective-permute-start | bytes 12296 | tf_op jit(solution)/shard_map/while/body/eval_jaxpr/ppermute | solution.py:558
  18.8 7.1 %collective-permute-start.2 = (f32[8,128]{1,0:T(8,128)S(1)}, f32[8,128]{1,0:T(8,128)S(1)}, u32[]{:S(2)}, u32[]{:S(2)}) collective-permute-start(f32[8,128]{1,0:T(8,128)S(1)} %get-tuple-element.786), channel_id=1, source_target_pairs={{0,1},{1,0},{2,3},{3,2},{7,6},{6,7},{5,4},{4,5},{8,9},{9,8},{10,11... | collective-permute-start | bytes 12296 | tf_op jit(solution)/shard_map/while/body/eval_jaxpr/ppermute | solution.py:558
  35.9 15.6 %collective-permute-start.2 = (f32[8,128]{1,0:T(8,128)S(1)}, f32[8,128]{1,0:T(8,128)S(1)}, u32[]{:S(2)}, u32[]{:S(2)}) collective-permute-start(f32[8,128]{1,0:T(8,128)S(1)} %get-tuple-element.786), channel_id=1, source_target_pairs={{0,1},{1,0},{2,3},{3,2},{7,6},{6,7},{5,4},{4,5},{8,9},{9,8},{10,11... | collective-permute-start | bytes 12296 | tf_op jit(solution)/shard_map/while/body/eval_jaxpr/ppermute | solution.py:558
  75.1 5.8 %collective-permute-start.2 = (f32[8,128]{1,0:T(8,128)S(1)}, f32[8,128]{1,0:T(8,128)S(1)}, u32[]{:S(2)}, u32[]{:S(2)}) collective-permute-start(f32[8,128]{1,0:T(8,128)S(1)} %get-tuple-element.786), channel_id=1, source_target_pairs={{0,1},{1,0},{2,3},{3,2},{7,6},{6,7},{5,4},{4,5},{8,9},{9,8},{10,11... | collective-permute-start | bytes 12296 | tf_op jit(solution)/shard_map/while/body/eval_jaxpr/ppermute | solution.py:558
  90.9 5.8 %collective-permute-start.2 = (f32[8,128]{1,0:T(8,128)S(1)}, f32[8,128]{1,0:T(8,128)S(1)}, u32[]{:S(2)}, u32[]{:S(2)}) collective-permute-start(f32[8,128]{1,0:T(8,128)S(1)} %get-tuple-element.786), channel_id=1, source_target_pairs={{0,1},{1,0},{2,3},{3,2},{7,6},{6,7},{5,4},{4,5},{8,9},{9,8},{10,11... | collective-permute-start | bytes 12296 | tf_op jit(solution)/shard_map/while/body/eval_jaxpr/ppermute | solution.py:558
  103.0 4.3 %collective-permute-start.3 = (f32[8,128]{1,0:T(8,128)S(1)}, f32[8,128]{1,0:T(8,128)S(1)}, u32[]{:S(2)}, u32[]{:S(2)}) collective-permute-start(f32[8,128]{1,0:T(8,128)S(1)} %get-tuple-element.786), channel_id=1, source_target_pairs={{0,16},{16,0},{32,48},{48,32},{64,80},{80,64},{96,112},{112,96},{1... | collective-permute-start | bytes 12296 | tf_op jit(solution)/shard_map/while/body/eval_jaxpr/ppermute | solution.py:558
  107.3 4.9 %collective-permute-start.2 = (f32[8,128]{1,0:T(8,128)S(1)}, f32[8,128]{1,0:T(8,128)S(1)}, u32[]{:S(2)}, u32[]{:S(2)}) collective-permute-start(f32[8,128]{1,0:T(8,128)S(1)} %get-tuple-element.786), channel_id=1, source_target_pairs={{0,1},{1,0},{2,3},{3,2},{7,6},{6,7},{5,4},{4,5},{8,9},{9,8},{10,11... | collective-permute-start | bytes 12296 | tf_op jit(solution)/shard_map/while/body/eval_jaxpr/ppermute | solution.py:558
  122.9 5.0 %collective-permute-start.2 = (f32[8,128]{1,0:T(8,128)S(1)}, f32[8,128]{1,0:T(8,128)S(1)}, u32[]{:S(2)}, u32[]{:S(2)}) collective-permute-start(f32[8,128]{1,0:T(8,128)S(1)} %get-tuple-element.786), channel_id=1, source_target_pairs={{0,1},{1,0},{2,3},{3,2},{7,6},{6,7},{5,4},{4,5},{8,9},{9,8},{10,11... | collective-permute-start | bytes 12296 | tf_op jit(solution)/shard_map/while/body/eval_jaxpr/ppermute | solution.py:558
  134.2 4.3 %collective-permute-start.3 = (f32[8,128]{1,0:T(8,128)S(1)}, f32[8,128]{1,0:T(8,128)S(1)}, u32[]{:S(2)}, u32[]{:S(2)}) collective-permute-start(f32[8,128]{1,0:T(8,128)S(1)} %get-tuple-element.786), channel_id=1, source_target_pairs={{0,16},{16,0},{32,48},{48,32},{64,80},{80,64},{96,112},{112,96},{1... | collective-permute-start | bytes 12296 | tf_op jit(solution)/shard_map/while/body/eval_jaxpr/ppermute | solution.py:558
  138.5 5.4 %collective-permute-start.2 = (f32[8,128]{1,0:T(8,128)S(1)}, f32[8,128]{1,0:T(8,128)S(1)}, u32[]{:S(2)}, u32[]{:S(2)}) collective-permute-start(f32[8,128]{1,0:T(8,128)S(1)} %get-tuple-element.786), channel_id=1, source_target_pairs={{0,1},{1,0},{2,3},{3,2},{7,6},{6,7},{5,4},{4,5},{8,9},{9,8},{10,11... | collective-permute-start | bytes 12296 | tf_op jit(solution)/shard_map/while/body/eval_jaxpr/ppermute | solution.py:558
  154.6 5.2 %collective-permute-start.2 = (f32[8,128]{1,0:T(8,128)S(1)}, f32[8,128]{1,0:T(8,128)S(1)}, u32[]{:S(2)}, u32[]{:S(2)}) collective-permute-start(f32[8,128]{1,0:T(8,128)S(1)} %get-tuple-element.786), channel_id=1, source_target_pairs={{0,1},{1,0},{2,3},{3,2},{7,6},{6,7},{5,4},{4,5},{8,9},{9,8},{10,11... | collective-permute-start | bytes 12296 | tf_op jit(solution)/shard_map/while/body/eval_jaxpr/ppermute | solution.py:558
  166.1 4.3 %collective-permute-start.3 = (f32[8,128]{1,0:T(8,128)S(1)}, f32[8,128]{1,0:T(8,128)S(1)}, u32[]{:S(2)}, u32[]{:S(2)}) collective-permute-start(f32[8,128]{1,0:T(8,128)S(1)} %get-tuple-element.786), channel_id=1, source_target_pairs={{0,16},{16,0},{32,48},{48,32},{64,80},{80,64},{96,112},{112,96},{1... | collective-permute-start | bytes 12296 | tf_op jit(solution)/shard_map/while/body/eval_jaxpr/ppermute | solution.py:558
  170.4 4.9 %collective-permute-start.2 = (f32[8,128]{1,0:T(8,128)S(1)}, f32[8,128]{1,0:T(8,128)S(1)}, u32[]{:S(2)}, u32[]{:S(2)}) collective-permute-start(f32[8,128]{1,0:T(8,128)S(1)} %get-tuple-element.786), channel_id=1, source_target_pairs={{0,1},{1,0},{2,3},{3,2},{7,6},{6,7},{5,4},{4,5},{8,9},{9,8},{10,11... | collective-permute-start | bytes 12296 | tf_op jit(solution)/shard_map/while/body/eval_jaxpr/ppermute | solution.py:558
  181.6 4.3 %collective-permute-start.3 = (f32[8,128]{1,0:T(8,128)S(1)}, f32[8,128]{1,0:T(8,128)S(1)}, u32[]{:S(2)}, u32[]{:S(2)}) collective-permute-start(f32[8,128]{1,0:T(8,128)S(1)} %get-tuple-element.786), channel_id=1, source_target_pairs={{0,16},{16,0},{32,48},{48,32},{64,80},{80,64},{96,112},{112,96},{1... | collective-permute-start | bytes 12296 | tf_op jit(solution)/shard_map/while/body/eval_jaxpr/ppermute | solution.py:558
  185.9 5.0 %collective-permute-start.2 = (f32[8,128]{1,0:T(8,128)S(1)}, f32[8,128]{1,0:T(8,128)S(1)}, u32[]{:S(2)}, u32[]{:S(2)}) collective-permute-start(f32[8,128]{1,0:T(8,128)S(1)} %get-tuple-element.786), channel_id=1, source_target_pairs={{0,1},{1,0},{2,3},{3,2},{7,6},{6,7},{5,4},{4,5},{8,9},{9,8},{10,11... | collective-permute-start | bytes 12296 | tf_op jit(solution)/shard_map/while/body/eval_jaxpr/ppermute | solution.py:558
  201.5 5.4 %collective-permute-start.2 = (f32[8,128]{1,0:T(8,128)S(1)}, f32[8,128]{1,0:T(8,128)S(1)}, u32[]{:S(2)}, u32[]{:S(2)}) collective-permute-start(f32[8,128]{1,0:T(8,128)S(1)} %get-tuple-element.786), channel_id=1, source_target_pairs={{0,1},{1,0},{2,3},{3,2},{7,6},{6,7},{5,4},{4,5},{8,9},{9,8},{10,11... | collective-permute-start | bytes 12296 | tf_op jit(solution)/shard_map/while/body/eval_jaxpr/ppermute | solution.py:558
  213.3 4.3 %collective-permute-start.3 = (f32[8,128]{1,0:T(8,128)S(1)}, f32[8,128]{1,0:T(8,128)S(1)}, u32[]{:S(2)}, u32[]{:S(2)}) collective-permute-start(f32[8,128]{1,0:T(8,128)S(1)} %get-tuple-element.786), channel_id=1, source_target_pairs={{0,16},{16,0},{32,48},{48,32},{64,80},{80,64},{96,112},{112,96},{1... | collective-permute-start | bytes 12296 | tf_op jit(solution)/shard_map/while/body/eval_jaxpr/ppermute | solution.py:558
  217.6 4.9 %collective-permute-start.2 = (f32[8,128]{1,0:T(8,128)S(1)}, f32[8,128]{1,0:T(8,128)S(1)}, u32[]{:S(2)}, u32[]{:S(2)}) collective-permute-start(f32[8,128]{1,0:T(8,128)S(1)} %get-tuple-element.786), channel_id=1, source_target_pairs={{0,1},{1,0},{2,3},{3,2},{7,6},{6,7},{5,4},{4,5},{8,9},{9,8},{10,11... | collective-permute-start | bytes 12296 | tf_op jit(solution)/shard_map/while/body/eval_jaxpr/ppermute | solution.py:558
  228.8 4.3 %collective-permute-start.3 = (f32[8,128]{1,0:T(8,128)S(1)}, f32[8,128]{1,0:T(8,128)S(1)}, u32[]{:S(2)}, u32[]{:S(2)}) collective-permute-start(f32[8,128]{1,0:T(8,128)S(1)} %get-tuple-element.786), channel_id=1, source_target_pairs={{0,16},{16,0},{32,48},{48,32},{64,80},{80,64},{96,112},{112,96},{1... | collective-permute-start | bytes 12296 | tf_op jit(solution)/shard_map/while/body/eval_jaxpr/ppermute | solution.py:558
  233.1 5.0 %collective-permute-start.2 = (f32[8,128]{1,0:T(8,128)S(1)}, f32[8,128]{1,0:T(8,128)S(1)}, u32[]{:S(2)}, u32[]{:S(2)}) collective-permute-start(f32[8,128]{1,0:T(8,128)S(1)} %get-tuple-element.786), channel_id=1, source_target_pairs={{0,1},{1,0},{2,3},{3,2},{7,6},{6,7},{5,4},{4,5},{8,9},{9,8},{10,11... | collective-permute-start | bytes 12296 | tf_op jit(solution)/shard_map/while/body/eval_jaxpr/ppermute | solution.py:558
  246.4 8.1 %collective-permute-start.12 = (f32[8,128]{1,0:T(8,128)S(1)}, f32[8,128]{1,0:T(8,128)S(1)}, u32[]{:S(2)}, u32[]{:S(2)}) collective-permute-start(f32[8,128]{1,0:T(8,128)S(1)} %get-tuple-element.493), channel_id=1, source_target_pairs={{0,16},{16,0},{32,48},{48,32},{64,80},{80,64},{96,112},{112,96},{1... | collective-permute-start | bytes 12296 | tf_op jit(solution)/shard_map/ppermute | solution.py:558
  254.5 5.2 %collective-permute-start.11 = (f32[8,128]{1,0:T(8,128)S(1)}, f32[8,128]{1,0:T(8,128)S(1)}, u32[]{:S(2)}, u32[]{:S(2)}) collective-permute-start(f32[8,128]{1,0:T(8,128)S(1)} %get-tuple-element.493), channel_id=1, source_target_pairs={{0,1},{1,0},{2,3},{3,2},{7,6},{6,7},{5,4},{4,5},{8,9},{9,8},{10,11... | collective-permute-start | bytes 12296 | tf_op jit(solution)/shard_map/ppermute | solution.py:558
  262.8 19.2 %all_to_all.5.pieces = bf16[16,96,128]{2,1,0:T(8,128)(2,1)S(1)} all-to-all(bf16[16,96,128]{2,1,0:T(8,128)(2,1)S(1)} %shard_map.114), channel_id=1, replica_groups=mesh['grp'=32,'dom'=16] {'dom'}, dimensions={0} | all-to-all | bytes 786432 | tf_op jit(solution)/shard_map/all_to_all | solution.py:677
  (217 shorter events, 137.2 us)
Async XLA Ops:
  12.9 15.2 %collective-permute-start = (f32[8,128]{1,0:T(8,128)S(1)}, f32[8,128]{1,0:T(8,128)S(1)}, u32[]{:S(2)}, u32[]{:S(2)}) collective-permute-start(f32[8,128]{1,0:T(8,128)S(1)} %get-tuple-element.786), channel_id=1, source_target_pairs={{1,2},{2,1},{3,7},{7,3},{6,5},{5,6},{4,8},{8,4},{9,10},{10,9},{11,... | collective-permute-start | bytes 12296 | tf_op jit(solution)/shard_map/while/body/eval_jaxpr/ppermute | solution.py:558
  13.5 14.6 %collective-permute-start.3 = (f32[8,128]{1,0:T(8,128)S(1)}, f32[8,128]{1,0:T(8,128)S(1)}, u32[]{:S(2)}, u32[]{:S(2)}) collective-permute-start(f32[8,128]{1,0:T(8,128)S(1)} %get-tuple-element.786), channel_id=1, source_target_pairs={{0,16},{16,0},{32,48},{48,32},{64,80},{80,64},{96,112},{112,96},{1... | collective-permute-start | bytes 12296 | tf_op jit(solution)/shard_map/while/body/eval_jaxpr/ppermute | solution.py:558
  31.5 22.2 %collective-permute-start = (f32[8,128]{1,0:T(8,128)S(1)}, f32[8,128]{1,0:T(8,128)S(1)}, u32[]{:S(2)}, u32[]{:S(2)}) collective-permute-start(f32[8,128]{1,0:T(8,128)S(1)} %get-tuple-element.786), channel_id=1, source_target_pairs={{1,2},{2,1},{3,7},{7,3},{6,5},{5,6},{4,8},{8,4},{9,10},{10,9},{11,... | collective-permute-start | bytes 12296 | tf_op jit(solution)/shard_map/while/body/eval_jaxpr/ppermute | solution.py:558
  32.1 21.6 %collective-permute-start.3 = (f32[8,128]{1,0:T(8,128)S(1)}, f32[8,128]{1,0:T(8,128)S(1)}, u32[]{:S(2)}, u32[]{:S(2)}) collective-permute-start(f32[8,128]{1,0:T(8,128)S(1)} %get-tuple-element.786), channel_id=1, source_target_pairs={{0,16},{16,0},{32,48},{48,32},{64,80},{80,64},{96,112},{112,96},{1... | collective-permute-start | bytes 12296 | tf_op jit(solution)/shard_map/while/body/eval_jaxpr/ppermute | solution.py:558
  35.9 17.8 %collective-permute-start.2 = (f32[8,128]{1,0:T(8,128)S(1)}, f32[8,128]{1,0:T(8,128)S(1)}, u32[]{:S(2)}, u32[]{:S(2)}) collective-permute-start(f32[8,128]{1,0:T(8,128)S(1)} %get-tuple-element.786), channel_id=1, source_target_pairs={{0,1},{1,0},{2,3},{3,2},{7,6},{6,7},{5,4},{4,5},{8,9},{9,8},{10,11... | collective-permute-start | bytes 12296 | tf_op jit(solution)/shard_map/while/body/eval_jaxpr/ppermute | solution.py:558
  70.6 12.5 %collective-permute-start = (f32[8,128]{1,0:T(8,128)S(1)}, f32[8,128]{1,0:T(8,128)S(1)}, u32[]{:S(2)}, u32[]{:S(2)}) collective-permute-start(f32[8,128]{1,0:T(8,128)S(1)} %get-tuple-element.786), channel_id=1, source_target_pairs={{1,2},{2,1},{3,7},{7,3},{6,5},{5,6},{4,8},{8,4},{9,10},{10,9},{11,... | collective-permute-start | bytes 12296 | tf_op jit(solution)/shard_map/while/body/eval_jaxpr/ppermute | solution.py:558
  71.3 11.8 %collective-permute-start.3 = (f32[8,128]{1,0:T(8,128)S(1)}, f32[8,128]{1,0:T(8,128)S(1)}, u32[]{:S(2)}, u32[]{:S(2)}) collective-permute-start(f32[8,128]{1,0:T(8,128)S(1)} %get-tuple-element.786), channel_id=1, source_target_pairs={{0,16},{16,0},{32,48},{48,32},{64,80},{80,64},{96,112},{112,96},{1... | collective-permute-start | bytes 12296 | tf_op jit(solution)/shard_map/while/body/eval_jaxpr/ppermute | solution.py:558
  86.5 12.5 %collective-permute-start = (f32[8,128]{1,0:T(8,128)S(1)}, f32[8,128]{1,0:T(8,128)S(1)}, u32[]{:S(2)}, u32[]{:S(2)}) collective-permute-start(f32[8,128]{1,0:T(8,128)S(1)} %get-tuple-element.786), channel_id=1, source_target_pairs={{1,2},{2,1},{3,7},{7,3},{6,5},{5,6},{4,8},{8,4},{9,10},{10,9},{11,... | collective-permute-start | bytes 12296 | tf_op jit(solution)/shard_map/while/body/eval_jaxpr/ppermute | solution.py:558
  87.2 11.8 %collective-permute-start.3 = (f32[8,128]{1,0:T(8,128)S(1)}, f32[8,128]{1,0:T(8,128)S(1)}, u32[]{:S(2)}, u32[]{:S(2)}) collective-permute-start(f32[8,128]{1,0:T(8,128)S(1)} %get-tuple-element.786), channel_id=1, source_target_pairs={{0,16},{16,0},{32,48},{48,32},{64,80},{80,64},{96,112},{112,96},{1... | collective-permute-start | bytes 12296 | tf_op jit(solution)/shard_map/while/body/eval_jaxpr/ppermute | solution.py:558
  102.4 12.1 %collective-permute-start = (f32[8,128]{1,0:T(8,128)S(1)}, f32[8,128]{1,0:T(8,128)S(1)}, u32[]{:S(2)}, u32[]{:S(2)}) collective-permute-start(f32[8,128]{1,0:T(8,128)S(1)} %get-tuple-element.786), channel_id=1, source_target_pairs={{1,2},{2,1},{3,7},{7,3},{6,5},{5,6},{4,8},{8,4},{9,10},{10,9},{11,... | collective-permute-start | bytes 12296 | tf_op jit(solution)/shard_map/while/body/eval_jaxpr/ppermute | solution.py:558
  117.9 12.2 %collective-permute-start = (f32[8,128]{1,0:T(8,128)S(1)}, f32[8,128]{1,0:T(8,128)S(1)}, u32[]{:S(2)}, u32[]{:S(2)}) collective-permute-start(f32[8,128]{1,0:T(8,128)S(1)} %get-tuple-element.786), channel_id=1, source_target_pairs={{1,2},{2,1},{3,7},{7,3},{6,5},{5,6},{4,8},{8,4},{9,10},{10,9},{11,... | collective-permute-start | bytes 12296 | tf_op jit(solution)/shard_map/while/body/eval_jaxpr/ppermute | solution.py:558
  133.5 12.7 %collective-permute-start = (f32[8,128]{1,0:T(8,128)S(1)}, f32[8,128]{1,0:T(8,128)S(1)}, u32[]{:S(2)}, u32[]{:S(2)}) collective-permute-start(f32[8,128]{1,0:T(8,128)S(1)} %get-tuple-element.786), channel_id=1, source_target_pairs={{1,2},{2,1},{3,7},{7,3},{6,5},{5,6},{4,8},{8,4},{9,10},{10,9},{11,... | collective-permute-start | bytes 12296 | tf_op jit(solution)/shard_map/while/body/eval_jaxpr/ppermute | solution.py:558
  134.2 12.0 %collective-permute-start.3 = (f32[8,128]{1,0:T(8,128)S(1)}, f32[8,128]{1,0:T(8,128)S(1)}, u32[]{:S(2)}, u32[]{:S(2)}) collective-permute-start(f32[8,128]{1,0:T(8,128)S(1)} %get-tuple-element.786), channel_id=1, source_target_pairs={{0,16},{16,0},{32,48},{48,32},{64,80},{80,64},{96,112},{112,96},{1... | collective-permute-start | bytes 12296 | tf_op jit(solution)/shard_map/while/body/eval_jaxpr/ppermute | solution.py:558
  149.6 12.4 %collective-permute-start = (f32[8,128]{1,0:T(8,128)S(1)}, f32[8,128]{1,0:T(8,128)S(1)}, u32[]{:S(2)}, u32[]{:S(2)}) collective-permute-start(f32[8,128]{1,0:T(8,128)S(1)} %get-tuple-element.786), channel_id=1, source_target_pairs={{1,2},{2,1},{3,7},{7,3},{6,5},{5,6},{4,8},{8,4},{9,10},{10,9},{11,... | collective-permute-start | bytes 12296 | tf_op jit(solution)/shard_map/while/body/eval_jaxpr/ppermute | solution.py:558
  150.3 11.7 %collective-permute-start.3 = (f32[8,128]{1,0:T(8,128)S(1)}, f32[8,128]{1,0:T(8,128)S(1)}, u32[]{:S(2)}, u32[]{:S(2)}) collective-permute-start(f32[8,128]{1,0:T(8,128)S(1)} %get-tuple-element.786), channel_id=1, source_target_pairs={{0,16},{16,0},{32,48},{48,32},{64,80},{80,64},{96,112},{112,96},{1... | collective-permute-start | bytes 12296 | tf_op jit(solution)/shard_map/while/body/eval_jaxpr/ppermute | solution.py:558
  165.4 12.1 %collective-permute-start = (f32[8,128]{1,0:T(8,128)S(1)}, f32[8,128]{1,0:T(8,128)S(1)}, u32[]{:S(2)}, u32[]{:S(2)}) collective-permute-start(f32[8,128]{1,0:T(8,128)S(1)} %get-tuple-element.786), channel_id=1, source_target_pairs={{1,2},{2,1},{3,7},{7,3},{6,5},{5,6},{4,8},{8,4},{9,10},{10,9},{11,... | collective-permute-start | bytes 12296 | tf_op jit(solution)/shard_map/while/body/eval_jaxpr/ppermute | solution.py:558
  180.9 12.2 %collective-permute-start = (f32[8,128]{1,0:T(8,128)S(1)}, f32[8,128]{1,0:T(8,128)S(1)}, u32[]{:S(2)}, u32[]{:S(2)}) collective-permute-start(f32[8,128]{1,0:T(8,128)S(1)} %get-tuple-element.786), channel_id=1, source_target_pairs={{1,2},{2,1},{3,7},{7,3},{6,5},{5,6},{4,8},{8,4},{9,10},{10,9},{11,... | collective-permute-start | bytes 12296 | tf_op jit(solution)/shard_map/while/body/eval_jaxpr/ppermute | solution.py:558
  196.6 12.7 %collective-permute-start = (f32[8,128]{1,0:T(8,128)S(1)}, f32[8,128]{1,0:T(8,128)S(1)}, u32[]{:S(2)}, u32[]{:S(2)}) collective-permute-start(f32[8,128]{1,0:T(8,128)S(1)} %get-tuple-element.786), channel_id=1, source_target_pairs={{1,2},{2,1},{3,7},{7,3},{6,5},{5,6},{4,8},{8,4},{9,10},{10,9},{11,... | collective-permute-start | bytes 12296 | tf_op jit(solution)/shard_map/while/body/eval_jaxpr/ppermute | solution.py:558
  197.2 12.0 %collective-permute-start.3 = (f32[8,128]{1,0:T(8,128)S(1)}, f32[8,128]{1,0:T(8,128)S(1)}, u32[]{:S(2)}, u32[]{:S(2)}) collective-permute-start(f32[8,128]{1,0:T(8,128)S(1)} %get-tuple-element.786), channel_id=1, source_target_pairs={{0,16},{16,0},{32,48},{48,32},{64,80},{80,64},{96,112},{112,96},{1... | collective-permute-start | bytes 12296 | tf_op jit(solution)/shard_map/while/body/eval_jaxpr/ppermute | solution.py:558
  212.6 12.1 %collective-permute-start = (f32[8,128]{1,0:T(8,128)S(1)}, f32[8,128]{1,0:T(8,128)S(1)}, u32[]{:S(2)}, u32[]{:S(2)}) collective-permute-start(f32[8,128]{1,0:T(8,128)S(1)} %get-tuple-element.786), channel_id=1, source_target_pairs={{1,2},{2,1},{3,7},{7,3},{6,5},{5,6},{4,8},{8,4},{9,10},{10,9},{11,... | collective-permute-start | bytes 12296 | tf_op jit(solution)/shard_map/while/body/eval_jaxpr/ppermute | solution.py:558
  228.2 12.2 %collective-permute-start = (f32[8,128]{1,0:T(8,128)S(1)}, f32[8,128]{1,0:T(8,128)S(1)}, u32[]{:S(2)}, u32[]{:S(2)}) collective-permute-start(f32[8,128]{1,0:T(8,128)S(1)} %get-tuple-element.786), channel_id=1, source_target_pairs={{1,2},{2,1},{3,7},{7,3},{6,5},{5,6},{4,8},{8,4},{9,10},{10,9},{11,... | collective-permute-start | bytes 12296 | tf_op jit(solution)/shard_map/while/body/eval_jaxpr/ppermute | solution.py:558
  243.8 16.2 %collective-permute-start.10 = (f32[8,128]{1,0:T(8,128)S(1)}, f32[8,128]{1,0:T(8,128)S(1)}, u32[]{:S(2)}, u32[]{:S(2)}) collective-permute-start(f32[8,128]{1,0:T(8,128)S(1)} %get-tuple-element.493), channel_id=1, source_target_pairs={{16,32},{32,16},{48,64},{64,48},{80,96},{96,80},{112,128},{128,112... | collective-permute-start | bytes 12296 | tf_op jit(solution)/shard_map/ppermute | solution.py:558
  245.7 14.2 %collective-permute-start.9 = (f32[8,128]{1,0:T(8,128)S(1)}, f32[8,128]{1,0:T(8,128)S(1)}, u32[]{:S(2)}, u32[]{:S(2)}) collective-permute-start(f32[8,128]{1,0:T(8,128)S(1)} %get-tuple-element.493), channel_id=1, source_target_pairs={{1,2},{2,1},{3,7},{7,3},{6,5},{5,6},{4,8},{8,4},{9,10},{10,9},{11,... | collective-permute-start | bytes 12296 | tf_op jit(solution)/shard_map/ppermute | solution.py:558
  246.4 13.6 %collective-permute-start.12 = (f32[8,128]{1,0:T(8,128)S(1)}, f32[8,128]{1,0:T(8,128)S(1)}, u32[]{:S(2)}, u32[]{:S(2)}) collective-permute-start(f32[8,128]{1,0:T(8,128)S(1)} %get-tuple-element.493), channel_id=1, source_target_pairs={{0,16},{16,0},{32,48},{48,32},{64,80},{80,64},{96,112},{112,96},{1... | collective-permute-start | bytes 12296 | tf_op jit(solution)/shard_map/ppermute | solution.py:558
  (41 other events, 289.0 us)

commit v2 on v1

--- a/solution.py
+++ b/solution.py
@@ -77,10 +77,12 @@
     return jnp.concatenate(out, axis=1)
 
 
-def merge_received(source, dom1, grp1, dom0, grp0):
-    out = jnp.where(source == 0, grp0, grp1)
-    out = jnp.where(source == 2, dom0, out)
-    return jnp.where(source == 3, dom1, out)
+def early_received(source, dom1, grp1):
+    return jnp.where(source == 3, dom1, jnp.where(source == 1, grp1, 0.0))
+
+
+def late_received(source, dom0, grp0):
+    return jnp.where(source == 2, dom0, jnp.where(source == 0, grp0, 0.0))
 
 
 def scatter_nodes(pieces, chunks, incidence):
@@ -228,6 +230,7 @@
 def prepare_kernel(
     packed,
     shape_t,
+    source,
     incidence,
     field,
     faces,
@@ -239,6 +242,8 @@
     lame_moduli,
     point_weights,
     rank,
+    late_index,
+    listed_index,
 ):
     nodes = field.shape[1]
     element_nodes = packed[CONNECT_ROW : CONNECT_ROW + NODE_ROWS, :].astype(jnp.int32)
@@ -252,9 +257,18 @@
     listed = packed[LISTED_ROW : LISTED_ROW + 1, :].astype(jnp.int32)
     column = jnp.broadcast_to(listed, (LANES, LANES)).T
     wide = jnp.concatenate([column] * (nodes // LANES), axis=1)
-    slot = lax.broadcasted_iota(jnp.int32, (LANES, nodes), 0) + 1
+    late = jnp.broadcast_to(256 * (1 - source[0:1, :] % 2), (LANES, LANES)).T
+    late = jnp.concatenate([late] * (nodes // LANES), axis=1)
+    slot = lax.broadcasted_iota(jnp.int32, (LANES, nodes), 0) + 1 + late
     found = jnp.sum(jnp.where(wide == lane, slot, 0), axis=0, keepdims=True)
-    inverse_index[...] = jnp.broadcast_to(found - 1, (8, nodes))
+    placed = jnp.bitwise_and(found, 255) - 1
+    inverse_index[...] = jnp.broadcast_to(placed, (8, nodes))
+    late_row = jnp.where(found >= 256, placed, -1).astype(jnp.float32)
+    late_row = jnp.broadcast_to(late_row, (8, nodes))
+    for b in range(NODE_ROWS // 8):
+        rows = slice(8 * b, 8 * b + 8)
+        late_index[rows, :] = pick_lanes(late_row, element_nodes[rows]).astype(jnp.int32)
+    listed_index[...] = jnp.broadcast_to(jnp.maximum(listed, 0), (8, LANES))
     set_faces(packed, faces)
     set_field(packed, incidence, field)
 
@@ -293,10 +307,21 @@
     return pltpu.roll(wave[...], STEPS - 1, 0)
 
 
+def at_elements(displace, connect):
+    index = connect[...]
+    columns = []
+    for c in range(3):
+        pieces = []
+        for b in range(NODE_ROWS // 8):
+            row = jnp.broadcast_to(displace[c : c + 1, :], (8, displace.shape[1]))
+            pieces.append(pick_lanes(row, index[8 * b : 8 * b + 8]))
+        columns.append(jnp.concatenate(pieces, axis=0))
+    return columns
+
+
 def strain_and_force(
-    displace,
+    columns,
     strain,
-    connect,
     wide_gradient,
     wide_force,
     inverse_jacobian,
@@ -305,22 +330,6 @@
     faces,
     need_force,
 ):
-    index = connect[...]
-    low = jnp.bitwise_and(index, LANES - 1)
-    chunk = jnp.right_shift(index, 7)
-    is_chunk = [chunk == j for j in range(1, displace.shape[1] // LANES)]
-    columns = []
-    for c in range(3):
-        pieces = []
-        for b in range(NODE_ROWS // 8):
-            rows = slice(8 * b, 8 * b + 8)
-            out = None
-            for j in range(displace.shape[1] // LANES):
-                row = jnp.broadcast_to(displace[c : c + 1, j * LANES : (j + 1) * LANES], (8, LANES))
-                taken = lane_gather(row, low[rows])
-                out = taken if j == 0 else jnp.where(is_chunk[j - 1][rows], taken, out)
-            pieces.append(out)
-        columns.append(jnp.concatenate(pieces, axis=0))
     along = contract(wide_gradient, columns, EL_NODES)
     jac = [inverse_jacobian[i : i + 1, :] for i in range(9)]
 
@@ -377,13 +386,6 @@
     return pieces
 
 
-def scatter_kernel(node_forces, connect, incidence, force):
-    parts = [node_forces[c] for c in range(3)]
-    chunk = jnp.right_shift(connect[...], 7)
-    chunks = [chunk[n : n + 1, :] for n in range(EL_NODES)]
-    force[...] = scatter_nodes(node_rows(parts), chunks, incidence[...])
-
-
 def keep_forces(result, node_forces, send):
     forces, faces = result
     for c in range(3):
@@ -399,6 +401,7 @@
     grp0,
     source,
     inverse_index,
+    listed_index,
     field,
     connect,
     wide_gradient,
@@ -412,24 +415,26 @@
     velocity,
     pattern,
     half_inverse_mass,
+    late_scale,
     node_forces,
     send,
     next_wave,
 ):
     next_wave[...] = moved_up(wave)
-    received = merge_received(source[...], dom1[...], grp1[...], dom0[...], grp0[...])
+    received = early_received(source[...], dom1[...], grp1[...])
+    received = received + late_received(source[...], dom0[...], grp0[...])
     total = field[...] + spread(received, inverse_index[...])
     scale = jnp.broadcast_to(time_step * (1.0 / total[3:4, :]), total.shape)
     pattern[...] = total
     half_inverse_mass[...] = scale
+    late_scale[...] = time_step * pick_lanes(scale, listed_index[...])
     new_velocity = scale * (wave_row(wave, total.shape[1]) * total)
     velocity[...] = new_velocity
     new_displace = time_step * new_velocity
     displace[...] = new_displace
     result = strain_and_force(
-        new_displace,
+        at_elements(new_displace, connect),
         strain,
-        connect,
         wide_gradient,
         wide_force,
         inverse_jacobian,
@@ -441,38 +446,72 @@
     keep_forces(result, node_forces, send)
 
 
-def step_kernel(
+def side_kernel(
     wave,
     dom1,
     grp1,
+    last_dom0,
+    last_grp0,
+    source,
+    inverse_index,
+    connect,
+    incidence,
+    pattern,
+    half_inverse_mass,
+    old_displace,
+    old_velocity,
+    node_forces,
+    displace,
+    velocity,
+    columns,
+    next_wave,
+):
+    next_wave[...] = moved_up(wave)
+    index, scale = inverse_index[...], half_inverse_mass[...]
+    missing = spread(late_received(source[...], last_dom0[...], last_grp0[...]), index) * scale
+    parts = [node_forces[c] for c in range(3)]
+    chunk = jnp.right_shift(connect[...], 7)
+    chunks = [chunk[n : n + 1, :] for n in range(EL_NODES)]
+    force = scatter_nodes(node_rows(parts), chunks, incidence[...])
+    stiff = force + spread(early_received(source[...], dom1[...], grp1[...]), index)
+    total = wave_row(wave, stiff.shape[1]) * pattern[...] - stiff
+    new_velocity = (old_velocity[...] - missing) + scale * total
+    velocity[...] = new_velocity
+    new_displace = (old_displace[...] - time_step * missing) + time_step * new_velocity
+    displace[...] = new_displace
+    for c, column in enumerate(at_elements(new_displace, connect)):
+        columns[c] = column
+
+
+def step_kernel(
     dom0,
     grp0,
     source,
-    inverse_index,
-    connect,
+    late_index,
+    late_scale,
+    base_columns,
     wide_gradient,
     wide_force,
     inverse_jacobian,
     lame_moduli,
     point_weights,
     faces,
-    pattern,
-    half_inverse_mass,
-    old_displace,
-    old_velocity,
-    old_force,
     strain,
     *rest,
 ):
-    received = merge_received(source[...], dom1[...], grp1[...], dom0[...], grp0[...])
-    stiff = old_force[...] + spread(received, inverse_index[...])
-    total = wave_row(wave, stiff.shape[1]) * pattern[...] - stiff
-    new_velocity = old_velocity[...] + half_inverse_mass[...] * total
-    new_displace = old_displace[...] + time_step * new_velocity
+    late = late_scale[...] * late_received(source[...], dom0[...], grp0[...])
+    columns = []
+    for c in range(3):
+        row = jnp.broadcast_to(late[c : c + 1, :], (8, LANES))
+        pieces = []
+        for b in range(NODE_ROWS // 8):
+            index = late_index[8 * b : 8 * b + 8, :]
+            taken = jnp.where(index >= 0, lane_gather(row, jnp.maximum(index, 0)), 0.0)
+            pieces.append(base_columns[c, 8 * b : 8 * b + 8, :] - taken)
+        columns.append(jnp.concatenate(pieces, axis=0))
     result = strain_and_force(
-        new_displace,
+        columns,
         strain,
-        connect,
         wide_gradient,
         wide_force,
         inverse_jacobian,
@@ -482,11 +521,7 @@
         bool(rest),
     )
     if rest:
-        displace, velocity, node_forces, send, next_wave = rest
-        next_wave[...] = moved_up(wave)
-        displace[...] = new_displace
-        velocity[...] = new_velocity
-        keep_forces(result, node_forces, send)
+        keep_forces(result, *rest)
 
 
 def order_kernel(rank, strains, last, out, store):
@@ -539,6 +574,7 @@
     f32 = jnp.float32
     field_t = jax.ShapeDtypeStruct((8, nodes), f32)
     lanes_t = jax.ShapeDtypeStruct((8, LANES), f32)
+    index_t = jax.ShapeDtypeStruct((8, LANES), jnp.int32)
     strain_t = jax.ShapeDtypeStruct((STRAIN * POINTS, LANES), f32)
 
     face = lax.broadcasted_iota(jnp.int32, (8, LANES), 1) // (LANES // FACES)
@@ -621,53 +657,69 @@
             jax.ShapeDtypeStruct(lame_moduli.shape, f32),
             jax.ShapeDtypeStruct(point_weights.shape, f32),
             jax.ShapeDtypeStruct(rank_rows.shape, i32),
+            jax.ShapeDtypeStruct((NODE_ROWS, LANES), i32),
+            index_t,
         ],
-        [VMEM, VMEM],
-    )
-    outs = prepare(packed, shape_t)
+        [VMEM] * 3,
+    )
+    outs = prepare(packed, shape_t, source)
     incidence, field, faces, inverse_index = outs[:4]
     rank = outs[10]
     connect_rows = outs[4]
-    element_data = (*outs[4:10], faces)
+    late_index, listed_index = outs[11:]
+    element_data = (*outs[5:10], faces)
     wave_t = jax.ShapeDtypeStruct((STEPS, LANES), f32)
     forces_t = jax.ShapeDtypeStruct((3, NODE_ROWS, LANES), f32)
-    strain, displace, velocity, pattern, half_inverse_mass, node_forces, send, wave = kernel_call(
+    (
+        strain,
+        displace,
+        velocity,
+        pattern,
+        half_inverse_mass,
+        late_scale,
+        node_forces,
+        send,
+        wave,
+    ) = kernel_call(
         first_kernel,
-        [strain_t, field_t, field_t, field_t, field_t, forces_t, lanes_t, wave_t],
-        [VMEM] * 15,
-    )(wave, *received, source, inverse_index, field, *element_data)
+        [strain_t, field_t, field_t, field_t, field_t, lanes_t, forces_t, lanes_t, wave_t],
+        [VMEM] * 16,
+    )(wave, *received, source, inverse_index, listed_index, field, connect_rows, *element_data)
     strains = jnp.zeros((STEPS - 1, STRAIN * POINTS, LANES), f32)
     strains = lax.dynamic_update_index_in_dim(strains, strain, 0, 0)
 
-    def advance(last, displace, velocity, node_forces, send, wave):
-        received = exchange(send)
-        scatter = kernel_call(scatter_kernel, [field_t], [VMEM] * 3)
-        (force,) = scatter(node_forces, connect_rows, incidence)
-        return kernel_call(
-            step_kernel,
-            [strain_t] + ([] if last else [field_t, field_t, forces_t, lanes_t, wave_t]),
-            [VMEM] * 19,
-        )(
+    def advance(last, displace, velocity, late, node_forces, send, wave):
+        dom1, grp1, *new_late = exchange(send)
+        side = kernel_call(side_kernel, [field_t, field_t, forces_t, wave_t], [VMEM] * 14)
+        displace, velocity, columns, wave = side(
             wave,
-            *received,
+            dom1,
+            grp1,
+            *late,
             source,
             inverse_index,
-            *element_data,
+            connect_rows,
+            incidence,
             pattern,
             half_inverse_mass,
             displace,
             velocity,
-            force,
+            node_forces,
         )
+        outs = kernel_call(
+            step_kernel, [strain_t] + ([] if last else [forces_t, lanes_t]), [VMEM] * 12
+        )(*new_late, source, late_index, late_scale, columns, *element_data)
+        return outs[0], displace, velocity, new_late, *outs[1:], wave
 
     def body(step, carried):
         strains, *state = carried
         strain, *state = advance(False, *state)
         return (lax.dynamic_update_index_in_dim(strains, strain, step, 0), *state)
 
-    carried = (strains, displace, velocity, node_forces, send, wave)
+    none = [jnp.zeros((8, LANES), f32)] * 2
+    carried = (strains, displace, velocity, none, node_forces, send, wave)
     strains, *state = lax.fori_loop(1, STEPS - 1, body, carried)
-    (strain,) = advance(True, *state)
+    strain = advance(True, *state)[0]
     (ordered,) = kernel_call(
         order_kernel,
         [jax.ShapeDtypeStruct((writers, STEPS * STRAIN, LANES), jnp.bfloat16)],

time: 285 us -> 260 us (0.912)
  waiting for transfers between devices: 38.7 us -> 4.97 us
  starting transfers between devices: 203 us -> 207 us
  blocking collectives: 19.2 us -> 22.5 us
    ppermute x60, waiting for transfers between devices: 38.7 us -> 4.95 us  [exchange(): received.append(lax.ppermute(send, axis, pairs))]
    ppermute x60, starting transfers between devices: 194 us -> 198 us  [exchange(): received.append(lax.ppermute(send, axis, pairs))]
    all_to_all x1, blocking collectives: 19.2 us -> 22.5 us  [shards(): lax.all_to_all(ordered, 'dom', split_axis=0, concat_axis=0, tiled=True)]
  transfers between devices with their start and end apart: 65 -> 65, of which waited for: 15 -> 15; matrix products, arithmetic and copies ran while one was open for 0% -> 0% of each run, Pallas kernels for 2% -> 3%
where the time goes in v2:
time: 260 us; the launch traced here: 258 us
  starting transfers between devices  207 us (80%)
  blocking collectives  22.5 us (9%)
  Pallas kernels  20.8 us (8%)
  waiting for transfers between devices  4.97 us (2%)
    ppermute x60, starting transfers between devices, exchange(): received.append(lax.ppermute(send, axis, pairs))  198 us
    all_to_all x1, blocking collectives, shards(): lax.all_to_all(ordered, 'dom', split_axis=0, concat_axis=0, tiled=True)  22.5 us
    pallas_call x15, Pallas kernels, advance(): kernel_call(step_kernel, [strain_t] + ([] if last else [forces_t, lanes_t...  8.46 us
    ppermute x4, starting transfers between devices, shards(): received.append(lax.ppermute(send, ('grp', 'dom'), pairs))  8.16 us
    pallas_call x15, Pallas kernels, advance(): side(wave, dom1, grp1, *late, source, inverse_index, connect_rows, incide...  6.56 us
  transfers between devices with their start and end apart: 65, of which 15 were waited for; matrix products, arithmetic and copies ran while one was open for 0% of the time, Pallas kernels for 3%

profile of v2, /device:TPU:200, one launch (start us, length us, event | category | flops | bytes accessed | tf_op | source)
XLA Modules:
  0.0 258.3 jit_solution(6939627825966649221)
XLA Ops:
  12.9 204.7 %while.30 = (s32[]{:T(128)}, f32[15,96,128]{2,1,0:T(8,128)S(1)}, f32[8,512]{1,0:T(8,128)S(1)}, f32[8,512]{1,0:T(8,128)S(1)}, f32[8,128]{1,0:T(8,128)S(1)}, /*ind...) while((s32[]{:T(128)}, f32[15,96,128]{2,1,0:T(8,128)S(1)}, ...), condition=%wide.region_1.2_spmd.clone, body=%wide.region_0.1_spmd.clone.sunk | while | flops 26629 | bytes 267859 | solution.py:721
  12.9 5.8 %collective-permute-start = (f32[8,128]{1,0:T(8,128)S(1)}, f32[8,128]{1,0:T(8,128)S(1)}, u32[]{:S(2)}, u32[]{:S(2)}) collective-permute-start(f32[8,128]{1,0:T(8,128)S(1)} %get-tuple-element.926), channel_id=1, source_target_pairs={{0,1},{1,0},{2,3},{3,2},{7,6},{6,7},{5,4},{4,5},{8,9},{9,8},{10,11... | collective-permute-start | bytes 12296 | tf_op jit(solution)/shard_map/while/body/eval_jaxpr/ppermute | solution.py:594
  22.3 4.8 %collective-permute-start.1 = (f32[8,128]{1,0:T(8,128)S(1)}, f32[8,128]{1,0:T(8,128)S(1)}, u32[]{:S(2)}, u32[]{:S(2)}) collective-permute-start(f32[8,128]{1,0:T(8,128)S(1)} %get-tuple-element.926), channel_id=1, source_target_pairs={{0,16},{16,0},{32,48},{48,32},{64,80},{80,64},{96,112},{112,96},{1... | collective-permute-start | bytes 12296 | tf_op jit(solution)/shard_map/while/body/eval_jaxpr/ppermute | solution.py:594
  28.5 9.4 %collective-permute-start = (f32[8,128]{1,0:T(8,128)S(1)}, f32[8,128]{1,0:T(8,128)S(1)}, u32[]{:S(2)}, u32[]{:S(2)}) collective-permute-start(f32[8,128]{1,0:T(8,128)S(1)} %get-tuple-element.926), channel_id=1, source_target_pairs={{0,1},{1,0},{2,3},{3,2},{7,6},{6,7},{5,4},{4,5},{8,9},{9,8},{10,11... | collective-permute-start | bytes 12296 | tf_op jit(solution)/shard_map/while/body/eval_jaxpr/ppermute | solution.py:594
  40.5 4.6 %collective-permute-start.1 = (f32[8,128]{1,0:T(8,128)S(1)}, f32[8,128]{1,0:T(8,128)S(1)}, u32[]{:S(2)}, u32[]{:S(2)}) collective-permute-start(f32[8,128]{1,0:T(8,128)S(1)} %get-tuple-element.926), channel_id=1, source_target_pairs={{0,16},{16,0},{32,48},{48,32},{64,80},{80,64},{96,112},{112,96},{1... | collective-permute-start | bytes 12296 | tf_op jit(solution)/shard_map/while/body/eval_jaxpr/ppermute | solution.py:594
  46.6 10.6 %collective-permute-start = (f32[8,128]{1,0:T(8,128)S(1)}, f32[8,128]{1,0:T(8,128)S(1)}, u32[]{:S(2)}, u32[]{:S(2)}) collective-permute-start(f32[8,128]{1,0:T(8,128)S(1)} %get-tuple-element.926), channel_id=1, source_target_pairs={{0,1},{1,0},{2,3},{3,2},{7,6},{6,7},{5,4},{4,5},{8,9},{9,8},{10,11... | collective-permute-start | bytes 12296 | tf_op jit(solution)/shard_map/while/body/eval_jaxpr/ppermute | solution.py:594
  64.7 5.2 %collective-permute-start = (f32[8,128]{1,0:T(8,128)S(1)}, f32[8,128]{1,0:T(8,128)S(1)}, u32[]{:S(2)}, u32[]{:S(2)}) collective-permute-start(f32[8,128]{1,0:T(8,128)S(1)} %get-tuple-element.926), channel_id=1, source_target_pairs={{0,1},{1,0},{2,3},{3,2},{7,6},{6,7},{5,4},{4,5},{8,9},{9,8},{10,11... | collective-permute-start | bytes 12296 | tf_op jit(solution)/shard_map/while/body/eval_jaxpr/ppermute | solution.py:594
  73.1 4.6 %collective-permute-start.1 = (f32[8,128]{1,0:T(8,128)S(1)}, f32[8,128]{1,0:T(8,128)S(1)}, u32[]{:S(2)}, u32[]{:S(2)}) collective-permute-start(f32[8,128]{1,0:T(8,128)S(1)} %get-tuple-element.926), channel_id=1, source_target_pairs={{0,16},{16,0},{32,48},{48,32},{64,80},{80,64},{96,112},{112,96},{1... | collective-permute-start | bytes 12296 | tf_op jit(solution)/shard_map/while/body/eval_jaxpr/ppermute | solution.py:594
  79.1 5.0 %collective-permute-start = (f32[8,128]{1,0:T(8,128)S(1)}, f32[8,128]{1,0:T(8,128)S(1)}, u32[]{:S(2)}, u32[]{:S(2)}) collective-permute-start(f32[8,128]{1,0:T(8,128)S(1)} %get-tuple-element.926), channel_id=1, source_target_pairs={{0,1},{1,0},{2,3},{3,2},{7,6},{6,7},{5,4},{4,5},{8,9},{9,8},{10,11... | collective-permute-start | bytes 12296 | tf_op jit(solution)/shard_map/while/body/eval_jaxpr/ppermute | solution.py:594
  91.4 7.5 %collective-permute-start = (f32[8,128]{1,0:T(8,128)S(1)}, f32[8,128]{1,0:T(8,128)S(1)}, u32[]{:S(2)}, u32[]{:S(2)}) collective-permute-start(f32[8,128]{1,0:T(8,128)S(1)} %get-tuple-element.926), channel_id=1, source_target_pairs={{0,1},{1,0},{2,3},{3,2},{7,6},{6,7},{5,4},{4,5},{8,9},{9,8},{10,11... | collective-permute-start | bytes 12296 | tf_op jit(solution)/shard_map/while/body/eval_jaxpr/ppermute | solution.py:594
  101.6 3.6 %collective-permute-start.1 = (f32[8,128]{1,0:T(8,128)S(1)}, f32[8,128]{1,0:T(8,128)S(1)}, u32[]{:S(2)}, u32[]{:S(2)}) collective-permute-start(f32[8,128]{1,0:T(8,128)S(1)} %get-tuple-element.926), channel_id=1, source_target_pairs={{0,16},{16,0},{32,48},{48,32},{64,80},{80,64},{96,112},{112,96},{1... | collective-permute-start | bytes 12296 | tf_op jit(solution)/shard_map/while/body/eval_jaxpr/ppermute | solution.py:594
  106.6 6.2 %collective-permute-start = (f32[8,128]{1,0:T(8,128)S(1)}, f32[8,128]{1,0:T(8,128)S(1)}, u32[]{:S(2)}, u32[]{:S(2)}) collective-permute-start(f32[8,128]{1,0:T(8,128)S(1)} %get-tuple-element.926), channel_id=1, source_target_pairs={{0,1},{1,0},{2,3},{3,2},{7,6},{6,7},{5,4},{4,5},{8,9},{9,8},{10,11... | collective-permute-start | bytes 12296 | tf_op jit(solution)/shard_map/while/body/eval_jaxpr/ppermute | solution.py:594
  120.5 6.2 %collective-permute-start = (f32[8,128]{1,0:T(8,128)S(1)}, f32[8,128]{1,0:T(8,128)S(1)}, u32[]{:S(2)}, u32[]{:S(2)}) collective-permute-start(f32[8,128]{1,0:T(8,128)S(1)} %get-tuple-element.926), channel_id=1, source_target_pairs={{0,1},{1,0},{2,3},{3,2},{7,6},{6,7},{5,4},{4,5},{8,9},{9,8},{10,11... | collective-permute-start | bytes 12296 | tf_op jit(solution)/shard_map/while/body/eval_jaxpr/ppermute | solution.py:594
  134.4 6.2 %collective-permute-start = (f32[8,128]{1,0:T(8,128)S(1)}, f32[8,128]{1,0:T(8,128)S(1)}, u32[]{:S(2)}, u32[]{:S(2)}) collective-permute-start(f32[8,128]{1,0:T(8,128)S(1)} %get-tuple-element.926), channel_id=1, source_target_pairs={{0,1},{1,0},{2,3},{3,2},{7,6},{6,7},{5,4},{4,5},{8,9},{9,8},{10,11... | collective-permute-start | bytes 12296 | tf_op jit(solution)/shard_map/while/body/eval_jaxpr/ppermute | solution.py:594
  148.2 6.2 %collective-permute-start = (f32[8,128]{1,0:T(8,128)S(1)}, f32[8,128]{1,0:T(8,128)S(1)}, u32[]{:S(2)}, u32[]{:S(2)}) collective-permute-start(f32[8,128]{1,0:T(8,128)S(1)} %get-tuple-element.926), channel_id=1, source_target_pairs={{0,1},{1,0},{2,3},{3,2},{7,6},{6,7},{5,4},{4,5},{8,9},{9,8},{10,11... | collective-permute-start | bytes 12296 | tf_op jit(solution)/shard_map/while/body/eval_jaxpr/ppermute | solution.py:594
  157.1 3.6 %collective-permute-start.1 = (f32[8,128]{1,0:T(8,128)S(1)}, f32[8,128]{1,0:T(8,128)S(1)}, u32[]{:S(2)}, u32[]{:S(2)}) collective-permute-start(f32[8,128]{1,0:T(8,128)S(1)} %get-tuple-element.926), channel_id=1, source_target_pairs={{0,16},{16,0},{32,48},{48,32},{64,80},{80,64},{96,112},{112,96},{1... | collective-permute-start | bytes 12296 | tf_op jit(solution)/shard_map/while/body/eval_jaxpr/ppermute | solution.py:594
  162.1 6.2 %collective-permute-start = (f32[8,128]{1,0:T(8,128)S(1)}, f32[8,128]{1,0:T(8,128)S(1)}, u32[]{:S(2)}, u32[]{:S(2)}) collective-permute-start(f32[8,128]{1,0:T(8,128)S(1)} %get-tuple-element.926), channel_id=1, source_target_pairs={{0,1},{1,0},{2,3},{3,2},{7,6},{6,7},{5,4},{4,5},{8,9},{9,8},{10,11... | collective-permute-start | bytes 12296 | tf_op jit(solution)/shard_map/while/body/eval_jaxpr/ppermute | solution.py:594
  176.0 6.2 %collective-permute-start = (f32[8,128]{1,0:T(8,128)S(1)}, f32[8,128]{1,0:T(8,128)S(1)}, u32[]{:S(2)}, u32[]{:S(2)}) collective-permute-start(f32[8,128]{1,0:T(8,128)S(1)} %get-tuple-element.926), channel_id=1, source_target_pairs={{0,1},{1,0},{2,3},{3,2},{7,6},{6,7},{5,4},{4,5},{8,9},{9,8},{10,11... | collective-permute-start | bytes 12296 | tf_op jit(solution)/shard_map/while/body/eval_jaxpr/ppermute | solution.py:594
  184.8 3.6 %collective-permute-start.1 = (f32[8,128]{1,0:T(8,128)S(1)}, f32[8,128]{1,0:T(8,128)S(1)}, u32[]{:S(2)}, u32[]{:S(2)}) collective-permute-start(f32[8,128]{1,0:T(8,128)S(1)} %get-tuple-element.926), channel_id=1, source_target_pairs={{0,16},{16,0},{32,48},{48,32},{64,80},{80,64},{96,112},{112,96},{1... | collective-permute-start | bytes 12296 | tf_op jit(solution)/shard_map/while/body/eval_jaxpr/ppermute | solution.py:594
  189.9 6.2 %collective-permute-start = (f32[8,128]{1,0:T(8,128)S(1)}, f32[8,128]{1,0:T(8,128)S(1)}, u32[]{:S(2)}, u32[]{:S(2)}) collective-permute-start(f32[8,128]{1,0:T(8,128)S(1)} %get-tuple-element.926), channel_id=1, source_target_pairs={{0,1},{1,0},{2,3},{3,2},{7,6},{6,7},{5,4},{4,5},{8,9},{9,8},{10,11... | collective-permute-start | bytes 12296 | tf_op jit(solution)/shard_map/while/body/eval_jaxpr/ppermute | solution.py:594
  203.7 6.2 %collective-permute-start = (f32[8,128]{1,0:T(8,128)S(1)}, f32[8,128]{1,0:T(8,128)S(1)}, u32[]{:S(2)}, u32[]{:S(2)}) collective-permute-start(f32[8,128]{1,0:T(8,128)S(1)} %get-tuple-element.926), channel_id=1, source_target_pairs={{0,1},{1,0},{2,3},{3,2},{7,6},{6,7},{5,4},{4,5},{8,9},{9,8},{10,11... | collective-permute-start | bytes 12296 | tf_op jit(solution)/shard_map/while/body/eval_jaxpr/ppermute | solution.py:594
  220.6 4.1 %collective-permute-start.10 = (f32[8,128]{1,0:T(8,128)S(1)}, f32[8,128]{1,0:T(8,128)S(1)}, u32[]{:S(2)}, u32[]{:S(2)}) collective-permute-start(f32[8,128]{1,0:T(8,128)S(1)} %get-tuple-element.580), channel_id=1, source_target_pairs={{0,16},{16,0},{32,48},{48,32},{64,80},{80,64},{96,112},{112,96},{1... | collective-permute-start | bytes 12296 | tf_op jit(solution)/shard_map/ppermute | solution.py:594
  224.7 7.3 %collective-permute-start.9 = (f32[8,128]{1,0:T(8,128)S(1)}, f32[8,128]{1,0:T(8,128)S(1)}, u32[]{:S(2)}, u32[]{:S(2)}) collective-permute-start(f32[8,128]{1,0:T(8,128)S(1)} %get-tuple-element.580), channel_id=1, source_target_pairs={{0,1},{1,0},{2,3},{3,2},{7,6},{6,7},{5,4},{4,5},{8,9},{9,8},{10,11... | collective-permute-start | bytes 12296 | tf_op jit(solution)/shard_map/ppermute | solution.py:594
  234.9 22.5 %all_to_all.5.pieces = bf16[16,96,128]{2,1,0:T(8,128)(2,1)S(1)} all-to-all(bf16[16,96,128]{2,1,0:T(8,128)(2,1)S(1)} %shard_map.114), channel_id=1, replica_groups=mesh['grp'=32,'dom'=16] {'dom'}, dimensions={0} | all-to-all | bytes 786432 | tf_op jit(solution)/shard_map/all_to_all | solution.py:729
  (247 shorter events, 104.0 us)
Async XLA Ops:
  1.7 10.4 %collective-permute-start.8 = (f32[8,128]{1,0:T(8,128)S(1)}, f32[8,128]{1,0:T(8,128)S(1)}, u32[]{:S(2)}, u32[]{:S(2)}) collective-permute-start(f32[8,128]{1,0:T(8,128)S(1)} %get-tuple-element.557), channel_id=1, source_target_pairs={{0,16},{1,17},{2,18},{3,19},{4,23},{5,22},{6,21},{7,20},{8,24},{9,... | collective-permute-start | bytes 12296 | tf_op jit(solution)/shard_map/ppermute | solution.py:644
  3.6 8.4 %collective-permute-start.7 = (f32[8,128]{1,0:T(8,128)S(1)}, f32[8,128]{1,0:T(8,128)S(1)}, u32[]{:S(2)}, u32[]{:S(2)}) collective-permute-start(f32[8,128]{1,0:T(8,128)S(1)} %get-tuple-element.557), channel_id=1, source_target_pairs={{0,1},{1,0},{2,3},{3,2},{4,6},{5,7},{6,4},{7,5},{8,9},{9,8},{10,11... | collective-permute-start | bytes 12296 | tf_op jit(solution)/shard_map/ppermute | solution.py:644
  12.9 14.6 %collective-permute-start = (f32[8,128]{1,0:T(8,128)S(1)}, f32[8,128]{1,0:T(8,128)S(1)}, u32[]{:S(2)}, u32[]{:S(2)}) collective-permute-start(f32[8,128]{1,0:T(8,128)S(1)} %get-tuple-element.926), channel_id=1, source_target_pairs={{0,1},{1,0},{2,3},{3,2},{7,6},{6,7},{5,4},{4,5},{8,9},{9,8},{10,11... | collective-permute-start | bytes 12296 | tf_op jit(solution)/shard_map/while/body/eval_jaxpr/ppermute | solution.py:594
  18.8 8.4 %collective-permute-start.3 = (f32[8,128]{1,0:T(8,128)S(1)}, f32[8,128]{1,0:T(8,128)S(1)}, u32[]{:S(2)}, u32[]{:S(2)}) collective-permute-start(f32[8,128]{1,0:T(8,128)S(1)} %get-tuple-element.926), channel_id=1, source_target_pairs={{16,32},{32,16},{48,64},{64,48},{80,96},{96,80},{112,128},{128,112... | collective-permute-start | bytes 12296 | tf_op jit(solution)/shard_map/while/body/eval_jaxpr/ppermute | solution.py:594
  28.5 17.1 %collective-permute-start = (f32[8,128]{1,0:T(8,128)S(1)}, f32[8,128]{1,0:T(8,128)S(1)}, u32[]{:S(2)}, u32[]{:S(2)}) collective-permute-start(f32[8,128]{1,0:T(8,128)S(1)} %get-tuple-element.926), channel_id=1, source_target_pairs={{0,1},{1,0},{2,3},{3,2},{7,6},{6,7},{5,4},{4,5},{8,9},{9,8},{10,11... | collective-permute-start | bytes 12296 | tf_op jit(solution)/shard_map/while/body/eval_jaxpr/ppermute | solution.py:594
  37.9 7.2 %collective-permute-start.3 = (f32[8,128]{1,0:T(8,128)S(1)}, f32[8,128]{1,0:T(8,128)S(1)}, u32[]{:S(2)}, u32[]{:S(2)}) collective-permute-start(f32[8,128]{1,0:T(8,128)S(1)} %get-tuple-element.926), channel_id=1, source_target_pairs={{16,32},{32,16},{48,64},{64,48},{80,96},{96,80},{112,128},{128,112... | collective-permute-start | bytes 12296 | tf_op jit(solution)/shard_map/while/body/eval_jaxpr/ppermute | solution.py:594
  46.6 17.2 %collective-permute-start = (f32[8,128]{1,0:T(8,128)S(1)}, f32[8,128]{1,0:T(8,128)S(1)}, u32[]{:S(2)}, u32[]{:S(2)}) collective-permute-start(f32[8,128]{1,0:T(8,128)S(1)} %get-tuple-element.926), channel_id=1, source_target_pairs={{0,1},{1,0},{2,3},{3,2},{7,6},{6,7},{5,4},{4,5},{8,9},{9,8},{10,11... | collective-permute-start | bytes 12296 | tf_op jit(solution)/shard_map/while/body/eval_jaxpr/ppermute | solution.py:594
  64.7 13.5 %collective-permute-start = (f32[8,128]{1,0:T(8,128)S(1)}, f32[8,128]{1,0:T(8,128)S(1)}, u32[]{:S(2)}, u32[]{:S(2)}) collective-permute-start(f32[8,128]{1,0:T(8,128)S(1)} %get-tuple-element.926), channel_id=1, source_target_pairs={{0,1},{1,0},{2,3},{3,2},{7,6},{6,7},{5,4},{4,5},{8,9},{9,8},{10,11... | collective-permute-start | bytes 12296 | tf_op jit(solution)/shard_map/while/body/eval_jaxpr/ppermute | solution.py:594
  69.9 7.8 %collective-permute-start.3 = (f32[8,128]{1,0:T(8,128)S(1)}, f32[8,128]{1,0:T(8,128)S(1)}, u32[]{:S(2)}, u32[]{:S(2)}) collective-permute-start(f32[8,128]{1,0:T(8,128)S(1)} %get-tuple-element.926), channel_id=1, source_target_pairs={{16,32},{32,16},{48,64},{64,48},{80,96},{96,80},{112,128},{128,112... | collective-permute-start | bytes 12296 | tf_op jit(solution)/shard_map/while/body/eval_jaxpr/ppermute | solution.py:594
  79.1 11.3 %collective-permute-start = (f32[8,128]{1,0:T(8,128)S(1)}, f32[8,128]{1,0:T(8,128)S(1)}, u32[]{:S(2)}, u32[]{:S(2)}) collective-permute-start(f32[8,128]{1,0:T(8,128)S(1)} %get-tuple-element.926), channel_id=1, source_target_pairs={{0,1},{1,0},{2,3},{3,2},{7,6},{6,7},{5,4},{4,5},{8,9},{9,8},{10,11... | collective-permute-start | bytes 12296 | tf_op jit(solution)/shard_map/while/body/eval_jaxpr/ppermute | solution.py:594
  91.4 14.3 %collective-permute-start = (f32[8,128]{1,0:T(8,128)S(1)}, f32[8,128]{1,0:T(8,128)S(1)}, u32[]{:S(2)}, u32[]{:S(2)}) collective-permute-start(f32[8,128]{1,0:T(8,128)S(1)} %get-tuple-element.926), channel_id=1, source_target_pairs={{0,1},{1,0},{2,3},{3,2},{7,6},{6,7},{5,4},{4,5},{8,9},{9,8},{10,11... | collective-permute-start | bytes 12296 | tf_op jit(solution)/shard_map/while/body/eval_jaxpr/ppermute | solution.py:594
  99.0 6.3 %collective-permute-start.3 = (f32[8,128]{1,0:T(8,128)S(1)}, f32[8,128]{1,0:T(8,128)S(1)}, u32[]{:S(2)}, u32[]{:S(2)}) collective-permute-start(f32[8,128]{1,0:T(8,128)S(1)} %get-tuple-element.926), channel_id=1, source_target_pairs={{16,32},{32,16},{48,64},{64,48},{80,96},{96,80},{112,128},{128,112... | collective-permute-start | bytes 12296 | tf_op jit(solution)/shard_map/while/body/eval_jaxpr/ppermute | solution.py:594
  106.6 12.9 %collective-permute-start = (f32[8,128]{1,0:T(8,128)S(1)}, f32[8,128]{1,0:T(8,128)S(1)}, u32[]{:S(2)}, u32[]{:S(2)}) collective-permute-start(f32[8,128]{1,0:T(8,128)S(1)} %get-tuple-element.926), channel_id=1, source_target_pairs={{0,1},{1,0},{2,3},{3,2},{7,6},{6,7},{5,4},{4,5},{8,9},{9,8},{10,11... | collective-permute-start | bytes 12296 | tf_op jit(solution)/shard_map/while/body/eval_jaxpr/ppermute | solution.py:594
  120.5 13.0 %collective-permute-start = (f32[8,128]{1,0:T(8,128)S(1)}, f32[8,128]{1,0:T(8,128)S(1)}, u32[]{:S(2)}, u32[]{:S(2)}) collective-permute-start(f32[8,128]{1,0:T(8,128)S(1)} %get-tuple-element.926), channel_id=1, source_target_pairs={{0,1},{1,0},{2,3},{3,2},{7,6},{6,7},{5,4},{4,5},{8,9},{9,8},{10,11... | collective-permute-start | bytes 12296 | tf_op jit(solution)/shard_map/while/body/eval_jaxpr/ppermute | solution.py:594
  134.4 12.9 %collective-permute-start = (f32[8,128]{1,0:T(8,128)S(1)}, f32[8,128]{1,0:T(8,128)S(1)}, u32[]{:S(2)}, u32[]{:S(2)}) collective-permute-start(f32[8,128]{1,0:T(8,128)S(1)} %get-tuple-element.926), channel_id=1, source_target_pairs={{0,1},{1,0},{2,3},{3,2},{7,6},{6,7},{5,4},{4,5},{8,9},{9,8},{10,11... | collective-permute-start | bytes 12296 | tf_op jit(solution)/shard_map/while/body/eval_jaxpr/ppermute | solution.py:594
  148.2 13.0 %collective-permute-start = (f32[8,128]{1,0:T(8,128)S(1)}, f32[8,128]{1,0:T(8,128)S(1)}, u32[]{:S(2)}, u32[]{:S(2)}) collective-permute-start(f32[8,128]{1,0:T(8,128)S(1)} %get-tuple-element.926), channel_id=1, source_target_pairs={{0,1},{1,0},{2,3},{3,2},{7,6},{6,7},{5,4},{4,5},{8,9},{9,8},{10,11... | collective-permute-start | bytes 12296 | tf_op jit(solution)/shard_map/while/body/eval_jaxpr/ppermute | solution.py:594
  162.1 12.9 %collective-permute-start = (f32[8,128]{1,0:T(8,128)S(1)}, f32[8,128]{1,0:T(8,128)S(1)}, u32[]{:S(2)}, u32[]{:S(2)}) collective-permute-start(f32[8,128]{1,0:T(8,128)S(1)} %get-tuple-element.926), channel_id=1, source_target_pairs={{0,1},{1,0},{2,3},{3,2},{7,6},{6,7},{5,4},{4,5},{8,9},{9,8},{10,11... | collective-permute-start | bytes 12296 | tf_op jit(solution)/shard_map/while/body/eval_jaxpr/ppermute | solution.py:594
  176.0 13.0 %collective-permute-start = (f32[8,128]{1,0:T(8,128)S(1)}, f32[8,128]{1,0:T(8,128)S(1)}, u32[]{:S(2)}, u32[]{:S(2)}) collective-permute-start(f32[8,128]{1,0:T(8,128)S(1)} %get-tuple-element.926), channel_id=1, source_target_pairs={{0,1},{1,0},{2,3},{3,2},{7,6},{6,7},{5,4},{4,5},{8,9},{9,8},{10,11... | collective-permute-start | bytes 12296 | tf_op jit(solution)/shard_map/while/body/eval_jaxpr/ppermute | solution.py:594
  189.9 12.9 %collective-permute-start = (f32[8,128]{1,0:T(8,128)S(1)}, f32[8,128]{1,0:T(8,128)S(1)}, u32[]{:S(2)}, u32[]{:S(2)}) collective-permute-start(f32[8,128]{1,0:T(8,128)S(1)} %get-tuple-element.926), channel_id=1, source_target_pairs={{0,1},{1,0},{2,3},{3,2},{7,6},{6,7},{5,4},{4,5},{8,9},{9,8},{10,11... | collective-permute-start | bytes 12296 | tf_op jit(solution)/shard_map/while/body/eval_jaxpr/ppermute | solution.py:594
  203.7 13.0 %collective-permute-start = (f32[8,128]{1,0:T(8,128)S(1)}, f32[8,128]{1,0:T(8,128)S(1)}, u32[]{:S(2)}, u32[]{:S(2)}) collective-permute-start(f32[8,128]{1,0:T(8,128)S(1)} %get-tuple-element.926), channel_id=1, source_target_pairs={{0,1},{1,0},{2,3},{3,2},{7,6},{6,7},{5,4},{4,5},{8,9},{9,8},{10,11... | collective-permute-start | bytes 12296 | tf_op jit(solution)/shard_map/while/body/eval_jaxpr/ppermute | solution.py:594
  217.6 14.3 %collective-permute-start.12 = (f32[8,128]{1,0:T(8,128)S(1)}, f32[8,128]{1,0:T(8,128)S(1)}, u32[]{:S(2)}, u32[]{:S(2)}) collective-permute-start(f32[8,128]{1,0:T(8,128)S(1)} %get-tuple-element.580), channel_id=1, source_target_pairs={{16,32},{32,16},{48,64},{64,48},{80,96},{96,80},{112,128},{128,112... | collective-permute-start | bytes 12296 | tf_op jit(solution)/shard_map/ppermute | solution.py:594
  219.9 12.0 %collective-permute-start.11 = (f32[8,128]{1,0:T(8,128)S(1)}, f32[8,128]{1,0:T(8,128)S(1)}, u32[]{:S(2)}, u32[]{:S(2)}) collective-permute-start(f32[8,128]{1,0:T(8,128)S(1)} %get-tuple-element.580), channel_id=1, source_target_pairs={{1,2},{2,1},{3,7},{7,3},{6,5},{5,6},{4,8},{8,4},{9,10},{10,9},{11,... | collective-permute-start | bytes 12296 | tf_op jit(solution)/shard_map/ppermute | solution.py:594
  220.6 12.3 %collective-permute-start.10 = (f32[8,128]{1,0:T(8,128)S(1)}, f32[8,128]{1,0:T(8,128)S(1)}, u32[]{:S(2)}, u32[]{:S(2)}) collective-permute-start(f32[8,128]{1,0:T(8,128)S(1)} %get-tuple-element.580), channel_id=1, source_target_pairs={{0,16},{16,0},{32,48},{48,32},{64,80},{80,64},{96,112},{112,96},{1... | collective-permute-start | bytes 12296 | tf_op jit(solution)/shard_map/ppermute | solution.py:594
  224.7 8.8 %collective-permute-start.9 = (f32[8,128]{1,0:T(8,128)S(1)}, f32[8,128]{1,0:T(8,128)S(1)}, u32[]{:S(2)}, u32[]{:S(2)}) collective-permute-start(f32[8,128]{1,0:T(8,128)S(1)} %get-tuple-element.580), channel_id=1, source_target_pairs={{0,1},{1,0},{2,3},{3,2},{7,6},{6,7},{5,4},{4,5},{8,9},{9,8},{10,11... | collective-permute-start | bytes 12296 | tf_op jit(solution)/shard_map/ppermute | solution.py:594
  (41 other events, 199.0 us)

commit v3 on v2

--- a/solution.py
+++ b/solution.py
@@ -54,7 +54,7 @@
 
 
 def lane_gather(row, index):
-    return jnp.take_along_axis(row, index, axis=1)
+    return jnp.take_along_axis(row, index, axis=1, mode="promise_in_bounds")
 
 
 def pick_lanes(field, index):
@@ -524,12 +524,16 @@
         keep_forces(result, *rest)
 
 
-def order_kernel(rank, strains, last, out, store):
+def order_kernel(rank, strains, before_last, last, out, store):
     for t in range(STEPS):
         for c in range(STRAIN):
             row = (c * STEPS + t) * POINTS
             rows = slice(c * POINTS, (c + 1) * POINTS)
-            store[row : row + POINTS, :] = strains[t, rows, :] if t < STEPS - 1 else last[rows, :]
+            if t < STEPS - 2:
+                store[row : row + POINTS, :] = strains[t, rows, :]
+            else:
+                end = before_last if t == STEPS - 2 else last
+                store[row : row + POINTS, :] = end[rows, :]
     lane = lax.broadcasted_iota(jnp.int32, (LANES, ORDER_WIDTH), 1)
     groups = rank.shape[0] * LANES // ORDER_WIDTH
     values, chosen = [], []
@@ -685,8 +689,7 @@
         [strain_t, field_t, field_t, field_t, field_t, lanes_t, forces_t, lanes_t, wave_t],
         [VMEM] * 16,
     )(wave, *received, source, inverse_index, listed_index, field, connect_rows, *element_data)
-    strains = jnp.zeros((STEPS - 1, STRAIN * POINTS, LANES), f32)
-    strains = lax.dynamic_update_index_in_dim(strains, strain, 0, 0)
+    strains = jnp.zeros((STEPS - 2, STRAIN * POINTS, LANES), f32)
 
     def advance(last, displace, velocity, late, node_forces, send, wave):
         dom1, grp1, *new_late = exchange(send)
@@ -712,20 +715,20 @@
         return outs[0], displace, velocity, new_late, *outs[1:], wave
 
     def body(step, carried):
-        strains, *state = carried
-        strain, *state = advance(False, *state)
-        return (lax.dynamic_update_index_in_dim(strains, strain, step, 0), *state)
+        strains, strain, *state = carried
+        strains = lax.dynamic_update_index_in_dim(strains, strain, step - 1, 0)
+        return (strains, *advance(False, *state))
 
     none = [jnp.zeros((8, LANES), f32)] * 2
-    carried = (strains, displace, velocity, none, node_forces, send, wave)
-    strains, *state = lax.fori_loop(1, STEPS - 1, body, carried)
-    strain = advance(True, *state)[0]
+    carried = (strains, strain, displace, velocity, none, node_forces, send, wave)
+    strains, strain, *state = lax.fori_loop(1, STEPS - 1, body, carried)
+    strain = (strain, advance(True, *state)[0])
     (ordered,) = kernel_call(
         order_kernel,
         [jax.ShapeDtypeStruct((writers, STEPS * STRAIN, LANES), jnp.bfloat16)],
-        [VMEM] * 3,
-        scratch=[pltpu.VMEM((STEPS * STRAIN * POINTS, LANES), f32)],
-    )(rank, strains, strain)
+        [VMEM] * 4,
+        scratch=[pltpu.VMEM(((STEPS * STRAIN + 1) * POINTS, LANES), f32)],
+    )(rank, strains, *strain)
     pieces = lax.all_to_all(ordered, "dom", split_axis=0, concat_axis=0, tiled=True)
     (placed,) = kernel_call(
         place_kernel, [jax.ShapeDtypeStruct((STRAIN, STEPS, writers * LANES), jnp.bfloat16)], [VMEM]

time: 260 us -> 260 us (level)
  no operation moved by 1% of the time
where the time goes in v3:
time: 260 us; the launch traced here: 258 us
  starting transfers between devices  207 us (80%)
  blocking collectives  22.5 us (9%)
  Pallas kernels  20.9 us (8%)
  waiting for transfers between devices  5.01 us (2%)
    ppermute x60, starting transfers between devices, exchange(): received.append(lax.ppermute(send, axis, pairs))  198 us
    all_to_all x1, blocking collectives, shards(): lax.all_to_all(ordered, 'dom', split_axis=0, concat_axis=0, tiled=True)  22.5 us
    pallas_call x15, Pallas kernels, advance(): kernel_call(step_kernel, [strain_t] + ([] if last else [forces_t, lanes_t...  8.5 us
    ppermute x4, starting transfers between devices, shards(): received.append(lax.ppermute(send, ('grp', 'dom'), pairs))  8.16 us
    pallas_call x15, Pallas kernels, advance(): side(wave, dom1, grp1, *late, source, inverse_index, connect_rows, incide...  6.56 us
  transfers between devices with their start and end apart: 65, of which 15 were waited for; matrix products, arithmetic and copies ran while one was open for 0% of the time, Pallas kernels for 3%

profile of v3, /device:TPU:200, one launch (start us, length us, event | category | flops | bytes accessed | tf_op | source)
XLA Modules:
  0.0 257.7 jit_solution(6011439352941347765)
XLA Ops:
  12.8 204.2 %while.34 = (s32[]{:T(128)}, f32[14,96,128]{2,1,0:T(8,128)S(1)}, f32[96,128]{1,0:T(8,128)S(1)}, f32[8,512]{1,0:T(8,128)S(1)}, f32[8,512]{1,0:T(8,128)S(1)}, /*in...) while((s32[]{:T(128)}, f32[14,96,128]{2,1,0:T(8,128)S(1)}, ...), condition=%wide.region_1.2_spmd.clone, body=%wide.region_0.1_spmd.clone.sunk | while | flops 26626 | bytes 267817 | solution.py:724
  12.8 5.8 %collective-permute-start = (f32[8,128]{1,0:T(8,128)S(1)}, f32[8,128]{1,0:T(8,128)S(1)}, u32[]{:S(2)}, u32[]{:S(2)}) collective-permute-start(f32[8,128]{1,0:T(8,128)S(1)} %get-tuple-element.1154), channel_id=1, source_target_pairs={{0,1},{1,0},{2,3},{3,2},{7,6},{6,7},{5,4},{4,5},{8,9},{9,8},{10,11... | collective-permute-start | bytes 12296 | tf_op jit(solution)/shard_map/while/body/eval_jaxpr/ppermute | solution.py:598
  22.2 4.8 %collective-permute-start.1 = (f32[8,128]{1,0:T(8,128)S(1)}, f32[8,128]{1,0:T(8,128)S(1)}, u32[]{:S(2)}, u32[]{:S(2)}) collective-permute-start(f32[8,128]{1,0:T(8,128)S(1)} %get-tuple-element.1154), channel_id=1, source_target_pairs={{0,16},{16,0},{32,48},{48,32},{64,80},{80,64},{96,112},{112,96},{1... | collective-permute-start | bytes 12296 | tf_op jit(solution)/shard_map/while/body/eval_jaxpr/ppermute | solution.py:598
  28.4 9.4 %collective-permute-start = (f32[8,128]{1,0:T(8,128)S(1)}, f32[8,128]{1,0:T(8,128)S(1)}, u32[]{:S(2)}, u32[]{:S(2)}) collective-permute-start(f32[8,128]{1,0:T(8,128)S(1)} %get-tuple-element.1154), channel_id=1, source_target_pairs={{0,1},{1,0},{2,3},{3,2},{7,6},{6,7},{5,4},{4,5},{8,9},{9,8},{10,11... | collective-permute-start | bytes 12296 | tf_op jit(solution)/shard_map/while/body/eval_jaxpr/ppermute | solution.py:598
  40.4 4.6 %collective-permute-start.1 = (f32[8,128]{1,0:T(8,128)S(1)}, f32[8,128]{1,0:T(8,128)S(1)}, u32[]{:S(2)}, u32[]{:S(2)}) collective-permute-start(f32[8,128]{1,0:T(8,128)S(1)} %get-tuple-element.1154), channel_id=1, source_target_pairs={{0,16},{16,0},{32,48},{48,32},{64,80},{80,64},{96,112},{112,96},{1... | collective-permute-start | bytes 12296 | tf_op jit(solution)/shard_map/while/body/eval_jaxpr/ppermute | solution.py:598
  46.4 10.6 %collective-permute-start = (f32[8,128]{1,0:T(8,128)S(1)}, f32[8,128]{1,0:T(8,128)S(1)}, u32[]{:S(2)}, u32[]{:S(2)}) collective-permute-start(f32[8,128]{1,0:T(8,128)S(1)} %get-tuple-element.1154), channel_id=1, source_target_pairs={{0,1},{1,0},{2,3},{3,2},{7,6},{6,7},{5,4},{4,5},{8,9},{9,8},{10,11... | collective-permute-start | bytes 12296 | tf_op jit(solution)/shard_map/while/body/eval_jaxpr/ppermute | solution.py:598
  64.5 5.2 %collective-permute-start = (f32[8,128]{1,0:T(8,128)S(1)}, f32[8,128]{1,0:T(8,128)S(1)}, u32[]{:S(2)}, u32[]{:S(2)}) collective-permute-start(f32[8,128]{1,0:T(8,128)S(1)} %get-tuple-element.1154), channel_id=1, source_target_pairs={{0,1},{1,0},{2,3},{3,2},{7,6},{6,7},{5,4},{4,5},{8,9},{9,8},{10,11... | collective-permute-start | bytes 12296 | tf_op jit(solution)/shard_map/while/body/eval_jaxpr/ppermute | solution.py:598
  72.9 4.6 %collective-permute-start.1 = (f32[8,128]{1,0:T(8,128)S(1)}, f32[8,128]{1,0:T(8,128)S(1)}, u32[]{:S(2)}, u32[]{:S(2)}) collective-permute-start(f32[8,128]{1,0:T(8,128)S(1)} %get-tuple-element.1154), channel_id=1, source_target_pairs={{0,16},{16,0},{32,48},{48,32},{64,80},{80,64},{96,112},{112,96},{1... | collective-permute-start | bytes 12296 | tf_op jit(solution)/shard_map/while/body/eval_jaxpr/ppermute | solution.py:598
  78.9 5.0 %collective-permute-start = (f32[8,128]{1,0:T(8,128)S(1)}, f32[8,128]{1,0:T(8,128)S(1)}, u32[]{:S(2)}, u32[]{:S(2)}) collective-permute-start(f32[8,128]{1,0:T(8,128)S(1)} %get-tuple-element.1154), channel_id=1, source_target_pairs={{0,1},{1,0},{2,3},{3,2},{7,6},{6,7},{5,4},{4,5},{8,9},{9,8},{10,11... | collective-permute-start | bytes 12296 | tf_op jit(solution)/shard_map/while/body/eval_jaxpr/ppermute | solution.py:598
  91.1 7.5 %collective-permute-start = (f32[8,128]{1,0:T(8,128)S(1)}, f32[8,128]{1,0:T(8,128)S(1)}, u32[]{:S(2)}, u32[]{:S(2)}) collective-permute-start(f32[8,128]{1,0:T(8,128)S(1)} %get-tuple-element.1154), channel_id=1, source_target_pairs={{0,1},{1,0},{2,3},{3,2},{7,6},{6,7},{5,4},{4,5},{8,9},{9,8},{10,11... | collective-permute-start | bytes 12296 | tf_op jit(solution)/shard_map/while/body/eval_jaxpr/ppermute | solution.py:598
  101.3 3.6 %collective-permute-start.1 = (f32[8,128]{1,0:T(8,128)S(1)}, f32[8,128]{1,0:T(8,128)S(1)}, u32[]{:S(2)}, u32[]{:S(2)}) collective-permute-start(f32[8,128]{1,0:T(8,128)S(1)} %get-tuple-element.1154), channel_id=1, source_target_pairs={{0,16},{16,0},{32,48},{48,32},{64,80},{80,64},{96,112},{112,96},{1... | collective-permute-start | bytes 12296 | tf_op jit(solution)/shard_map/while/body/eval_jaxpr/ppermute | solution.py:598
  106.3 6.2 %collective-permute-start = (f32[8,128]{1,0:T(8,128)S(1)}, f32[8,128]{1,0:T(8,128)S(1)}, u32[]{:S(2)}, u32[]{:S(2)}) collective-permute-start(f32[8,128]{1,0:T(8,128)S(1)} %get-tuple-element.1154), channel_id=1, source_target_pairs={{0,1},{1,0},{2,3},{3,2},{7,6},{6,7},{5,4},{4,5},{8,9},{9,8},{10,11... | collective-permute-start | bytes 12296 | tf_op jit(solution)/shard_map/while/body/eval_jaxpr/ppermute | solution.py:598
  120.1 6.2 %collective-permute-start = (f32[8,128]{1,0:T(8,128)S(1)}, f32[8,128]{1,0:T(8,128)S(1)}, u32[]{:S(2)}, u32[]{:S(2)}) collective-permute-start(f32[8,128]{1,0:T(8,128)S(1)} %get-tuple-element.1154), channel_id=1, source_target_pairs={{0,1},{1,0},{2,3},{3,2},{7,6},{6,7},{5,4},{4,5},{8,9},{9,8},{10,11... | collective-permute-start | bytes 12296 | tf_op jit(solution)/shard_map/while/body/eval_jaxpr/ppermute | solution.py:598
  128.9 3.6 %collective-permute-start.1 = (f32[8,128]{1,0:T(8,128)S(1)}, f32[8,128]{1,0:T(8,128)S(1)}, u32[]{:S(2)}, u32[]{:S(2)}) collective-permute-start(f32[8,128]{1,0:T(8,128)S(1)} %get-tuple-element.1154), channel_id=1, source_target_pairs={{0,16},{16,0},{32,48},{48,32},{64,80},{80,64},{96,112},{112,96},{1... | collective-permute-start | bytes 12296 | tf_op jit(solution)/shard_map/while/body/eval_jaxpr/ppermute | solution.py:598
  134.0 6.2 %collective-permute-start = (f32[8,128]{1,0:T(8,128)S(1)}, f32[8,128]{1,0:T(8,128)S(1)}, u32[]{:S(2)}, u32[]{:S(2)}) collective-permute-start(f32[8,128]{1,0:T(8,128)S(1)} %get-tuple-element.1154), channel_id=1, source_target_pairs={{0,1},{1,0},{2,3},{3,2},{7,6},{6,7},{5,4},{4,5},{8,9},{9,8},{10,11... | collective-permute-start | bytes 12296 | tf_op jit(solution)/shard_map/while/body/eval_jaxpr/ppermute | solution.py:598
  147.8 6.2 %collective-permute-start = (f32[8,128]{1,0:T(8,128)S(1)}, f32[8,128]{1,0:T(8,128)S(1)}, u32[]{:S(2)}, u32[]{:S(2)}) collective-permute-start(f32[8,128]{1,0:T(8,128)S(1)} %get-tuple-element.1154), channel_id=1, source_target_pairs={{0,1},{1,0},{2,3},{3,2},{7,6},{6,7},{5,4},{4,5},{8,9},{9,8},{10,11... | collective-permute-start | bytes 12296 | tf_op jit(solution)/shard_map/while/body/eval_jaxpr/ppermute | solution.py:598
  156.6 3.6 %collective-permute-start.1 = (f32[8,128]{1,0:T(8,128)S(1)}, f32[8,128]{1,0:T(8,128)S(1)}, u32[]{:S(2)}, u32[]{:S(2)}) collective-permute-start(f32[8,128]{1,0:T(8,128)S(1)} %get-tuple-element.1154), channel_id=1, source_target_pairs={{0,16},{16,0},{32,48},{48,32},{64,80},{80,64},{96,112},{112,96},{1... | collective-permute-start | bytes 12296 | tf_op jit(solution)/shard_map/while/body/eval_jaxpr/ppermute | solution.py:598
  161.7 6.2 %collective-permute-start = (f32[8,128]{1,0:T(8,128)S(1)}, f32[8,128]{1,0:T(8,128)S(1)}, u32[]{:S(2)}, u32[]{:S(2)}) collective-permute-start(f32[8,128]{1,0:T(8,128)S(1)} %get-tuple-element.1154), channel_id=1, source_target_pairs={{0,1},{1,0},{2,3},{3,2},{7,6},{6,7},{5,4},{4,5},{8,9},{9,8},{10,11... | collective-permute-start | bytes 12296 | tf_op jit(solution)/shard_map/while/body/eval_jaxpr/ppermute | solution.py:598
  175.5 6.2 %collective-permute-start = (f32[8,128]{1,0:T(8,128)S(1)}, f32[8,128]{1,0:T(8,128)S(1)}, u32[]{:S(2)}, u32[]{:S(2)}) collective-permute-start(f32[8,128]{1,0:T(8,128)S(1)} %get-tuple-element.1154), channel_id=1, source_target_pairs={{0,1},{1,0},{2,3},{3,2},{7,6},{6,7},{5,4},{4,5},{8,9},{9,8},{10,11... | collective-permute-start | bytes 12296 | tf_op jit(solution)/shard_map/while/body/eval_jaxpr/ppermute | solution.py:598
  189.3 6.2 %collective-permute-start = (f32[8,128]{1,0:T(8,128)S(1)}, f32[8,128]{1,0:T(8,128)S(1)}, u32[]{:S(2)}, u32[]{:S(2)}) collective-permute-start(f32[8,128]{1,0:T(8,128)S(1)} %get-tuple-element.1154), channel_id=1, source_target_pairs={{0,1},{1,0},{2,3},{3,2},{7,6},{6,7},{5,4},{4,5},{8,9},{9,8},{10,11... | collective-permute-start | bytes 12296 | tf_op jit(solution)/shard_map/while/body/eval_jaxpr/ppermute | solution.py:598
  203.1 6.2 %collective-permute-start = (f32[8,128]{1,0:T(8,128)S(1)}, f32[8,128]{1,0:T(8,128)S(1)}, u32[]{:S(2)}, u32[]{:S(2)}) collective-permute-start(f32[8,128]{1,0:T(8,128)S(1)} %get-tuple-element.1154), channel_id=1, source_target_pairs={{0,1},{1,0},{2,3},{3,2},{7,6},{6,7},{5,4},{4,5},{8,9},{9,8},{10,11... | collective-permute-start | bytes 12296 | tf_op jit(solution)/shard_map/while/body/eval_jaxpr/ppermute | solution.py:598
  220.0 4.1 %collective-permute-start.10 = (f32[8,128]{1,0:T(8,128)S(1)}, f32[8,128]{1,0:T(8,128)S(1)}, u32[]{:S(2)}, u32[]{:S(2)}) collective-permute-start(f32[8,128]{1,0:T(8,128)S(1)} %get-tuple-element.798), channel_id=1, source_target_pairs={{0,16},{16,0},{32,48},{48,32},{64,80},{80,64},{96,112},{112,96},{1... | collective-permute-start | bytes 12296 | tf_op jit(solution)/shard_map/ppermute | solution.py:598
  224.1 7.3 %collective-permute-start.9 = (f32[8,128]{1,0:T(8,128)S(1)}, f32[8,128]{1,0:T(8,128)S(1)}, u32[]{:S(2)}, u32[]{:S(2)}) collective-permute-start(f32[8,128]{1,0:T(8,128)S(1)} %get-tuple-element.798), channel_id=1, source_target_pairs={{0,1},{1,0},{2,3},{3,2},{7,6},{6,7},{5,4},{4,5},{8,9},{9,8},{10,11... | collective-permute-start | bytes 12296 | tf_op jit(solution)/shard_map/ppermute | solution.py:598
  234.4 22.5 %all_to_all.5.pieces = bf16[16,96,128]{2,1,0:T(8,128)(2,1)S(1)} all-to-all(bf16[16,96,128]{2,1,0:T(8,128)(2,1)S(1)} %shard_map.114), channel_id=1, replica_groups=mesh['grp'=32,'dom'=16] {'dom'}, dimensions={0} | all-to-all | bytes 786432 | tf_op jit(solution)/shard_map/all_to_all | solution.py:732
  (247 shorter events, 104.1 us)
Async XLA Ops:
  1.7 10.4 %collective-permute-start.8 = (f32[8,128]{1,0:T(8,128)S(1)}, f32[8,128]{1,0:T(8,128)S(1)}, u32[]{:S(2)}, u32[]{:S(2)}) collective-permute-start(f32[8,128]{1,0:T(8,128)S(1)} %get-tuple-element.774), channel_id=1, source_target_pairs={{0,16},{1,17},{2,18},{3,19},{4,23},{5,22},{6,21},{7,20},{8,24},{9,... | collective-permute-start | bytes 12296 | tf_op jit(solution)/shard_map/ppermute | solution.py:648
  3.6 8.4 %collective-permute-start.7 = (f32[8,128]{1,0:T(8,128)S(1)}, f32[8,128]{1,0:T(8,128)S(1)}, u32[]{:S(2)}, u32[]{:S(2)}) collective-permute-start(f32[8,128]{1,0:T(8,128)S(1)} %get-tuple-element.774), channel_id=1, source_target_pairs={{0,1},{1,0},{2,3},{3,2},{4,6},{5,7},{6,4},{7,5},{8,9},{9,8},{10,11... | collective-permute-start | bytes 12296 | tf_op jit(solution)/shard_map/ppermute | solution.py:648
  12.8 15.0 %collective-permute-start = (f32[8,128]{1,0:T(8,128)S(1)}, f32[8,128]{1,0:T(8,128)S(1)}, u32[]{:S(2)}, u32[]{:S(2)}) collective-permute-start(f32[8,128]{1,0:T(8,128)S(1)} %get-tuple-element.1154), channel_id=1, source_target_pairs={{0,1},{1,0},{2,3},{3,2},{7,6},{6,7},{5,4},{4,5},{8,9},{9,8},{10,11... | collective-permute-start | bytes 12296 | tf_op jit(solution)/shard_map/while/body/eval_jaxpr/ppermute | solution.py:598
  18.7 8.4 %collective-permute-start.3 = (f32[8,128]{1,0:T(8,128)S(1)}, f32[8,128]{1,0:T(8,128)S(1)}, u32[]{:S(2)}, u32[]{:S(2)}) collective-permute-start(f32[8,128]{1,0:T(8,128)S(1)} %get-tuple-element.1154), channel_id=1, source_target_pairs={{16,32},{32,16},{48,64},{64,48},{80,96},{96,80},{112,128},{128,112... | collective-permute-start | bytes 12296 | tf_op jit(solution)/shard_map/while/body/eval_jaxpr/ppermute | solution.py:598
  28.4 17.4 %collective-permute-start = (f32[8,128]{1,0:T(8,128)S(1)}, f32[8,128]{1,0:T(8,128)S(1)}, u32[]{:S(2)}, u32[]{:S(2)}) collective-permute-start(f32[8,128]{1,0:T(8,128)S(1)} %get-tuple-element.1154), channel_id=1, source_target_pairs={{0,1},{1,0},{2,3},{3,2},{7,6},{6,7},{5,4},{4,5},{8,9},{9,8},{10,11... | collective-permute-start | bytes 12296 | tf_op jit(solution)/shard_map/while/body/eval_jaxpr/ppermute | solution.py:598
  37.8 7.2 %collective-permute-start.3 = (f32[8,128]{1,0:T(8,128)S(1)}, f32[8,128]{1,0:T(8,128)S(1)}, u32[]{:S(2)}, u32[]{:S(2)}) collective-permute-start(f32[8,128]{1,0:T(8,128)S(1)} %get-tuple-element.1154), channel_id=1, source_target_pairs={{16,32},{32,16},{48,64},{64,48},{80,96},{96,80},{112,128},{128,112... | collective-permute-start | bytes 12296 | tf_op jit(solution)/shard_map/while/body/eval_jaxpr/ppermute | solution.py:598
  46.4 17.6 %collective-permute-start = (f32[8,128]{1,0:T(8,128)S(1)}, f32[8,128]{1,0:T(8,128)S(1)}, u32[]{:S(2)}, u32[]{:S(2)}) collective-permute-start(f32[8,128]{1,0:T(8,128)S(1)} %get-tuple-element.1154), channel_id=1, source_target_pairs={{0,1},{1,0},{2,3},{3,2},{7,6},{6,7},{5,4},{4,5},{8,9},{9,8},{10,11... | collective-permute-start | bytes 12296 | tf_op jit(solution)/shard_map/while/body/eval_jaxpr/ppermute | solution.py:598
  64.5 13.8 %collective-permute-start = (f32[8,128]{1,0:T(8,128)S(1)}, f32[8,128]{1,0:T(8,128)S(1)}, u32[]{:S(2)}, u32[]{:S(2)}) collective-permute-start(f32[8,128]{1,0:T(8,128)S(1)} %get-tuple-element.1154), channel_id=1, source_target_pairs={{0,1},{1,0},{2,3},{3,2},{7,6},{6,7},{5,4},{4,5},{8,9},{9,8},{10,11... | collective-permute-start | bytes 12296 | tf_op jit(solution)/shard_map/while/body/eval_jaxpr/ppermute | solution.py:598
  69.7 7.9 %collective-permute-start.3 = (f32[8,128]{1,0:T(8,128)S(1)}, f32[8,128]{1,0:T(8,128)S(1)}, u32[]{:S(2)}, u32[]{:S(2)}) collective-permute-start(f32[8,128]{1,0:T(8,128)S(1)} %get-tuple-element.1154), channel_id=1, source_target_pairs={{16,32},{32,16},{48,64},{64,48},{80,96},{96,80},{112,128},{128,112... | collective-permute-start | bytes 12296 | tf_op jit(solution)/shard_map/while/body/eval_jaxpr/ppermute | solution.py:598
  78.9 11.6 %collective-permute-start = (f32[8,128]{1,0:T(8,128)S(1)}, f32[8,128]{1,0:T(8,128)S(1)}, u32[]{:S(2)}, u32[]{:S(2)}) collective-permute-start(f32[8,128]{1,0:T(8,128)S(1)} %get-tuple-element.1154), channel_id=1, source_target_pairs={{0,1},{1,0},{2,3},{3,2},{7,6},{6,7},{5,4},{4,5},{8,9},{9,8},{10,11... | collective-permute-start | bytes 12296 | tf_op jit(solution)/shard_map/while/body/eval_jaxpr/ppermute | solution.py:598
  91.1 14.6 %collective-permute-start = (f32[8,128]{1,0:T(8,128)S(1)}, f32[8,128]{1,0:T(8,128)S(1)}, u32[]{:S(2)}, u32[]{:S(2)}) collective-permute-start(f32[8,128]{1,0:T(8,128)S(1)} %get-tuple-element.1154), channel_id=1, source_target_pairs={{0,1},{1,0},{2,3},{3,2},{7,6},{6,7},{5,4},{4,5},{8,9},{9,8},{10,11... | collective-permute-start | bytes 12296 | tf_op jit(solution)/shard_map/while/body/eval_jaxpr/ppermute | solution.py:598
  98.7 6.3 %collective-permute-start.3 = (f32[8,128]{1,0:T(8,128)S(1)}, f32[8,128]{1,0:T(8,128)S(1)}, u32[]{:S(2)}, u32[]{:S(2)}) collective-permute-start(f32[8,128]{1,0:T(8,128)S(1)} %get-tuple-element.1154), channel_id=1, source_target_pairs={{16,32},{32,16},{48,64},{64,48},{80,96},{96,80},{112,128},{128,112... | collective-permute-start | bytes 12296 | tf_op jit(solution)/shard_map/while/body/eval_jaxpr/ppermute | solution.py:598
  106.3 13.2 %collective-permute-start = (f32[8,128]{1,0:T(8,128)S(1)}, f32[8,128]{1,0:T(8,128)S(1)}, u32[]{:S(2)}, u32[]{:S(2)}) collective-permute-start(f32[8,128]{1,0:T(8,128)S(1)} %get-tuple-element.1154), channel_id=1, source_target_pairs={{0,1},{1,0},{2,3},{3,2},{7,6},{6,7},{5,4},{4,5},{8,9},{9,8},{10,11... | collective-permute-start | bytes 12296 | tf_op jit(solution)/shard_map/while/body/eval_jaxpr/ppermute | solution.py:598
  120.1 13.3 %collective-permute-start = (f32[8,128]{1,0:T(8,128)S(1)}, f32[8,128]{1,0:T(8,128)S(1)}, u32[]{:S(2)}, u32[]{:S(2)}) collective-permute-start(f32[8,128]{1,0:T(8,128)S(1)} %get-tuple-element.1154), channel_id=1, source_target_pairs={{0,1},{1,0},{2,3},{3,2},{7,6},{6,7},{5,4},{4,5},{8,9},{9,8},{10,11... | collective-permute-start | bytes 12296 | tf_op jit(solution)/shard_map/while/body/eval_jaxpr/ppermute | solution.py:598
  134.0 13.2 %collective-permute-start = (f32[8,128]{1,0:T(8,128)S(1)}, f32[8,128]{1,0:T(8,128)S(1)}, u32[]{:S(2)}, u32[]{:S(2)}) collective-permute-start(f32[8,128]{1,0:T(8,128)S(1)} %get-tuple-element.1154), channel_id=1, source_target_pairs={{0,1},{1,0},{2,3},{3,2},{7,6},{6,7},{5,4},{4,5},{8,9},{9,8},{10,11... | collective-permute-start | bytes 12296 | tf_op jit(solution)/shard_map/while/body/eval_jaxpr/ppermute | solution.py:598
  147.8 13.3 %collective-permute-start = (f32[8,128]{1,0:T(8,128)S(1)}, f32[8,128]{1,0:T(8,128)S(1)}, u32[]{:S(2)}, u32[]{:S(2)}) collective-permute-start(f32[8,128]{1,0:T(8,128)S(1)} %get-tuple-element.1154), channel_id=1, source_target_pairs={{0,1},{1,0},{2,3},{3,2},{7,6},{6,7},{5,4},{4,5},{8,9},{9,8},{10,11... | collective-permute-start | bytes 12296 | tf_op jit(solution)/shard_map/while/body/eval_jaxpr/ppermute | solution.py:598
  161.7 13.2 %collective-permute-start = (f32[8,128]{1,0:T(8,128)S(1)}, f32[8,128]{1,0:T(8,128)S(1)}, u32[]{:S(2)}, u32[]{:S(2)}) collective-permute-start(f32[8,128]{1,0:T(8,128)S(1)} %get-tuple-element.1154), channel_id=1, source_target_pairs={{0,1},{1,0},{2,3},{3,2},{7,6},{6,7},{5,4},{4,5},{8,9},{9,8},{10,11... | collective-permute-start | bytes 12296 | tf_op jit(solution)/shard_map/while/body/eval_jaxpr/ppermute | solution.py:598
  175.5 13.3 %collective-permute-start = (f32[8,128]{1,0:T(8,128)S(1)}, f32[8,128]{1,0:T(8,128)S(1)}, u32[]{:S(2)}, u32[]{:S(2)}) collective-permute-start(f32[8,128]{1,0:T(8,128)S(1)} %get-tuple-element.1154), channel_id=1, source_target_pairs={{0,1},{1,0},{2,3},{3,2},{7,6},{6,7},{5,4},{4,5},{8,9},{9,8},{10,11... | collective-permute-start | bytes 12296 | tf_op jit(solution)/shard_map/while/body/eval_jaxpr/ppermute | solution.py:598
  189.3 13.2 %collective-permute-start = (f32[8,128]{1,0:T(8,128)S(1)}, f32[8,128]{1,0:T(8,128)S(1)}, u32[]{:S(2)}, u32[]{:S(2)}) collective-permute-start(f32[8,128]{1,0:T(8,128)S(1)} %get-tuple-element.1154), channel_id=1, source_target_pairs={{0,1},{1,0},{2,3},{3,2},{7,6},{6,7},{5,4},{4,5},{8,9},{9,8},{10,11... | collective-permute-start | bytes 12296 | tf_op jit(solution)/shard_map/while/body/eval_jaxpr/ppermute | solution.py:598
  203.1 13.3 %collective-permute-start = (f32[8,128]{1,0:T(8,128)S(1)}, f32[8,128]{1,0:T(8,128)S(1)}, u32[]{:S(2)}, u32[]{:S(2)}) collective-permute-start(f32[8,128]{1,0:T(8,128)S(1)} %get-tuple-element.1154), channel_id=1, source_target_pairs={{0,1},{1,0},{2,3},{3,2},{7,6},{6,7},{5,4},{4,5},{8,9},{9,8},{10,11... | collective-permute-start | bytes 12296 | tf_op jit(solution)/shard_map/while/body/eval_jaxpr/ppermute | solution.py:598
  217.0 14.3 %collective-permute-start.12 = (f32[8,128]{1,0:T(8,128)S(1)}, f32[8,128]{1,0:T(8,128)S(1)}, u32[]{:S(2)}, u32[]{:S(2)}) collective-permute-start(f32[8,128]{1,0:T(8,128)S(1)} %get-tuple-element.798), channel_id=1, source_target_pairs={{16,32},{32,16},{48,64},{64,48},{80,96},{96,80},{112,128},{128,112... | collective-permute-start | bytes 12296 | tf_op jit(solution)/shard_map/ppermute | solution.py:598
  219.3 12.1 %collective-permute-start.11 = (f32[8,128]{1,0:T(8,128)S(1)}, f32[8,128]{1,0:T(8,128)S(1)}, u32[]{:S(2)}, u32[]{:S(2)}) collective-permute-start(f32[8,128]{1,0:T(8,128)S(1)} %get-tuple-element.798), channel_id=1, source_target_pairs={{1,2},{2,1},{3,7},{7,3},{6,5},{5,6},{4,8},{8,4},{9,10},{10,9},{11,... | collective-permute-start | bytes 12296 | tf_op jit(solution)/shard_map/ppermute | solution.py:598
  220.0 12.4 %collective-permute-start.10 = (f32[8,128]{1,0:T(8,128)S(1)}, f32[8,128]{1,0:T(8,128)S(1)}, u32[]{:S(2)}, u32[]{:S(2)}) collective-permute-start(f32[8,128]{1,0:T(8,128)S(1)} %get-tuple-element.798), channel_id=1, source_target_pairs={{0,16},{16,0},{32,48},{48,32},{64,80},{80,64},{96,112},{112,96},{1... | collective-permute-start | bytes 12296 | tf_op jit(solution)/shard_map/ppermute | solution.py:598
  224.1 8.9 %collective-permute-start.9 = (f32[8,128]{1,0:T(8,128)S(1)}, f32[8,128]{1,0:T(8,128)S(1)}, u32[]{:S(2)}, u32[]{:S(2)}) collective-permute-start(f32[8,128]{1,0:T(8,128)S(1)} %get-tuple-element.798), channel_id=1, source_target_pairs={{0,1},{1,0},{2,3},{3,2},{7,6},{6,7},{5,4},{4,5},{8,9},{9,8},{10,11... | collective-permute-start | bytes 12296 | tf_op jit(solution)/shard_map/ppermute | solution.py:598
  (41 other events, 199.2 us)

commit v4 on v3

--- a/solution.py
+++ b/solution.py
@@ -524,34 +524,54 @@
         keep_forces(result, *rest)
 
 
-def order_kernel(rank, strains, before_last, last, out, store):
+def order_kernel(rank, strains, before_last, total, chosen, store):
     for t in range(STEPS):
         for c in range(STRAIN):
             row = (c * STEPS + t) * POINTS
             rows = slice(c * POINTS, (c + 1) * POINTS)
             if t < STEPS - 2:
-                store[row : row + POINTS, :] = strains[t, rows, :]
+                block = strains[t, rows, :]
+            elif t == STEPS - 2:
+                block = before_last[rows, :]
             else:
-                end = before_last if t == STEPS - 2 else last
-                store[row : row + POINTS, :] = end[rows, :]
+                block = jnp.zeros((POINTS, LANES), jnp.float32)
+            store[row : row + POINTS, :] = block
     lane = lax.broadcasted_iota(jnp.int32, (LANES, ORDER_WIDTH), 1)
-    groups = rank.shape[0] * LANES // ORDER_WIDTH
-    values, chosen = [], []
     for q in range(POINTS):
-        block = store[pl.ds(q, STEPS * STRAIN, stride=POINTS), :]
-        row = rank[q : q + 1, :]
-        group = row // ORDER_WIDTH
-        masked = [jnp.where(group == k, block, 0.0) for k in range(groups)]
+        column = jnp.broadcast_to(rank[q : q + 1, :] % ORDER_WIDTH, (LANES, LANES)).T
+        wide = jnp.concatenate([column] * (ORDER_WIDTH // LANES), axis=1)
+        chosen[q * LANES : (q + 1) * LANES, :] = jnp.where(wide == lane, 1.0, 0.0).astype(
+            jnp.bfloat16
+        )
+    total[...] = matmul(grouped_values(rank, store, STEPS * STRAIN), chosen[...])
+
+
+def grouped_values(rank, store, height):
+    values = []
+    for q in range(POINTS):
+        block = store[pl.ds(q, height, stride=POINTS), :]
+        group = rank[q : q + 1, :] // ORDER_WIDTH
+        masked = [
+            jnp.where(group == k, block, 0.0) for k in range(POINTS * LANES // ORDER_WIDTH)
+        ]
         values.append(jnp.concatenate(masked, axis=0).astype(jnp.bfloat16))
-        column = jnp.broadcast_to(row % ORDER_WIDTH, (LANES, LANES)).T
-        wide = jnp.concatenate([column] * (ORDER_WIDTH // LANES), axis=1)
-        chosen.append(jnp.where(wide == lane, 1.0, 0.0).astype(jnp.bfloat16))
-    total = matmul(jnp.concatenate(values, axis=1), jnp.concatenate(chosen, axis=0))
+    return jnp.concatenate(values, axis=1)
+
+
+def finish_kernel(rank, total, chosen, last, out, store):
+    store[...] = jnp.zeros(store.shape, jnp.float32)
+    store[0 : STRAIN * POINTS, :] = last[...]
+    ends = matmul(grouped_values(rank, store, 8), chosen[...])
     height = STEPS * STRAIN
+    row_id = lax.broadcasted_iota(jnp.int32, (STEPS, LANES), 0)
     for w in range(rank.shape[0]):
         k, i = w * LANES // ORDER_WIDTH, w % (ORDER_WIDTH // LANES)
-        block = total[k * height : (k + 1) * height, i * LANES : (i + 1) * LANES]
-        out[w] = block.astype(jnp.bfloat16)
+        lanes = slice(i * LANES, (i + 1) * LANES)
+        for c in range(STRAIN):
+            row = k * height + c * STEPS
+            end = jnp.broadcast_to(ends[8 * k + c : 8 * k + c + 1, lanes], (STEPS, LANES))
+            block = jnp.where(row_id == STEPS - 1, end, total[row : row + STEPS, lanes])
+            out[w, c * STEPS : (c + 1) * STEPS, :] = block.astype(jnp.bfloat16)
 
 
 def place_kernel(pieces, out):
@@ -722,13 +742,23 @@
     none = [jnp.zeros((8, LANES), f32)] * 2
     carried = (strains, strain, displace, velocity, none, node_forces, send, wave)
     strains, strain, *state = lax.fori_loop(1, STEPS - 1, body, carried)
-    strain = (strain, advance(True, *state)[0])
+    order = kernel_call(
+        order_kernel,
+        [
+            jax.ShapeDtypeStruct((POINTS * LANES // ORDER_WIDTH * STEPS * STRAIN, ORDER_WIDTH), f32),
+            jax.ShapeDtypeStruct((POINTS * LANES, ORDER_WIDTH), bf16),
+        ],
+        [VMEM] * 3,
+        scratch=[pltpu.VMEM(((STEPS * STRAIN + 1) * POINTS, LANES), f32)],
+    )
+    total, chosen = order(rank, strains, strain)
+    strain = advance(True, *state)[0]
     (ordered,) = kernel_call(
-        order_kernel,
-        [jax.ShapeDtypeStruct((writers, STEPS * STRAIN, LANES), jnp.bfloat16)],
+        finish_kernel,
+        [jax.ShapeDtypeStruct((writers, STEPS * STRAIN, LANES), bf16)],
         [VMEM] * 4,
-        scratch=[pltpu.VMEM(((STEPS * STRAIN + 1) * POINTS, LANES), f32)],
-    )(rank, strains, *strain)
+        scratch=[pltpu.VMEM((9 * POINTS, LANES), f32)],
+    )(rank, total, chosen, strain)
     pieces = lax.all_to_all(ordered, "dom", split_axis=0, concat_axis=0, tiled=True)
     (placed,) = kernel_call(
         place_kernel, [jax.ShapeDtypeStruct((STRAIN, STEPS, writers * LANES), jnp.bfloat16)], [VMEM]

time: 260 us -> 259 us (level)
  the two profiles are of different devices: /device:TPU:200 before, /device:TPU:256 now
where the time goes in v4:
time: 259 us; the launch traced here: 257 us
  starting transfers between devices  198 us (76%)
  blocking collectives  23.2 us (9%)
  Pallas kernels  21.1 us (8%)
  waiting for transfers between devices  12.6 us (5%)
    ppermute x60, starting transfers between devices, exchange(): received.append(lax.ppermute(send, axis, pairs))  189 us
    all_to_all x1, blocking collectives, shards(): lax.all_to_all(ordered, 'dom', split_axis=0, concat_axis=0, tiled=True)  23.2 us
    ppermute x60, waiting for transfers between devices, exchange(): received.append(lax.ppermute(send, axis, pairs))  10.8 us
    pallas_call x15, Pallas kernels, advance(): kernel_call(step_kernel, [strain_t] + ([] if last else [forces_t, lanes_t...  8.51 us
    ppermute x4, starting transfers between devices, shards(): received.append(lax.ppermute(send, ('grp', 'dom'), pairs))  8.38 us
    pallas_call x15, Pallas kernels, advance(): side(wave, dom1, grp1, *late, source, inverse_index, connect_rows, incide...  6.5 us
  transfers between devices with their start and end apart: 65, of which 25 were waited for; matrix products, arithmetic and copies ran while one was open for 0% of the time, Pallas kernels for 4%

profile of v4, /device:TPU:256, one launch (start us, length us, event | category | flops | bytes accessed | tf_op | source)
XLA Modules:
  0.0 256.7 jit_solution(842556154403727437)
XLA Ops:
  14.8 201.2 %while.34 = (s32[]{:T(128)}, f32[14,96,128]{2,1,0:T(8,128)S(1)}, f32[96,128]{1,0:T(8,128)S(1)}, f32[8,512]{1,0:T(8,128)S(1)}, f32[8,512]{1,0:T(8,128)S(1)}, /*in...) while((s32[]{:T(128)}, f32[14,96,128]{2,1,0:T(8,128)S(1)}, ...), condition=%wide.region_1.2_spmd.clone, body=%wide.region_0.1_spmd.clone.sunk | while | flops 26626 | bytes 267817 | solution.py:744
  18.9 4.7 %collective-permute-start.3 = (f32[8,128]{1,0:T(8,128)S(1)}, f32[8,128]{1,0:T(8,128)S(1)}, u32[]{:S(2)}, u32[]{:S(2)}) collective-permute-start(f32[8,128]{1,0:T(8,128)S(1)} %get-tuple-element.1158), channel_id=1, source_target_pairs={{16,32},{32,16},{48,64},{64,48},{80,96},{96,80},{112,128},{128,112... | collective-permute-start | bytes 12296 | tf_op jit(solution)/shard_map/while/body/eval_jaxpr/ppermute | solution.py:618
  28.0 8.9 %collective-permute-start = (f32[8,128]{1,0:T(8,128)S(1)}, f32[8,128]{1,0:T(8,128)S(1)}, u32[]{:S(2)}, u32[]{:S(2)}) collective-permute-start(f32[8,128]{1,0:T(8,128)S(1)} %get-tuple-element.1158), channel_id=1, source_target_pairs={{0,1},{1,0},{2,3},{3,2},{7,6},{6,7},{5,4},{4,5},{8,9},{9,8},{10,11... | collective-permute-start | bytes 12296 | tf_op jit(solution)/shard_map/while/body/eval_jaxpr/ppermute | solution.py:618
  45.0 10.1 %collective-permute-start = (f32[8,128]{1,0:T(8,128)S(1)}, f32[8,128]{1,0:T(8,128)S(1)}, u32[]{:S(2)}, u32[]{:S(2)}) collective-permute-start(f32[8,128]{1,0:T(8,128)S(1)} %get-tuple-element.1158), channel_id=1, source_target_pairs={{0,1},{1,0},{2,3},{3,2},{7,6},{6,7},{5,4},{4,5},{8,9},{9,8},{10,11... | collective-permute-start | bytes 12296 | tf_op jit(solution)/shard_map/while/body/eval_jaxpr/ppermute | solution.py:618
  55.0 4.2 %collective-permute-start.3 = (f32[8,128]{1,0:T(8,128)S(1)}, f32[8,128]{1,0:T(8,128)S(1)}, u32[]{:S(2)}, u32[]{:S(2)}) collective-permute-start(f32[8,128]{1,0:T(8,128)S(1)} %get-tuple-element.1158), channel_id=1, source_target_pairs={{16,32},{32,16},{48,64},{64,48},{80,96},{96,80},{112,128},{128,112... | collective-permute-start | bytes 12296 | tf_op jit(solution)/shard_map/while/body/eval_jaxpr/ppermute | solution.py:618
  63.6 5.8 %collective-permute-start = (f32[8,128]{1,0:T(8,128)S(1)}, f32[8,128]{1,0:T(8,128)S(1)}, u32[]{:S(2)}, u32[]{:S(2)}) collective-permute-start(f32[8,128]{1,0:T(8,128)S(1)} %get-tuple-element.1158), channel_id=1, source_target_pairs={{0,1},{1,0},{2,3},{3,2},{7,6},{6,7},{5,4},{4,5},{8,9},{9,8},{10,11... | collective-permute-start | bytes 12296 | tf_op jit(solution)/shard_map/while/body/eval_jaxpr/ppermute | solution.py:618
  77.5 4.1 %collective-permute-start = (f32[8,128]{1,0:T(8,128)S(1)}, f32[8,128]{1,0:T(8,128)S(1)}, u32[]{:S(2)}, u32[]{:S(2)}) collective-permute-start(f32[8,128]{1,0:T(8,128)S(1)} %get-tuple-element.1158), channel_id=1, source_target_pairs={{0,1},{1,0},{2,3},{3,2},{7,6},{6,7},{5,4},{4,5},{8,9},{9,8},{10,11... | collective-permute-start | bytes 12296 | tf_op jit(solution)/shard_map/while/body/eval_jaxpr/ppermute | solution.py:618
  81.6 4.5 %collective-permute-start.3 = (f32[8,128]{1,0:T(8,128)S(1)}, f32[8,128]{1,0:T(8,128)S(1)}, u32[]{:S(2)}, u32[]{:S(2)}) collective-permute-start(f32[8,128]{1,0:T(8,128)S(1)} %get-tuple-element.1158), channel_id=1, source_target_pairs={{16,32},{32,16},{48,64},{64,48},{80,96},{96,80},{112,128},{128,112... | collective-permute-start | bytes 12296 | tf_op jit(solution)/shard_map/while/body/eval_jaxpr/ppermute | solution.py:618
  90.5 6.3 %collective-permute-start = (f32[8,128]{1,0:T(8,128)S(1)}, f32[8,128]{1,0:T(8,128)S(1)}, u32[]{:S(2)}, u32[]{:S(2)}) collective-permute-start(f32[8,128]{1,0:T(8,128)S(1)} %get-tuple-element.1158), channel_id=1, source_target_pairs={{0,1},{1,0},{2,3},{3,2},{7,6},{6,7},{5,4},{4,5},{8,9},{9,8},{10,11... | collective-permute-start | bytes 12296 | tf_op jit(solution)/shard_map/while/body/eval_jaxpr/ppermute | solution.py:618
  96.8 4.1 %collective-permute-start.3 = (f32[8,128]{1,0:T(8,128)S(1)}, f32[8,128]{1,0:T(8,128)S(1)}, u32[]{:S(2)}, u32[]{:S(2)}) collective-permute-start(f32[8,128]{1,0:T(8,128)S(1)} %get-tuple-element.1158), channel_id=1, source_target_pairs={{16,32},{32,16},{48,64},{64,48},{80,96},{96,80},{112,128},{128,112... | collective-permute-start | bytes 12296 | tf_op jit(solution)/shard_map/while/body/eval_jaxpr/ppermute | solution.py:618
  105.3 5.4 %collective-permute-start = (f32[8,128]{1,0:T(8,128)S(1)}, f32[8,128]{1,0:T(8,128)S(1)}, u32[]{:S(2)}, u32[]{:S(2)}) collective-permute-start(f32[8,128]{1,0:T(8,128)S(1)} %get-tuple-element.1158), channel_id=1, source_target_pairs={{0,1},{1,0},{2,3},{3,2},{7,6},{6,7},{5,4},{4,5},{8,9},{9,8},{10,11... | collective-permute-start | bytes 12296 | tf_op jit(solution)/shard_map/while/body/eval_jaxpr/ppermute | solution.py:618
  110.6 4.2 %collective-permute-start.3 = (f32[8,128]{1,0:T(8,128)S(1)}, f32[8,128]{1,0:T(8,128)S(1)}, u32[]{:S(2)}, u32[]{:S(2)}) collective-permute-start(f32[8,128]{1,0:T(8,128)S(1)} %get-tuple-element.1158), channel_id=1, source_target_pairs={{16,32},{32,16},{48,64},{64,48},{80,96},{96,80},{112,128},{128,112... | collective-permute-start | bytes 12296 | tf_op jit(solution)/shard_map/while/body/eval_jaxpr/ppermute | solution.py:618
  119.1 5.4 %collective-permute-start = (f32[8,128]{1,0:T(8,128)S(1)}, f32[8,128]{1,0:T(8,128)S(1)}, u32[]{:S(2)}, u32[]{:S(2)}) collective-permute-start(f32[8,128]{1,0:T(8,128)S(1)} %get-tuple-element.1158), channel_id=1, source_target_pairs={{0,1},{1,0},{2,3},{3,2},{7,6},{6,7},{5,4},{4,5},{8,9},{9,8},{10,11... | collective-permute-start | bytes 12296 | tf_op jit(solution)/shard_map/while/body/eval_jaxpr/ppermute | solution.py:618
  132.9 5.4 %collective-permute-start = (f32[8,128]{1,0:T(8,128)S(1)}, f32[8,128]{1,0:T(8,128)S(1)}, u32[]{:S(2)}, u32[]{:S(2)}) collective-permute-start(f32[8,128]{1,0:T(8,128)S(1)} %get-tuple-element.1158), channel_id=1, source_target_pairs={{0,1},{1,0},{2,3},{3,2},{7,6},{6,7},{5,4},{4,5},{8,9},{9,8},{10,11... | collective-permute-start | bytes 12296 | tf_op jit(solution)/shard_map/while/body/eval_jaxpr/ppermute | solution.py:618
  138.3 4.2 %collective-permute-start.3 = (f32[8,128]{1,0:T(8,128)S(1)}, f32[8,128]{1,0:T(8,128)S(1)}, u32[]{:S(2)}, u32[]{:S(2)}) collective-permute-start(f32[8,128]{1,0:T(8,128)S(1)} %get-tuple-element.1158), channel_id=1, source_target_pairs={{16,32},{32,16},{48,64},{64,48},{80,96},{96,80},{112,128},{128,112... | collective-permute-start | bytes 12296 | tf_op jit(solution)/shard_map/while/body/eval_jaxpr/ppermute | solution.py:618
  146.8 5.4 %collective-permute-start = (f32[8,128]{1,0:T(8,128)S(1)}, f32[8,128]{1,0:T(8,128)S(1)}, u32[]{:S(2)}, u32[]{:S(2)}) collective-permute-start(f32[8,128]{1,0:T(8,128)S(1)} %get-tuple-element.1158), channel_id=1, source_target_pairs={{0,1},{1,0},{2,3},{3,2},{7,6},{6,7},{5,4},{4,5},{8,9},{9,8},{10,11... | collective-permute-start | bytes 12296 | tf_op jit(solution)/shard_map/while/body/eval_jaxpr/ppermute | solution.py:618
  160.6 5.4 %collective-permute-start = (f32[8,128]{1,0:T(8,128)S(1)}, f32[8,128]{1,0:T(8,128)S(1)}, u32[]{:S(2)}, u32[]{:S(2)}) collective-permute-start(f32[8,128]{1,0:T(8,128)S(1)} %get-tuple-element.1158), channel_id=1, source_target_pairs={{0,1},{1,0},{2,3},{3,2},{7,6},{6,7},{5,4},{4,5},{8,9},{9,8},{10,11... | collective-permute-start | bytes 12296 | tf_op jit(solution)/shard_map/while/body/eval_jaxpr/ppermute | solution.py:618
  166.0 4.2 %collective-permute-start.3 = (f32[8,128]{1,0:T(8,128)S(1)}, f32[8,128]{1,0:T(8,128)S(1)}, u32[]{:S(2)}, u32[]{:S(2)}) collective-permute-start(f32[8,128]{1,0:T(8,128)S(1)} %get-tuple-element.1158), channel_id=1, source_target_pairs={{16,32},{32,16},{48,64},{64,48},{80,96},{96,80},{112,128},{128,112... | collective-permute-start | bytes 12296 | tf_op jit(solution)/shard_map/while/body/eval_jaxpr/ppermute | solution.py:618
  174.5 5.4 %collective-permute-start = (f32[8,128]{1,0:T(8,128)S(1)}, f32[8,128]{1,0:T(8,128)S(1)}, u32[]{:S(2)}, u32[]{:S(2)}) collective-permute-start(f32[8,128]{1,0:T(8,128)S(1)} %get-tuple-element.1158), channel_id=1, source_target_pairs={{0,1},{1,0},{2,3},{3,2},{7,6},{6,7},{5,4},{4,5},{8,9},{9,8},{10,11... | collective-permute-start | bytes 12296 | tf_op jit(solution)/shard_map/while/body/eval_jaxpr/ppermute | solution.py:618
  188.3 5.4 %collective-permute-start = (f32[8,128]{1,0:T(8,128)S(1)}, f32[8,128]{1,0:T(8,128)S(1)}, u32[]{:S(2)}, u32[]{:S(2)}) collective-permute-start(f32[8,128]{1,0:T(8,128)S(1)} %get-tuple-element.1158), channel_id=1, source_target_pairs={{0,1},{1,0},{2,3},{3,2},{7,6},{6,7},{5,4},{4,5},{8,9},{9,8},{10,11... | collective-permute-start | bytes 12296 | tf_op jit(solution)/shard_map/while/body/eval_jaxpr/ppermute | solution.py:618
  193.7 4.2 %collective-permute-start.3 = (f32[8,128]{1,0:T(8,128)S(1)}, f32[8,128]{1,0:T(8,128)S(1)}, u32[]{:S(2)}, u32[]{:S(2)}) collective-permute-start(f32[8,128]{1,0:T(8,128)S(1)} %get-tuple-element.1158), channel_id=1, source_target_pairs={{16,32},{32,16},{48,64},{64,48},{80,96},{96,80},{112,128},{128,112... | collective-permute-start | bytes 12296 | tf_op jit(solution)/shard_map/while/body/eval_jaxpr/ppermute | solution.py:618
  202.2 5.4 %collective-permute-start = (f32[8,128]{1,0:T(8,128)S(1)}, f32[8,128]{1,0:T(8,128)S(1)}, u32[]{:S(2)}, u32[]{:S(2)}) collective-permute-start(f32[8,128]{1,0:T(8,128)S(1)} %get-tuple-element.1158), channel_id=1, source_target_pairs={{0,1},{1,0},{2,3},{3,2},{7,6},{6,7},{5,4},{4,5},{8,9},{9,8},{10,11... | collective-permute-start | bytes 12296 | tf_op jit(solution)/shard_map/while/body/eval_jaxpr/ppermute | solution.py:618
  222.3 7.6 %collective-permute-start.9 = (f32[8,128]{1,0:T(8,128)S(1)}, f32[8,128]{1,0:T(8,128)S(1)}, u32[]{:S(2)}, u32[]{:S(2)}) collective-permute-start(f32[8,128]{1,0:T(8,128)S(1)} %get-tuple-element.802), channel_id=1, source_target_pairs={{0,1},{1,0},{2,3},{3,2},{7,6},{6,7},{5,4},{4,5},{8,9},{9,8},{10,11... | collective-permute-start | bytes 12296 | tf_op jit(solution)/shard_map/ppermute | solution.py:618
  232.7 23.2 %all_to_all.5.pieces = bf16[16,96,128]{2,1,0:T(8,128)(2,1)S(1)} all-to-all(bf16[16,96,128]{2,1,0:T(8,128)(2,1)S(1)} %shard_map.115), channel_id=1, replica_groups=mesh['grp'=32,'dom'=16] {'dom'}, dimensions={0} | all-to-all | bytes 786432 | tf_op jit(solution)/shard_map/all_to_all | solution.py:762
  (248 shorter events, 112.2 us)
Async XLA Ops:
  1.7 10.6 %collective-permute-start.8 = (f32[8,128]{1,0:T(8,128)S(1)}, f32[8,128]{1,0:T(8,128)S(1)}, u32[]{:S(2)}, u32[]{:S(2)}) collective-permute-start(f32[8,128]{1,0:T(8,128)S(1)} %get-tuple-element.776), channel_id=1, source_target_pairs={{0,16},{1,17},{2,18},{3,19},{4,23},{5,22},{6,21},{7,20},{8,24},{9,... | collective-permute-start | bytes 12296 | tf_op jit(solution)/shard_map/ppermute | solution.py:668
  3.6 8.7 %collective-permute-start.7 = (f32[8,128]{1,0:T(8,128)S(1)}, f32[8,128]{1,0:T(8,128)S(1)}, u32[]{:S(2)}, u32[]{:S(2)}) collective-permute-start(f32[8,128]{1,0:T(8,128)S(1)} %get-tuple-element.776), channel_id=1, source_target_pairs={{0,1},{1,0},{2,3},{3,2},{4,6},{5,7},{6,4},{7,5},{8,9},{9,8},{10,11... | collective-permute-start | bytes 12296 | tf_op jit(solution)/shard_map/ppermute | solution.py:668
  14.8 12.6 %collective-permute-start = (f32[8,128]{1,0:T(8,128)S(1)}, f32[8,128]{1,0:T(8,128)S(1)}, u32[]{:S(2)}, u32[]{:S(2)}) collective-permute-start(f32[8,128]{1,0:T(8,128)S(1)} %get-tuple-element.1158), channel_id=1, source_target_pairs={{0,1},{1,0},{2,3},{3,2},{7,6},{6,7},{5,4},{4,5},{8,9},{9,8},{10,11... | collective-permute-start | bytes 12296 | tf_op jit(solution)/shard_map/while/body/eval_jaxpr/ppermute | solution.py:618
  18.9 7.4 %collective-permute-start.3 = (f32[8,128]{1,0:T(8,128)S(1)}, f32[8,128]{1,0:T(8,128)S(1)}, u32[]{:S(2)}, u32[]{:S(2)}) collective-permute-start(f32[8,128]{1,0:T(8,128)S(1)} %get-tuple-element.1158), channel_id=1, source_target_pairs={{16,32},{32,16},{48,64},{64,48},{80,96},{96,80},{112,128},{128,112... | collective-permute-start | bytes 12296 | tf_op jit(solution)/shard_map/while/body/eval_jaxpr/ppermute | solution.py:618
  28.0 16.4 %collective-permute-start = (f32[8,128]{1,0:T(8,128)S(1)}, f32[8,128]{1,0:T(8,128)S(1)}, u32[]{:S(2)}, u32[]{:S(2)}) collective-permute-start(f32[8,128]{1,0:T(8,128)S(1)} %get-tuple-element.1158), channel_id=1, source_target_pairs={{0,1},{1,0},{2,3},{3,2},{7,6},{6,7},{5,4},{4,5},{8,9},{9,8},{10,11... | collective-permute-start | bytes 12296 | tf_op jit(solution)/shard_map/while/body/eval_jaxpr/ppermute | solution.py:618
  36.9 7.0 %collective-permute-start.3 = (f32[8,128]{1,0:T(8,128)S(1)}, f32[8,128]{1,0:T(8,128)S(1)}, u32[]{:S(2)}, u32[]{:S(2)}) collective-permute-start(f32[8,128]{1,0:T(8,128)S(1)} %get-tuple-element.1158), channel_id=1, source_target_pairs={{16,32},{32,16},{48,64},{64,48},{80,96},{96,80},{112,128},{128,112... | collective-permute-start | bytes 12296 | tf_op jit(solution)/shard_map/while/body/eval_jaxpr/ppermute | solution.py:618
  45.0 18.0 %collective-permute-start = (f32[8,128]{1,0:T(8,128)S(1)}, f32[8,128]{1,0:T(8,128)S(1)}, u32[]{:S(2)}, u32[]{:S(2)}) collective-permute-start(f32[8,128]{1,0:T(8,128)S(1)} %get-tuple-element.1158), channel_id=1, source_target_pairs={{0,1},{1,0},{2,3},{3,2},{7,6},{6,7},{5,4},{4,5},{8,9},{9,8},{10,11... | collective-permute-start | bytes 12296 | tf_op jit(solution)/shard_map/while/body/eval_jaxpr/ppermute | solution.py:618
  63.6 13.3 %collective-permute-start = (f32[8,128]{1,0:T(8,128)S(1)}, f32[8,128]{1,0:T(8,128)S(1)}, u32[]{:S(2)}, u32[]{:S(2)}) collective-permute-start(f32[8,128]{1,0:T(8,128)S(1)} %get-tuple-element.1158), channel_id=1, source_target_pairs={{0,1},{1,0},{2,3},{3,2},{7,6},{6,7},{5,4},{4,5},{8,9},{9,8},{10,11... | collective-permute-start | bytes 12296 | tf_op jit(solution)/shard_map/while/body/eval_jaxpr/ppermute | solution.py:618
  69.4 7.0 %collective-permute-start.3 = (f32[8,128]{1,0:T(8,128)S(1)}, f32[8,128]{1,0:T(8,128)S(1)}, u32[]{:S(2)}, u32[]{:S(2)}) collective-permute-start(f32[8,128]{1,0:T(8,128)S(1)} %get-tuple-element.1158), channel_id=1, source_target_pairs={{16,32},{32,16},{48,64},{64,48},{80,96},{96,80},{112,128},{128,112... | collective-permute-start | bytes 12296 | tf_op jit(solution)/shard_map/while/body/eval_jaxpr/ppermute | solution.py:618
  77.5 12.4 %collective-permute-start = (f32[8,128]{1,0:T(8,128)S(1)}, f32[8,128]{1,0:T(8,128)S(1)}, u32[]{:S(2)}, u32[]{:S(2)}) collective-permute-start(f32[8,128]{1,0:T(8,128)S(1)} %get-tuple-element.1158), channel_id=1, source_target_pairs={{0,1},{1,0},{2,3},{3,2},{7,6},{6,7},{5,4},{4,5},{8,9},{9,8},{10,11... | collective-permute-start | bytes 12296 | tf_op jit(solution)/shard_map/while/body/eval_jaxpr/ppermute | solution.py:618
  81.6 7.2 %collective-permute-start.3 = (f32[8,128]{1,0:T(8,128)S(1)}, f32[8,128]{1,0:T(8,128)S(1)}, u32[]{:S(2)}, u32[]{:S(2)}) collective-permute-start(f32[8,128]{1,0:T(8,128)S(1)} %get-tuple-element.1158), channel_id=1, source_target_pairs={{16,32},{32,16},{48,64},{64,48},{80,96},{96,80},{112,128},{128,112... | collective-permute-start | bytes 12296 | tf_op jit(solution)/shard_map/while/body/eval_jaxpr/ppermute | solution.py:618
  90.5 14.1 %collective-permute-start = (f32[8,128]{1,0:T(8,128)S(1)}, f32[8,128]{1,0:T(8,128)S(1)}, u32[]{:S(2)}, u32[]{:S(2)}) collective-permute-start(f32[8,128]{1,0:T(8,128)S(1)} %get-tuple-element.1158), channel_id=1, source_target_pairs={{0,1},{1,0},{2,3},{3,2},{7,6},{6,7},{5,4},{4,5},{8,9},{9,8},{10,11... | collective-permute-start | bytes 12296 | tf_op jit(solution)/shard_map/while/body/eval_jaxpr/ppermute | solution.py:618
  105.3 13.3 %collective-permute-start = (f32[8,128]{1,0:T(8,128)S(1)}, f32[8,128]{1,0:T(8,128)S(1)}, u32[]{:S(2)}, u32[]{:S(2)}) collective-permute-start(f32[8,128]{1,0:T(8,128)S(1)} %get-tuple-element.1158), channel_id=1, source_target_pairs={{0,1},{1,0},{2,3},{3,2},{7,6},{6,7},{5,4},{4,5},{8,9},{9,8},{10,11... | collective-permute-start | bytes 12296 | tf_op jit(solution)/shard_map/while/body/eval_jaxpr/ppermute | solution.py:618
  119.1 13.2 %collective-permute-start = (f32[8,128]{1,0:T(8,128)S(1)}, f32[8,128]{1,0:T(8,128)S(1)}, u32[]{:S(2)}, u32[]{:S(2)}) collective-permute-start(f32[8,128]{1,0:T(8,128)S(1)} %get-tuple-element.1158), channel_id=1, source_target_pairs={{0,1},{1,0},{2,3},{3,2},{7,6},{6,7},{5,4},{4,5},{8,9},{9,8},{10,11... | collective-permute-start | bytes 12296 | tf_op jit(solution)/shard_map/while/body/eval_jaxpr/ppermute | solution.py:618
  132.9 13.3 %collective-permute-start = (f32[8,128]{1,0:T(8,128)S(1)}, f32[8,128]{1,0:T(8,128)S(1)}, u32[]{:S(2)}, u32[]{:S(2)}) collective-permute-start(f32[8,128]{1,0:T(8,128)S(1)} %get-tuple-element.1158), channel_id=1, source_target_pairs={{0,1},{1,0},{2,3},{3,2},{7,6},{6,7},{5,4},{4,5},{8,9},{9,8},{10,11... | collective-permute-start | bytes 12296 | tf_op jit(solution)/shard_map/while/body/eval_jaxpr/ppermute | solution.py:618
  146.8 13.2 %collective-permute-start = (f32[8,128]{1,0:T(8,128)S(1)}, f32[8,128]{1,0:T(8,128)S(1)}, u32[]{:S(2)}, u32[]{:S(2)}) collective-permute-start(f32[8,128]{1,0:T(8,128)S(1)} %get-tuple-element.1158), channel_id=1, source_target_pairs={{0,1},{1,0},{2,3},{3,2},{7,6},{6,7},{5,4},{4,5},{8,9},{9,8},{10,11... | collective-permute-start | bytes 12296 | tf_op jit(solution)/shard_map/while/body/eval_jaxpr/ppermute | solution.py:618
  160.6 13.3 %collective-permute-start = (f32[8,128]{1,0:T(8,128)S(1)}, f32[8,128]{1,0:T(8,128)S(1)}, u32[]{:S(2)}, u32[]{:S(2)}) collective-permute-start(f32[8,128]{1,0:T(8,128)S(1)} %get-tuple-element.1158), channel_id=1, source_target_pairs={{0,1},{1,0},{2,3},{3,2},{7,6},{6,7},{5,4},{4,5},{8,9},{9,8},{10,11... | collective-permute-start | bytes 12296 | tf_op jit(solution)/shard_map/while/body/eval_jaxpr/ppermute | solution.py:618
  174.5 13.2 %collective-permute-start = (f32[8,128]{1,0:T(8,128)S(1)}, f32[8,128]{1,0:T(8,128)S(1)}, u32[]{:S(2)}, u32[]{:S(2)}) collective-permute-start(f32[8,128]{1,0:T(8,128)S(1)} %get-tuple-element.1158), channel_id=1, source_target_pairs={{0,1},{1,0},{2,3},{3,2},{7,6},{6,7},{5,4},{4,5},{8,9},{9,8},{10,11... | collective-permute-start | bytes 12296 | tf_op jit(solution)/shard_map/while/body/eval_jaxpr/ppermute | solution.py:618
  188.3 13.3 %collective-permute-start = (f32[8,128]{1,0:T(8,128)S(1)}, f32[8,128]{1,0:T(8,128)S(1)}, u32[]{:S(2)}, u32[]{:S(2)}) collective-permute-start(f32[8,128]{1,0:T(8,128)S(1)} %get-tuple-element.1158), channel_id=1, source_target_pairs={{0,1},{1,0},{2,3},{3,2},{7,6},{6,7},{5,4},{4,5},{8,9},{9,8},{10,11... | collective-permute-start | bytes 12296 | tf_op jit(solution)/shard_map/while/body/eval_jaxpr/ppermute | solution.py:618
  202.2 13.2 %collective-permute-start = (f32[8,128]{1,0:T(8,128)S(1)}, f32[8,128]{1,0:T(8,128)S(1)}, u32[]{:S(2)}, u32[]{:S(2)}) collective-permute-start(f32[8,128]{1,0:T(8,128)S(1)} %get-tuple-element.1158), channel_id=1, source_target_pairs={{0,1},{1,0},{2,3},{3,2},{7,6},{6,7},{5,4},{4,5},{8,9},{9,8},{10,11... | collective-permute-start | bytes 12296 | tf_op jit(solution)/shard_map/while/body/eval_jaxpr/ppermute | solution.py:618
  216.0 15.2 %collective-permute-start.12 = (f32[8,128]{1,0:T(8,128)S(1)}, f32[8,128]{1,0:T(8,128)S(1)}, u32[]{:S(2)}, u32[]{:S(2)}) collective-permute-start(f32[8,128]{1,0:T(8,128)S(1)} %get-tuple-element.802), channel_id=1, source_target_pairs={{16,32},{32,16},{48,64},{64,48},{80,96},{96,80},{112,128},{128,112... | collective-permute-start | bytes 12296 | tf_op jit(solution)/shard_map/ppermute | solution.py:618
  219.7 11.4 %collective-permute-start.11 = (f32[8,128]{1,0:T(8,128)S(1)}, f32[8,128]{1,0:T(8,128)S(1)}, u32[]{:S(2)}, u32[]{:S(2)}) collective-permute-start(f32[8,128]{1,0:T(8,128)S(1)} %get-tuple-element.802), channel_id=1, source_target_pairs={{1,2},{2,1},{3,7},{7,3},{6,5},{5,6},{4,8},{8,4},{9,10},{10,9},{11,... | collective-permute-start | bytes 12296 | tf_op jit(solution)/shard_map/ppermute | solution.py:618
  220.4 11.7 %collective-permute-start.10 = (f32[8,128]{1,0:T(8,128)S(1)}, f32[8,128]{1,0:T(8,128)S(1)}, u32[]{:S(2)}, u32[]{:S(2)}) collective-permute-start(f32[8,128]{1,0:T(8,128)S(1)} %get-tuple-element.802), channel_id=1, source_target_pairs={{0,16},{16,0},{32,48},{48,32},{64,80},{80,64},{96,112},{112,96},{1... | collective-permute-start | bytes 12296 | tf_op jit(solution)/shard_map/ppermute | solution.py:618
  222.3 9.8 %collective-permute-start.9 = (f32[8,128]{1,0:T(8,128)S(1)}, f32[8,128]{1,0:T(8,128)S(1)}, u32[]{:S(2)}, u32[]{:S(2)}) collective-permute-start(f32[8,128]{1,0:T(8,128)S(1)} %get-tuple-element.802), channel_id=1, source_target_pairs={{0,1},{1,0},{2,3},{3,2},{7,6},{6,7},{5,4},{4,5},{8,9},{9,8},{10,11... | collective-permute-start | bytes 12296 | tf_op jit(solution)/shard_map/ppermute | solution.py:618
  (41 other events, 170.0 us)

commit v5 on v4

--- a/solution.py
+++ b/solution.py
@@ -19,7 +19,8 @@
 
 DOM_ROW = 4
 
-EXCHANGES = ("dom1", "grp1", "dom0", "grp0")
+EXCHANGES = ("grp1", "dom1", "dom0", "grp0")
+HANDED = ("dom1", "grp1", "dom0", "grp0")
 
 VMEM = pl.BlockSpec(memory_space=pltpu.VMEM)
 HBM = pl.BlockSpec(memory_space=pltpu.MemorySpace.HBM)
@@ -370,9 +371,9 @@
         ]
         columns.append(jnp.concatenate(mapped, axis=0))
     node_forces = contract(wide_force, columns, 3 * POINTS)
-    parts = parts_of(jnp.concatenate(node_rows(node_forces), axis=1))
+    parts = parts_of(jnp.concatenate(node_rows(node_forces), axis=1))[:2]
     sums = matmul(jnp.concatenate(parts, axis=0).astype(jnp.bfloat16), faces[...])
-    return node_forces, (sums[16:24] + sums[8:16]) + sums[0:8]
+    return node_forces, sums[8:16] + sums[0:8]
 
 
 def node_rows(node_forces):
@@ -607,7 +608,7 @@
     source = 2 * (face // 2) + jnp.bitwise_xor(parity, 1 - face % 2)
 
     def exchange(send):
-        received = []
+        received = {}
         for name in EXCHANGES:
             axis, offset = name[:3], int(name[3])
             count = lax.axis_size(axis)
@@ -615,8 +616,8 @@
             for i in range(offset, count - 1, 2):
                 first, second = snake(axis, i), snake(axis, i + 1)
                 pairs += [(first, second), (second, first)]
-            received.append(lax.ppermute(send, axis, pairs))
-        return received
+            received[name] = lax.ppermute(send, axis, pairs)
+        return [received[name] for name in HANDED]
 
     i32, bf16 = jnp.int32, jnp.bfloat16
     rank_rows = point_rank.reshape(POINTS, LANES)
@@ -653,7 +654,7 @@
     )(*(pltpu.with_memory_space_constraint(x, pltpu.MemorySpace.HBM) for x in arguments))
     writers = lax.axis_size("dom")
     packed = lax.ppermute(packed, "dom", [(i, snake("dom", i)) for i in range(writers)])
-    received = []
+    received = {}
     for name in EXCHANGES:
         axis, offset = name[:3], int(name[3])
         pairs = []
@@ -665,8 +666,9 @@
                     to_g, to_w = (other, w) if axis == "grp" else (g, other)
                     target = to_g * writers + snake("dom", to_w)
                     pairs.append((g * writers + w, target))
-        received.append(lax.ppermute(send, ("grp", "dom"), pairs))
-
+        received[name] = lax.ppermute(send, ("grp", "dom"), pairs)
+
+    received = [received[name] for name in HANDED]
     prepare = kernel_call(
         prepare_kernel,
         [

time: 259 us -> 258 us (level)
  the two profiles are of different devices: /device:TPU:256 before, /device:TPU:200 now
where the time goes in v5:
time: 258 us; the launch traced here: 256 us
  starting transfers between devices  207 us (80%)
  blocking collectives  21.9 us (8%)
  Pallas kernels  20.5 us (8%)
  waiting for transfers between devices  4.41 us (2%)
    ppermute x60, starting transfers between devices, exchange(): received[name] = lax.ppermute(send, axis, pairs)  198 us
    all_to_all x1, blocking collectives, shards(): lax.all_to_all(ordered, 'dom', split_axis=0, concat_axis=0, tiled=True)  21.9 us
    ppermute x4, starting transfers between devices, shards(): received[name] = lax.ppermute(send, ('grp', 'dom'), pairs)  8.16 us
    pallas_call x15, Pallas kernels, advance(): kernel_call(step_kernel, [strain_t] + ([] if last else [forces_t, lanes_t...  7.84 us
    pallas_call x15, Pallas kernels, advance(): side(wave, dom1, grp1, *late, source, inverse_index, connect_rows, incide...  6.55 us
  transfers between devices with their start and end apart: 65, of which 14 were waited for; matrix products, arithmetic and copies ran while one was open for 0% of the time, Pallas kernels for 4%

profile of v5, /device:TPU:200, one launch (start us, length us, event | category | flops | bytes accessed | tf_op | source)
XLA Modules:
  0.0 256.2 jit_solution(8235808558594368827)
XLA Ops:
  12.8 203.6 %while.34 = (s32[]{:T(128)}, f32[14,96,128]{2,1,0:T(8,128)S(1)}, f32[96,128]{1,0:T(8,128)S(1)}, f32[8,512]{1,0:T(8,128)S(1)}, f32[8,512]{1,0:T(8,128)S(1)}, /*in...) while((s32[]{:T(128)}, f32[14,96,128]{2,1,0:T(8,128)S(1)}, ...), condition=%wide.region_1.2_spmd.clone, body=%wide.region_0.1_spmd.clone.sunk | while | flops 26626 | bytes 267817 | solution.py:746
  12.8 5.8 %collective-permute-start = (f32[8,128]{1,0:T(8,128)S(1)}, f32[8,128]{1,0:T(8,128)S(1)}, u32[]{:S(2)}, u32[]{:S(2)}) collective-permute-start(f32[8,128]{1,0:T(8,128)S(1)} %get-tuple-element.1158), channel_id=1, source_target_pairs={{0,1},{1,0},{2,3},{3,2},{7,6},{6,7},{5,4},{4,5},{8,9},{9,8},{10,11... | collective-permute-start | bytes 12296 | tf_op jit(solution)/shard_map/while/body/eval_jaxpr/ppermute | solution.py:619
  22.1 4.8 %collective-permute-start.1 = (f32[8,128]{1,0:T(8,128)S(1)}, f32[8,128]{1,0:T(8,128)S(1)}, u32[]{:S(2)}, u32[]{:S(2)}) collective-permute-start(f32[8,128]{1,0:T(8,128)S(1)} %get-tuple-element.1158), channel_id=1, source_target_pairs={{0,16},{16,0},{32,48},{48,32},{64,80},{80,64},{96,112},{112,96},{1... | collective-permute-start | bytes 12296 | tf_op jit(solution)/shard_map/while/body/eval_jaxpr/ppermute | solution.py:619
  28.3 9.4 %collective-permute-start = (f32[8,128]{1,0:T(8,128)S(1)}, f32[8,128]{1,0:T(8,128)S(1)}, u32[]{:S(2)}, u32[]{:S(2)}) collective-permute-start(f32[8,128]{1,0:T(8,128)S(1)} %get-tuple-element.1158), channel_id=1, source_target_pairs={{0,1},{1,0},{2,3},{3,2},{7,6},{6,7},{5,4},{4,5},{8,9},{9,8},{10,11... | collective-permute-start | bytes 12296 | tf_op jit(solution)/shard_map/while/body/eval_jaxpr/ppermute | solution.py:619
  40.3 4.6 %collective-permute-start.1 = (f32[8,128]{1,0:T(8,128)S(1)}, f32[8,128]{1,0:T(8,128)S(1)}, u32[]{:S(2)}, u32[]{:S(2)}) collective-permute-start(f32[8,128]{1,0:T(8,128)S(1)} %get-tuple-element.1158), channel_id=1, source_target_pairs={{0,16},{16,0},{32,48},{48,32},{64,80},{80,64},{96,112},{112,96},{1... | collective-permute-start | bytes 12296 | tf_op jit(solution)/shard_map/while/body/eval_jaxpr/ppermute | solution.py:619
  46.2 10.6 %collective-permute-start = (f32[8,128]{1,0:T(8,128)S(1)}, f32[8,128]{1,0:T(8,128)S(1)}, u32[]{:S(2)}, u32[]{:S(2)}) collective-permute-start(f32[8,128]{1,0:T(8,128)S(1)} %get-tuple-element.1158), channel_id=1, source_target_pairs={{0,1},{1,0},{2,3},{3,2},{7,6},{6,7},{5,4},{4,5},{8,9},{9,8},{10,11... | collective-permute-start | bytes 12296 | tf_op jit(solution)/shard_map/while/body/eval_jaxpr/ppermute | solution.py:619
  64.3 5.2 %collective-permute-start = (f32[8,128]{1,0:T(8,128)S(1)}, f32[8,128]{1,0:T(8,128)S(1)}, u32[]{:S(2)}, u32[]{:S(2)}) collective-permute-start(f32[8,128]{1,0:T(8,128)S(1)} %get-tuple-element.1158), channel_id=1, source_target_pairs={{0,1},{1,0},{2,3},{3,2},{7,6},{6,7},{5,4},{4,5},{8,9},{9,8},{10,11... | collective-permute-start | bytes 12296 | tf_op jit(solution)/shard_map/while/body/eval_jaxpr/ppermute | solution.py:619
  72.6 4.6 %collective-permute-start.1 = (f32[8,128]{1,0:T(8,128)S(1)}, f32[8,128]{1,0:T(8,128)S(1)}, u32[]{:S(2)}, u32[]{:S(2)}) collective-permute-start(f32[8,128]{1,0:T(8,128)S(1)} %get-tuple-element.1158), channel_id=1, source_target_pairs={{0,16},{16,0},{32,48},{48,32},{64,80},{80,64},{96,112},{112,96},{1... | collective-permute-start | bytes 12296 | tf_op jit(solution)/shard_map/while/body/eval_jaxpr/ppermute | solution.py:619
  78.7 5.0 %collective-permute-start = (f32[8,128]{1,0:T(8,128)S(1)}, f32[8,128]{1,0:T(8,128)S(1)}, u32[]{:S(2)}, u32[]{:S(2)}) collective-permute-start(f32[8,128]{1,0:T(8,128)S(1)} %get-tuple-element.1158), channel_id=1, source_target_pairs={{0,1},{1,0},{2,3},{3,2},{7,6},{6,7},{5,4},{4,5},{8,9},{9,8},{10,11... | collective-permute-start | bytes 12296 | tf_op jit(solution)/shard_map/while/body/eval_jaxpr/ppermute | solution.py:619
  90.8 7.5 %collective-permute-start = (f32[8,128]{1,0:T(8,128)S(1)}, f32[8,128]{1,0:T(8,128)S(1)}, u32[]{:S(2)}, u32[]{:S(2)}) collective-permute-start(f32[8,128]{1,0:T(8,128)S(1)} %get-tuple-element.1158), channel_id=1, source_target_pairs={{0,1},{1,0},{2,3},{3,2},{7,6},{6,7},{5,4},{4,5},{8,9},{9,8},{10,11... | collective-permute-start | bytes 12296 | tf_op jit(solution)/shard_map/while/body/eval_jaxpr/ppermute | solution.py:619
  101.0 3.6 %collective-permute-start.1 = (f32[8,128]{1,0:T(8,128)S(1)}, f32[8,128]{1,0:T(8,128)S(1)}, u32[]{:S(2)}, u32[]{:S(2)}) collective-permute-start(f32[8,128]{1,0:T(8,128)S(1)} %get-tuple-element.1158), channel_id=1, source_target_pairs={{0,16},{16,0},{32,48},{48,32},{64,80},{80,64},{96,112},{112,96},{1... | collective-permute-start | bytes 12296 | tf_op jit(solution)/shard_map/while/body/eval_jaxpr/ppermute | solution.py:619
  106.0 6.2 %collective-permute-start = (f32[8,128]{1,0:T(8,128)S(1)}, f32[8,128]{1,0:T(8,128)S(1)}, u32[]{:S(2)}, u32[]{:S(2)}) collective-permute-start(f32[8,128]{1,0:T(8,128)S(1)} %get-tuple-element.1158), channel_id=1, source_target_pairs={{0,1},{1,0},{2,3},{3,2},{7,6},{6,7},{5,4},{4,5},{8,9},{9,8},{10,11... | collective-permute-start | bytes 12296 | tf_op jit(solution)/shard_map/while/body/eval_jaxpr/ppermute | solution.py:619
  119.7 6.2 %collective-permute-start = (f32[8,128]{1,0:T(8,128)S(1)}, f32[8,128]{1,0:T(8,128)S(1)}, u32[]{:S(2)}, u32[]{:S(2)}) collective-permute-start(f32[8,128]{1,0:T(8,128)S(1)} %get-tuple-element.1158), channel_id=1, source_target_pairs={{0,1},{1,0},{2,3},{3,2},{7,6},{6,7},{5,4},{4,5},{8,9},{9,8},{10,11... | collective-permute-start | bytes 12296 | tf_op jit(solution)/shard_map/while/body/eval_jaxpr/ppermute | solution.py:619
  128.6 3.6 %collective-permute-start.1 = (f32[8,128]{1,0:T(8,128)S(1)}, f32[8,128]{1,0:T(8,128)S(1)}, u32[]{:S(2)}, u32[]{:S(2)}) collective-permute-start(f32[8,128]{1,0:T(8,128)S(1)} %get-tuple-element.1158), channel_id=1, source_target_pairs={{0,16},{16,0},{32,48},{48,32},{64,80},{80,64},{96,112},{112,96},{1... | collective-permute-start | bytes 12296 | tf_op jit(solution)/shard_map/while/body/eval_jaxpr/ppermute | solution.py:619
  133.5 6.2 %collective-permute-start = (f32[8,128]{1,0:T(8,128)S(1)}, f32[8,128]{1,0:T(8,128)S(1)}, u32[]{:S(2)}, u32[]{:S(2)}) collective-permute-start(f32[8,128]{1,0:T(8,128)S(1)} %get-tuple-element.1158), channel_id=1, source_target_pairs={{0,1},{1,0},{2,3},{3,2},{7,6},{6,7},{5,4},{4,5},{8,9},{9,8},{10,11... | collective-permute-start | bytes 12296 | tf_op jit(solution)/shard_map/while/body/eval_jaxpr/ppermute | solution.py:619
  147.3 6.2 %collective-permute-start = (f32[8,128]{1,0:T(8,128)S(1)}, f32[8,128]{1,0:T(8,128)S(1)}, u32[]{:S(2)}, u32[]{:S(2)}) collective-permute-start(f32[8,128]{1,0:T(8,128)S(1)} %get-tuple-element.1158), channel_id=1, source_target_pairs={{0,1},{1,0},{2,3},{3,2},{7,6},{6,7},{5,4},{4,5},{8,9},{9,8},{10,11... | collective-permute-start | bytes 12296 | tf_op jit(solution)/shard_map/while/body/eval_jaxpr/ppermute | solution.py:619
  161.1 6.2 %collective-permute-start = (f32[8,128]{1,0:T(8,128)S(1)}, f32[8,128]{1,0:T(8,128)S(1)}, u32[]{:S(2)}, u32[]{:S(2)}) collective-permute-start(f32[8,128]{1,0:T(8,128)S(1)} %get-tuple-element.1158), channel_id=1, source_target_pairs={{0,1},{1,0},{2,3},{3,2},{7,6},{6,7},{5,4},{4,5},{8,9},{9,8},{10,11... | collective-permute-start | bytes 12296 | tf_op jit(solution)/shard_map/while/body/eval_jaxpr/ppermute | solution.py:619
  174.9 6.2 %collective-permute-start = (f32[8,128]{1,0:T(8,128)S(1)}, f32[8,128]{1,0:T(8,128)S(1)}, u32[]{:S(2)}, u32[]{:S(2)}) collective-permute-start(f32[8,128]{1,0:T(8,128)S(1)} %get-tuple-element.1158), channel_id=1, source_target_pairs={{0,1},{1,0},{2,3},{3,2},{7,6},{6,7},{5,4},{4,5},{8,9},{9,8},{10,11... | collective-permute-start | bytes 12296 | tf_op jit(solution)/shard_map/while/body/eval_jaxpr/ppermute | solution.py:619
  188.7 6.2 %collective-permute-start = (f32[8,128]{1,0:T(8,128)S(1)}, f32[8,128]{1,0:T(8,128)S(1)}, u32[]{:S(2)}, u32[]{:S(2)}) collective-permute-start(f32[8,128]{1,0:T(8,128)S(1)} %get-tuple-element.1158), channel_id=1, source_target_pairs={{0,1},{1,0},{2,3},{3,2},{7,6},{6,7},{5,4},{4,5},{8,9},{9,8},{10,11... | collective-permute-start | bytes 12296 | tf_op jit(solution)/shard_map/while/body/eval_jaxpr/ppermute | solution.py:619
  202.5 6.2 %collective-permute-start = (f32[8,128]{1,0:T(8,128)S(1)}, f32[8,128]{1,0:T(8,128)S(1)}, u32[]{:S(2)}, u32[]{:S(2)}) collective-permute-start(f32[8,128]{1,0:T(8,128)S(1)} %get-tuple-element.1158), channel_id=1, source_target_pairs={{0,1},{1,0},{2,3},{3,2},{7,6},{6,7},{5,4},{4,5},{8,9},{9,8},{10,11... | collective-permute-start | bytes 12296 | tf_op jit(solution)/shard_map/while/body/eval_jaxpr/ppermute | solution.py:619
  211.3 3.6 %collective-permute-start.1 = (f32[8,128]{1,0:T(8,128)S(1)}, f32[8,128]{1,0:T(8,128)S(1)}, u32[]{:S(2)}, u32[]{:S(2)}) collective-permute-start(f32[8,128]{1,0:T(8,128)S(1)} %get-tuple-element.1158), channel_id=1, source_target_pairs={{0,16},{16,0},{32,48},{48,32},{64,80},{80,64},{96,112},{112,96},{1... | collective-permute-start | bytes 12296 | tf_op jit(solution)/shard_map/while/body/eval_jaxpr/ppermute | solution.py:619
  219.3 4.1 %collective-permute-start.10 = (f32[8,128]{1,0:T(8,128)S(1)}, f32[8,128]{1,0:T(8,128)S(1)}, u32[]{:S(2)}, u32[]{:S(2)}) collective-permute-start(f32[8,128]{1,0:T(8,128)S(1)} %get-tuple-element.802), channel_id=1, source_target_pairs={{0,16},{16,0},{32,48},{48,32},{64,80},{80,64},{96,112},{112,96},{1... | collective-permute-start | bytes 12296 | tf_op jit(solution)/shard_map/ppermute | solution.py:619
  223.3 7.3 %collective-permute-start.9 = (f32[8,128]{1,0:T(8,128)S(1)}, f32[8,128]{1,0:T(8,128)S(1)}, u32[]{:S(2)}, u32[]{:S(2)}) collective-permute-start(f32[8,128]{1,0:T(8,128)S(1)} %get-tuple-element.802), channel_id=1, source_target_pairs={{0,1},{1,0},{2,3},{3,2},{7,6},{6,7},{5,4},{4,5},{8,9},{9,8},{10,11... | collective-permute-start | bytes 12296 | tf_op jit(solution)/shard_map/ppermute | solution.py:619
  233.4 21.9 %all_to_all.5.pieces = bf16[16,96,128]{2,1,0:T(8,128)(2,1)S(1)} all-to-all(bf16[16,96,128]{2,1,0:T(8,128)(2,1)S(1)} %shard_map.115), channel_id=1, replica_groups=mesh['grp'=32,'dom'=16] {'dom'}, dimensions={0} | all-to-all | bytes 786432 | tf_op jit(solution)/shard_map/all_to_all | solution.py:764
  (248 shorter events, 103.1 us)
Async XLA Ops:
  1.7 10.4 %collective-permute-start.8 = (f32[8,128]{1,0:T(8,128)S(1)}, f32[8,128]{1,0:T(8,128)S(1)}, u32[]{:S(2)}, u32[]{:S(2)}) collective-permute-start(f32[8,128]{1,0:T(8,128)S(1)} %get-tuple-element.776), channel_id=1, source_target_pairs={{0,16},{1,17},{2,18},{3,19},{4,23},{5,22},{6,21},{7,20},{8,24},{9,... | collective-permute-start | bytes 12296 | tf_op jit(solution)/shard_map/ppermute | solution.py:669
  3.6 8.4 %collective-permute-start.7 = (f32[8,128]{1,0:T(8,128)S(1)}, f32[8,128]{1,0:T(8,128)S(1)}, u32[]{:S(2)}, u32[]{:S(2)}) collective-permute-start(f32[8,128]{1,0:T(8,128)S(1)} %get-tuple-element.776), channel_id=1, source_target_pairs={{0,1},{1,0},{2,3},{3,2},{4,6},{5,7},{6,4},{7,5},{8,9},{9,8},{10,11... | collective-permute-start | bytes 12296 | tf_op jit(solution)/shard_map/ppermute | solution.py:669
  12.8 15.0 %collective-permute-start = (f32[8,128]{1,0:T(8,128)S(1)}, f32[8,128]{1,0:T(8,128)S(1)}, u32[]{:S(2)}, u32[]{:S(2)}) collective-permute-start(f32[8,128]{1,0:T(8,128)S(1)} %get-tuple-element.1158), channel_id=1, source_target_pairs={{0,1},{1,0},{2,3},{3,2},{7,6},{6,7},{5,4},{4,5},{8,9},{9,8},{10,11... | collective-permute-start | bytes 12296 | tf_op jit(solution)/shard_map/while/body/eval_jaxpr/ppermute | solution.py:619
  18.6 8.4 %collective-permute-start.3 = (f32[8,128]{1,0:T(8,128)S(1)}, f32[8,128]{1,0:T(8,128)S(1)}, u32[]{:S(2)}, u32[]{:S(2)}) collective-permute-start(f32[8,128]{1,0:T(8,128)S(1)} %get-tuple-element.1158), channel_id=1, source_target_pairs={{16,32},{32,16},{48,64},{64,48},{80,96},{96,80},{112,128},{128,112... | collective-permute-start | bytes 12296 | tf_op jit(solution)/shard_map/while/body/eval_jaxpr/ppermute | solution.py:619
  28.3 17.4 %collective-permute-start = (f32[8,128]{1,0:T(8,128)S(1)}, f32[8,128]{1,0:T(8,128)S(1)}, u32[]{:S(2)}, u32[]{:S(2)}) collective-permute-start(f32[8,128]{1,0:T(8,128)S(1)} %get-tuple-element.1158), channel_id=1, source_target_pairs={{0,1},{1,0},{2,3},{3,2},{7,6},{6,7},{5,4},{4,5},{8,9},{9,8},{10,11... | collective-permute-start | bytes 12296 | tf_op jit(solution)/shard_map/while/body/eval_jaxpr/ppermute | solution.py:619
  37.7 7.2 %collective-permute-start.3 = (f32[8,128]{1,0:T(8,128)S(1)}, f32[8,128]{1,0:T(8,128)S(1)}, u32[]{:S(2)}, u32[]{:S(2)}) collective-permute-start(f32[8,128]{1,0:T(8,128)S(1)} %get-tuple-element.1158), channel_id=1, source_target_pairs={{16,32},{32,16},{48,64},{64,48},{80,96},{96,80},{112,128},{128,112... | collective-permute-start | bytes 12296 | tf_op jit(solution)/shard_map/while/body/eval_jaxpr/ppermute | solution.py:619
  46.2 17.6 %collective-permute-start = (f32[8,128]{1,0:T(8,128)S(1)}, f32[8,128]{1,0:T(8,128)S(1)}, u32[]{:S(2)}, u32[]{:S(2)}) collective-permute-start(f32[8,128]{1,0:T(8,128)S(1)} %get-tuple-element.1158), channel_id=1, source_target_pairs={{0,1},{1,0},{2,3},{3,2},{7,6},{6,7},{5,4},{4,5},{8,9},{9,8},{10,11... | collective-permute-start | bytes 12296 | tf_op jit(solution)/shard_map/while/body/eval_jaxpr/ppermute | solution.py:619
  64.3 13.8 %collective-permute-start = (f32[8,128]{1,0:T(8,128)S(1)}, f32[8,128]{1,0:T(8,128)S(1)}, u32[]{:S(2)}, u32[]{:S(2)}) collective-permute-start(f32[8,128]{1,0:T(8,128)S(1)} %get-tuple-element.1158), channel_id=1, source_target_pairs={{0,1},{1,0},{2,3},{3,2},{7,6},{6,7},{5,4},{4,5},{8,9},{9,8},{10,11... | collective-permute-start | bytes 12296 | tf_op jit(solution)/shard_map/while/body/eval_jaxpr/ppermute | solution.py:619
  69.5 7.9 %collective-permute-start.3 = (f32[8,128]{1,0:T(8,128)S(1)}, f32[8,128]{1,0:T(8,128)S(1)}, u32[]{:S(2)}, u32[]{:S(2)}) collective-permute-start(f32[8,128]{1,0:T(8,128)S(1)} %get-tuple-element.1158), channel_id=1, source_target_pairs={{16,32},{32,16},{48,64},{64,48},{80,96},{96,80},{112,128},{128,112... | collective-permute-start | bytes 12296 | tf_op jit(solution)/shard_map/while/body/eval_jaxpr/ppermute | solution.py:619
  78.7 11.6 %collective-permute-start = (f32[8,128]{1,0:T(8,128)S(1)}, f32[8,128]{1,0:T(8,128)S(1)}, u32[]{:S(2)}, u32[]{:S(2)}) collective-permute-start(f32[8,128]{1,0:T(8,128)S(1)} %get-tuple-element.1158), channel_id=1, source_target_pairs={{0,1},{1,0},{2,3},{3,2},{7,6},{6,7},{5,4},{4,5},{8,9},{9,8},{10,11... | collective-permute-start | bytes 12296 | tf_op jit(solution)/shard_map/while/body/eval_jaxpr/ppermute | solution.py:619
  90.8 14.6 %collective-permute-start = (f32[8,128]{1,0:T(8,128)S(1)}, f32[8,128]{1,0:T(8,128)S(1)}, u32[]{:S(2)}, u32[]{:S(2)}) collective-permute-start(f32[8,128]{1,0:T(8,128)S(1)} %get-tuple-element.1158), channel_id=1, source_target_pairs={{0,1},{1,0},{2,3},{3,2},{7,6},{6,7},{5,4},{4,5},{8,9},{9,8},{10,11... | collective-permute-start | bytes 12296 | tf_op jit(solution)/shard_map/while/body/eval_jaxpr/ppermute | solution.py:619
  98.4 6.3 %collective-permute-start.3 = (f32[8,128]{1,0:T(8,128)S(1)}, f32[8,128]{1,0:T(8,128)S(1)}, u32[]{:S(2)}, u32[]{:S(2)}) collective-permute-start(f32[8,128]{1,0:T(8,128)S(1)} %get-tuple-element.1158), channel_id=1, source_target_pairs={{16,32},{32,16},{48,64},{64,48},{80,96},{96,80},{112,128},{128,112... | collective-permute-start | bytes 12296 | tf_op jit(solution)/shard_map/while/body/eval_jaxpr/ppermute | solution.py:619
  106.0 13.2 %collective-permute-start = (f32[8,128]{1,0:T(8,128)S(1)}, f32[8,128]{1,0:T(8,128)S(1)}, u32[]{:S(2)}, u32[]{:S(2)}) collective-permute-start(f32[8,128]{1,0:T(8,128)S(1)} %get-tuple-element.1158), channel_id=1, source_target_pairs={{0,1},{1,0},{2,3},{3,2},{7,6},{6,7},{5,4},{4,5},{8,9},{9,8},{10,11... | collective-permute-start | bytes 12296 | tf_op jit(solution)/shard_map/while/body/eval_jaxpr/ppermute | solution.py:619
  119.7 13.3 %collective-permute-start = (f32[8,128]{1,0:T(8,128)S(1)}, f32[8,128]{1,0:T(8,128)S(1)}, u32[]{:S(2)}, u32[]{:S(2)}) collective-permute-start(f32[8,128]{1,0:T(8,128)S(1)} %get-tuple-element.1158), channel_id=1, source_target_pairs={{0,1},{1,0},{2,3},{3,2},{7,6},{6,7},{5,4},{4,5},{8,9},{9,8},{10,11... | collective-permute-start | bytes 12296 | tf_op jit(solution)/shard_map/while/body/eval_jaxpr/ppermute | solution.py:619
  133.5 13.2 %collective-permute-start = (f32[8,128]{1,0:T(8,128)S(1)}, f32[8,128]{1,0:T(8,128)S(1)}, u32[]{:S(2)}, u32[]{:S(2)}) collective-permute-start(f32[8,128]{1,0:T(8,128)S(1)} %get-tuple-element.1158), channel_id=1, source_target_pairs={{0,1},{1,0},{2,3},{3,2},{7,6},{6,7},{5,4},{4,5},{8,9},{9,8},{10,11... | collective-permute-start | bytes 12296 | tf_op jit(solution)/shard_map/while/body/eval_jaxpr/ppermute | solution.py:619
  147.3 13.3 %collective-permute-start = (f32[8,128]{1,0:T(8,128)S(1)}, f32[8,128]{1,0:T(8,128)S(1)}, u32[]{:S(2)}, u32[]{:S(2)}) collective-permute-start(f32[8,128]{1,0:T(8,128)S(1)} %get-tuple-element.1158), channel_id=1, source_target_pairs={{0,1},{1,0},{2,3},{3,2},{7,6},{6,7},{5,4},{4,5},{8,9},{9,8},{10,11... | collective-permute-start | bytes 12296 | tf_op jit(solution)/shard_map/while/body/eval_jaxpr/ppermute | solution.py:619
  161.1 13.2 %collective-permute-start = (f32[8,128]{1,0:T(8,128)S(1)}, f32[8,128]{1,0:T(8,128)S(1)}, u32[]{:S(2)}, u32[]{:S(2)}) collective-permute-start(f32[8,128]{1,0:T(8,128)S(1)} %get-tuple-element.1158), channel_id=1, source_target_pairs={{0,1},{1,0},{2,3},{3,2},{7,6},{6,7},{5,4},{4,5},{8,9},{9,8},{10,11... | collective-permute-start | bytes 12296 | tf_op jit(solution)/shard_map/while/body/eval_jaxpr/ppermute | solution.py:619
  174.9 13.3 %collective-permute-start = (f32[8,128]{1,0:T(8,128)S(1)}, f32[8,128]{1,0:T(8,128)S(1)}, u32[]{:S(2)}, u32[]{:S(2)}) collective-permute-start(f32[8,128]{1,0:T(8,128)S(1)} %get-tuple-element.1158), channel_id=1, source_target_pairs={{0,1},{1,0},{2,3},{3,2},{7,6},{6,7},{5,4},{4,5},{8,9},{9,8},{10,11... | collective-permute-start | bytes 12296 | tf_op jit(solution)/shard_map/while/body/eval_jaxpr/ppermute | solution.py:619
  188.7 13.2 %collective-permute-start = (f32[8,128]{1,0:T(8,128)S(1)}, f32[8,128]{1,0:T(8,128)S(1)}, u32[]{:S(2)}, u32[]{:S(2)}) collective-permute-start(f32[8,128]{1,0:T(8,128)S(1)} %get-tuple-element.1158), channel_id=1, source_target_pairs={{0,1},{1,0},{2,3},{3,2},{7,6},{6,7},{5,4},{4,5},{8,9},{9,8},{10,11... | collective-permute-start | bytes 12296 | tf_op jit(solution)/shard_map/while/body/eval_jaxpr/ppermute | solution.py:619
  202.5 13.3 %collective-permute-start = (f32[8,128]{1,0:T(8,128)S(1)}, f32[8,128]{1,0:T(8,128)S(1)}, u32[]{:S(2)}, u32[]{:S(2)}) collective-permute-start(f32[8,128]{1,0:T(8,128)S(1)} %get-tuple-element.1158), channel_id=1, source_target_pairs={{0,1},{1,0},{2,3},{3,2},{7,6},{6,7},{5,4},{4,5},{8,9},{9,8},{10,11... | collective-permute-start | bytes 12296 | tf_op jit(solution)/shard_map/while/body/eval_jaxpr/ppermute | solution.py:619
  216.3 15.5 %collective-permute-start.12 = (f32[8,128]{1,0:T(8,128)S(1)}, f32[8,128]{1,0:T(8,128)S(1)}, u32[]{:S(2)}, u32[]{:S(2)}) collective-permute-start(f32[8,128]{1,0:T(8,128)S(1)} %get-tuple-element.802), channel_id=1, source_target_pairs={{16,32},{32,16},{48,64},{64,48},{80,96},{96,80},{112,128},{128,112... | collective-permute-start | bytes 12296 | tf_op jit(solution)/shard_map/ppermute | solution.py:619
  218.6 13.3 %collective-permute-start.11 = (f32[8,128]{1,0:T(8,128)S(1)}, f32[8,128]{1,0:T(8,128)S(1)}, u32[]{:S(2)}, u32[]{:S(2)}) collective-permute-start(f32[8,128]{1,0:T(8,128)S(1)} %get-tuple-element.802), channel_id=1, source_target_pairs={{1,2},{2,1},{3,7},{7,3},{6,5},{5,6},{4,8},{8,4},{9,10},{10,9},{11,... | collective-permute-start | bytes 12296 | tf_op jit(solution)/shard_map/ppermute | solution.py:619
  219.3 13.6 %collective-permute-start.10 = (f32[8,128]{1,0:T(8,128)S(1)}, f32[8,128]{1,0:T(8,128)S(1)}, u32[]{:S(2)}, u32[]{:S(2)}) collective-permute-start(f32[8,128]{1,0:T(8,128)S(1)} %get-tuple-element.802), channel_id=1, source_target_pairs={{0,16},{16,0},{32,48},{48,32},{64,80},{80,64},{96,112},{112,96},{1... | collective-permute-start | bytes 12296 | tf_op jit(solution)/shard_map/ppermute | solution.py:619
  223.3 9.5 %collective-permute-start.9 = (f32[8,128]{1,0:T(8,128)S(1)}, f32[8,128]{1,0:T(8,128)S(1)}, u32[]{:S(2)}, u32[]{:S(2)}) collective-permute-start(f32[8,128]{1,0:T(8,128)S(1)} %get-tuple-element.802), channel_id=1, source_target_pairs={{0,1},{1,0},{2,3},{3,2},{7,6},{6,7},{5,4},{4,5},{8,9},{9,8},{10,11... | collective-permute-start | bytes 12296 | tf_op jit(solution)/shard_map/ppermute | solution.py:619
  (41 other events, 199.2 us)
